TPU v7x, 128 devices: a whole 4x4x4 slice. The times are simulated.
128 devices in a mesh: area: 16 (over z, y), tie: 8 (over x, core).
Axes of the slice: x: 4, y: 4, z: 4, core: 2. Of those that a mesh axis runs over, the one named last changes fastest.
Arguments:
- ginv: bfloat16 [512, 1024, 1024], P(('area', 'tie'))
- rhs: float32 [524288, 128], P(('area', 'tie')), may hold values from -6 to 6
- bnd_row: int32 [512, 128], P(('area', 'tie')), may hold values from -1 to 1023, as said below
- bnd_var: int32 [512, 128], P(('area', 'tie')), may hold values from -1 to 8191, as said below
Outputs:
- states: float32 [524288, 128], P(('area', 'tie'))
- consensus: float32 [8192, 128], P(('area', 'tie'))
- dual_value: float32 [65536, 128], P(('area', 'tie'))
Inputs may be any that keep to these rules, and one draw needn't show every extreme that they name: `bnd_row`: -1 marks an unused entry slot; the live rows of one area are distinct. `bnd_var`: -1 exactly where bnd_row is -1. Variable v is owned by the device holding rows v of the consensus output, block v // 64. The areas of one device hold at most 4 live entries owned by any one device; in every draw some owner holds exactly 4 from every device.
All inputs are finite; a program needn't handle non-finite values.
Results may differ from a plain program's by a relative error of at most 0.003.
Values sent between devices are 32-bit elements; how exact they have to be, the bound alone decides.
No kernel may reach another device: no remote copies, remote signals or barrier semaphores. Data moves between devices by JAX's collectives and lax.ppermute only.
A program may use at most 64 MiB of HBM per device.

v0:
```python
import jax
import jax.numpy as jnp
from jax import lax
from jax.sharding import PartitionSpec as P

SLOT = 4
VAR_DEV = 64
ITERS = 4


PENALTY = 1.0


def on_device(ginv, rhs, bnd_row, bnd_var):
    area_dev, state_size, _ = ginv.shape
    snap_count = rhs.shape[1]
    bound_size = bnd_row.shape[1]
    entries = area_dev * bound_size
    area_count = lax.axis_size("area")
    tie_count = lax.axis_size("tie")
    device_total = area_count * tie_count
    capacity = device_total * SLOT
    row_flat = bnd_row.reshape(entries)
    var_flat = bnd_var.reshape(entries)
    active = row_flat >= 0
    offsets = jnp.repeat(jnp.arange(area_dev, dtype=jnp.int32) * state_size, bound_size)
    state_row = jnp.where(active, offsets + row_flat, 0)
    owners = jnp.where(active, var_flat // VAR_DEV, device_total)
    onehot = (owners[:, None] == jnp.arange(device_total, dtype=jnp.int32)[None, :]).astype(
        jnp.int32
    )
    placed = jnp.sum(onehot * (jnp.cumsum(onehot, axis=0) - 1), axis=1)
    slot_of_entry = jnp.where(active, owners * SLOT + placed, capacity)
    entry_of_slot = jnp.full((capacity + 1,), entries, jnp.int32)
    entry_of_slot = entry_of_slot.at[slot_of_entry].set(jnp.arange(entries, dtype=jnp.int32))[
        :capacity
    ]
    local_var = jnp.where(active, var_flat % VAR_DEV, -1)
    slot_var = jnp.concatenate([local_var, jnp.full((1,), -1, jnp.int32)])[entry_of_slot]
    recv_var = lax.all_to_all(
        slot_var.reshape(device_total, SLOT),
        ("area", "tie"),
        split_axis=0,
        concat_axis=0,
        tiled=True,
    ).reshape(capacity)
    member = (recv_var[None, :] == jnp.arange(VAR_DEV, dtype=jnp.int32)[:, None]).astype(
        jnp.float32
    )
    counts = jnp.sum(member, axis=1)
    inverse = 1.0 / jnp.maximum(counts, 1.0)
    mask = active[:, None]
    zero_row = jnp.zeros((1, snap_count), jnp.float32)
    dual_value = jnp.zeros((entries, snap_count), jnp.float32)
    agreed = jnp.zeros((entries, snap_count), jnp.float32)
    states = None
    consensus = None
    for iteration in range(ITERS):
        shifted = jnp.where(mask, agreed - dual_value, 0.0)
        update = (
            jnp.zeros((area_dev * state_size, snap_count), jnp.float32).at[state_row].add(shifted)
        )
        blended = (
            (rhs + PENALTY * update).astype(jnp.bfloat16).reshape(area_dev, state_size, snap_count)
        )
        states = jnp.einsum("aij,ajs->ais", ginv, blended, preferred_element_type=jnp.float32)
        states = states.reshape(area_dev * state_size, snap_count)
        local_part = jnp.where(mask, states[state_row] + dual_value, 0.0)
        outgoing = jnp.concatenate([local_part, zero_row])[entry_of_slot]
        incoming = lax.all_to_all(
            outgoing.reshape(device_total, SLOT, snap_count),
            ("area", "tie"),
            split_axis=0,
            concat_axis=0,
            tiled=True,
        )
        incoming = incoming.reshape(capacity, snap_count)
        totals = jnp.dot(member, incoming, precision=lax.Precision.HIGHEST)
        consensus = totals * inverse[:, None]
        returning = jnp.dot(member.T, consensus, precision=lax.Precision.HIGHEST)
        returned = lax.all_to_all(
            returning.reshape(device_total, SLOT, snap_count),
            ("area", "tie"),
            split_axis=0,
            concat_axis=0,
            tiled=True,
        )
        returned = returned.reshape(capacity, snap_count)
        agreed = jnp.concatenate([returned, zero_row])[slot_of_entry]
        agreed = jnp.where(mask, agreed, 0.0)
        dual_value = jnp.where(mask, local_part - agreed, 0.0)
    return (states, consensus, dual_value)


def solution(mesh):
    in_specs = (
        P(("area", "tie"), None, None),
        P(("area", "tie"), None),
        P(("area", "tie"), None),
        P(("area", "tie"), None),
    )
    out_specs = (P(("area", "tie"), None), P(("area", "tie"), None), P(("area", "tie"), None))
    return jax.shard_map(
        on_device, mesh=mesh, in_specs=in_specs, out_specs=out_specs, check_vma=False
    )
```

profile of v0, /device:TPU:1, one launch (start us, length us, event | category | flops | bytes accessed | tf_op | source)
XLA Modules:
  0.0 226.1 jit_solution(18356299583947733285)
XLA Ops:
  0.7 1.6 copy.67
  3.1 2.4 %scatter_custom_fusion = s32[513]{0:T(1024)S(1)} fusion(s32[512]{0:T(512)S(1)} %bitcast.143, s32[512]{0:T(512)S(1)} %iota.19, s32[]{:T(128)} %constant.51.clone.1), kind=kCustom, calls=%fused_computation.110 | custom fusion | bytes 2056 | tf_op jit(solution)/shard_map/scatter | solution.py:35
  5.6 2.3 %gather_fusion = s32[512]{0:T(512)S(1)} fusion(s32[513]{0:T(1024)S(1)} %pad_add_fusion, s32[1024]{0:T(1024)S(1)} %pad_clamp_fusion.2), kind=kCustom, calls=%fused_computation | custom fusion | bytes 6144 | tf_op jit(solution)/shard_map/gather | solution.py:39
  8.6 11.5 %all-to-all-start = ((s32[128,1,4]{2,1,0:T(1,128)}), s32[128,1,4]{2,1,0:T(1,128)S(1)}, u32[]{:S(2)}, u32[]{:S(2)}) async-start(s32[128,1,4]{2,1,0:T(1,128)} %bitcast.10), calls=%async_computation | async-start | bytes 131072 | tf_op jit(solution)/shard_map/all_to_all | solution.py:40
  20.1 1.3 copy.63
  21.4 1.4 copy.64
  22.8 1.3 copy.65
  24.1 4.1 %scatter_custom_fusion.1 = f32[4096,128]{1,0:T(8,128)S(1)} fusion(f32[4096,128]{1,0:T(8,128)S(1)} %copy.67, s32[512]{0:T(512)S(1)} %bitcast.139, f32[]{:T(128)} %constant.57.clone.1), kind=kCustom, calls=%fused_computation.56 | custom fusion | flops 65536 | bytes 2097156 | tf_op jit(solution)/shard_map/scatter-add | solution.py:61
  28.3 7.6 %convolution_bitcast_fusion.3 = f32[4,1024,128]{1,2,0:T(8,128)} fusion(bf16[4,1024,128]{2,1,0:T(8,128)(2,1)S(1)} %bitcast.109, bf16[4,1024,1024]{2,1,0:T(8,128)(2,1)} %param.4), kind=kOutput, calls=%fused_computation.21 | convolution fusion | flops 1073741824 | bytes 11534336 | tf_op jit(solution)/shard_map/aij,ajs->ais/dot_general | solution.py:66
  35.9 1.9 copy.37
  39.0 1.6 gather_fusion.2
  40.7 9.8 %all-to-all-start.1 = ((f32[128,4,128]{2,1,0:T(4,128)}), f32[128,4,128]{2,1,0:T(4,128)S(1)}, u32[]{:S(2)}, u32[]{:S(2)}) async-start(f32[128,4,128]{2,1,0:T(4,128)} %bitcast.14), calls=%async_computation.1 | async-start | bytes 524288 | tf_op jit(solution)/shard_map/all_to_all | solution.py:70
  52.2 9.4 %all-to-all-done.1 = f32[128,4,128]{2,1,0:T(4,128)S(1)} async-done(((f32[128,4,128]{2,1,0:T(4,128)}), f32[128,4,128]{2,1,0:T(4,128)S(1)}, u32[]{:S(2)}, u32[]{:S(2)}) %all-to-all-start.1) | async-done | bytes 262176 | tf_op jit(solution)/shard_map/all_to_all | solution.py:70
  61.8 1.1 fusion.23
  62.9 4.4 %all-to-all-start.2 = ((f32[128,4,128]{2,1,0:T(4,128)}), f32[128,4,128]{2,1,0:T(4,128)S(1)}, u32[]{:S(2)}, u32[]{:S(2)}) async-start(f32[128,4,128]{2,1,0:T(4,128)} %bitcast.16), calls=%async_computation.2 | async-start | bytes 524288 | tf_op jit(solution)/shard_map/all_to_all | solution.py:81
  67.3 11.1 %all-to-all-done.2 = f32[128,4,128]{2,1,0:T(4,128)S(1)} async-done(((f32[128,4,128]{2,1,0:T(4,128)}), f32[128,4,128]{2,1,0:T(4,128)S(1)}, u32[]{:S(2)}, u32[]{:S(2)}) %all-to-all-start.2) | async-done | bytes 262176 | tf_op jit(solution)/shard_map/all_to_all | solution.py:81
  79.4 4.4 %scatter_custom_fusion.2 = f32[4096,128]{1,0:T(8,128)S(1)} fusion(f32[4096,128]{1,0:T(8,128)S(1)} %copy-done.2, s32[512]{0:T(512)S(1)} %bitcast.140, f32[512,128]{1,0:T(8,128)S(1)} %gather_fusion.3, f32[]{:T(128)} %constant.57.clone.1, pred[512]{0:T(512)(128)(4,1)S(1)} %bitcast.129, f32[512,128]{1,0:T(8,128)S(1)} %gather_fusion.1), kind=kCustom, calls=%fused_computation.40 | custom fusion | flops 458752 | bytes 2621956 | tf_op jit(solution)/shard_map/scatter-add | solution.py:61
  83.9 7.6 %convolution_bitcast_fusion.2 = f32[4,1024,128]{1,2,0:T(8,128)} fusion(bf16[4,1024,128]{2,1,0:T(8,128)(2,1)S(1)} %bitcast.110, bf16[4,1024,1024]{2,1,0:T(8,128)(2,1)} %param.4), kind=kOutput, calls=%fused_computation.20 | convolution fusion | flops 1073741824 | bytes 11534336 | tf_op jit(solution)/shard_map/aij,ajs->ais/dot_general | solution.py:66
  91.5 1.9 copy.39
  94.7 1.0 gather_fusion.5
  95.7 15.4 %all_to_all.49 = f32[128,4,128]{2,1,0:T(4,128)S(1)} all-to-all(f32[128,4,128]{2,1,0:T(4,128)S(1)} %bitcast.125), channel_id=1, replica_groups=mesh['area'=16,'tie'=8] {'area','tie'}, dimensions={0} | all-to-all | bytes 524288 | tf_op jit(solution)/shard_map/all_to_all | solution.py:70
  111.8 15.3 %all_to_all.50 = f32[128,4,128]{2,1,0:T(4,128)S(1)} all-to-all(f32[128,4,128]{2,1,0:T(4,128)S(1)} %bitcast.120), channel_id=1, replica_groups=mesh['area'=16,'tie'=8] {'area','tie'}, dimensions={0} | all-to-all | bytes 524288 | tf_op jit(solution)/shard_map/all_to_all | solution.py:81
  128.1 4.4 %scatter_custom_fusion.3 = f32[4096,128]{1,0:T(8,128)S(1)} fusion(f32[4096,128]{1,0:T(8,128)S(1)} %copy-done.1, s32[512]{0:T(512)S(1)} %bitcast.141, f32[512,128]{1,0:T(8,128)S(1)} %gather_fusion.6, f32[512,128]{1,0:T(8,128)S(1)} %add_select_fusion.2, f32[]{:T(128)} %constant.57.clone.1, pred[512]{0:T(512)(128)(4,1)S(1)} %bitcast.131), kind=kCustom, calls=%fused_computation.35 | custom fusion | flops 393216 | bytes 2621956 | tf_op jit(solution)/shard_map/scatter-add | solution.py:61
  132.7 7.6 %convolution_bitcast_fusion.1 = f32[4,1024,128]{1,2,0:T(8,128)} fusion(bf16[4,1024,128]{2,1,0:T(8,128)(2,1)S(1)} %bitcast.111, bf16[4,1024,1024]{2,1,0:T(8,128)(2,1)} %param.4), kind=kOutput, calls=%fused_computation.19 | convolution fusion | flops 1073741824 | bytes 11534336 | tf_op jit(solution)/shard_map/aij,ajs->ais/dot_general | solution.py:66
  140.3 1.9 copy.41
  144.5 15.3 %all_to_all.51 = f32[128,4,128]{2,1,0:T(4,128)S(1)} all-to-all(f32[128,4,128]{2,1,0:T(4,128)S(1)} %bitcast.126), channel_id=1, replica_groups=mesh['area'=16,'tie'=8] {'area','tie'}, dimensions={0} | all-to-all | bytes 524288 | tf_op jit(solution)/shard_map/all_to_all | solution.py:70
  160.5 15.3 %all_to_all.52 = f32[128,4,128]{2,1,0:T(4,128)S(1)} all-to-all(f32[128,4,128]{2,1,0:T(4,128)S(1)} %bitcast.122), channel_id=1, replica_groups=mesh['area'=16,'tie'=8] {'area','tie'}, dimensions={0} | all-to-all | bytes 524288 | tf_op jit(solution)/shard_map/all_to_all | solution.py:81
  176.8 4.2 %scatter_custom_fusion.4 = f32[4096,128]{1,0:T(8,128)S(1)} fusion(f32[4096,128]{1,0:T(8,128)S(1)} %copy-done, s32[512]{0:T(512)S(1)} %bitcast.142, f32[512,128]{1,0:T(8,128)S(1)} %gather_fusion.9, f32[512,128]{1,0:T(8,128)S(1)} %add_select_fusion.1, f32[]{:T(128)} %constant.57.clone.1, pred[512]{0:T(512)(128)(4,1)S(1)} %bitcast.133), kind=kCustom, calls=%fused_computation.30 | custom fusion | flops 393216 | bytes 2621956 | tf_op jit(solution)/shard_map/scatter-add | solution.py:61
  181.1 7.6 %convolution_bitcast_fusion = f32[4,1024,128]{1,2,0:T(8,128)} fusion(bf16[4,1024,128]{2,1,0:T(8,128)(2,1)S(1)} %bitcast.112, bf16[4,1024,1024]{2,1,0:T(8,128)(2,1)} %param.4), kind=kOutput, calls=%fused_computation.18 | convolution fusion | flops 1073741824 | bytes 11534336 | tf_op jit(solution)/shard_map/aij,ajs->ais/dot_general | solution.py:66
  188.7 1.9 copy.43
  193.0 15.3 %all_to_all.53 = f32[128,4,128]{2,1,0:T(4,128)S(1)} all-to-all(f32[128,4,128]{2,1,0:T(4,128)S(1)} %bitcast.124), channel_id=1, replica_groups=mesh['area'=16,'tie'=8] {'area','tie'}, dimensions={0} | all-to-all | bytes 524288 | tf_op jit(solution)/shard_map/all_to_all | solution.py:70
  208.9 15.3 %all_to_all.54 = f32[128,4,128]{2,1,0:T(4,128)S(1)} all-to-all(f32[128,4,128]{2,1,0:T(4,128)S(1)} %bitcast.123), channel_id=1, replica_groups=mesh['area'=16,'tie'=8] {'area','tie'}, dimensions={0} | all-to-all | bytes 524288 | tf_op jit(solution)/shard_map/all_to_all | solution.py:81
  (75 shorter events, 17.8 us)
Async XLA Ops:
  0.6 1.6 copy-start.6
  0.6 1.6 copy-start.5
  8.6 32.0 %all-to-all-start = ((s32[128,1,4]{2,1,0:T(1,128)}), s32[128,1,4]{2,1,0:T(1,128)S(1)}, u32[]{:S(2)}, u32[]{:S(2)}) async-start(s32[128,1,4]{2,1,0:T(1,128)} %bitcast.10), calls=%async_computation | async-start | bytes 131072 | tf_op jit(solution)/shard_map/all_to_all | solution.py:40
  40.7 20.8 %all-to-all-start.1 = ((f32[128,4,128]{2,1,0:T(4,128)}), f32[128,4,128]{2,1,0:T(4,128)S(1)}, u32[]{:S(2)}, u32[]{:S(2)}) async-start(f32[128,4,128]{2,1,0:T(4,128)} %bitcast.14), calls=%async_computation.1 | async-start | bytes 524288 | tf_op jit(solution)/shard_map/all_to_all | solution.py:70
  51.0 28.5 %copy-start.2 = (f32[4096,128]{1,0:T(8,128)S(1)}, f32[4096,128]{1,0:T(8,128)}, u32[]{:S(2)}) copy-start(f32[4096,128]{1,0:T(8,128)} %copy.63) | copy-start | bytes 6291460
  62.9 15.5 %all-to-all-start.2 = ((f32[128,4,128]{2,1,0:T(4,128)}), f32[128,4,128]{2,1,0:T(4,128)S(1)}, u32[]{:S(2)}, u32[]{:S(2)}) async-start(f32[128,4,128]{2,1,0:T(4,128)} %bitcast.16), calls=%async_computation.2 | async-start | bytes 524288 | tf_op jit(solution)/shard_map/all_to_all | solution.py:81
  111.1 17.0 %copy-start.1 = (f32[4096,128]{1,0:T(8,128)S(1)}, f32[4096,128]{1,0:T(8,128)}, u32[]{:S(2)}) copy-start(f32[4096,128]{1,0:T(8,128)} %copy.64) | copy-start | bytes 6291460
  159.8 17.0 %copy-start = (f32[4096,128]{1,0:T(8,128)S(1)}, f32[4096,128]{1,0:T(8,128)}, u32[]{:S(2)}) copy-start(f32[4096,128]{1,0:T(8,128)} %copy.65) | copy-start | bytes 6291460
  190.7 2.3 %copy-start.3 = (f32[4,1024,128]{2,1,0:T(8,128)}, f32[4,1024,128]{2,1,0:T(8,128)S(1)}, u32[]{:S(2)}) copy-start(f32[4,1024,128]{2,1,0:T(8,128)S(1)} %copy.43) | copy-start | bytes 6291460
  208.5 17.6 %copy-start.4 = (f32[64,128]{1,0:T(8,128)}, f32[64,128]{1,0:T(8,128)S(1)}, u32[]{:S(2)}) copy-start(f32[64,128]{1,0:T(8,128)S(1)} %convolution_multiply_fusion) | copy-start | bytes 98308
where the time goes:
time: 227 us; the launch traced here: 226 us
  blocking collectives  91.9 us (40%)
  matrix products  33.6 us (15%)
  local copies, waits for them, and re-layouts  32.7 us (14%)
  starting transfers between devices  25.7 us (11%)
  other arithmetic  20.7 us (9%)
  waiting for transfers between devices  20.4 us (9%)
    all_to_all x3, blocking collectives, on_device(): lax.all_to_all(outgoing.reshape(device_total, SLOT, snap_count), ('area',...  46 us
    all_to_all x3, blocking collectives, on_device(): lax.all_to_all(returning.reshape(device_total, SLOT, snap_count), ('area'...  45.9 us
    dot_general x4, matrix products, on_device(): jnp.einsum('aij,ajs->ais', ginv, blended, preferred_element_type=jnp.floa...  30.4 us
    scatter-add x4, other arithmetic, on_device(): jnp.zeros((area_dev * state_size, snap_count), jnp.float32).at[state_row]  17.1 us
    all_to_all x1, starting transfers between devices, on_device(): lax.all_to_all(slot_var.reshape(device_total, SLOT), ('area', 'tie'), spl...  11.5 us
    all_to_all x1, waiting for transfers between devices, on_device(): lax.all_to_all(returning.reshape(device_total, SLOT, snap_count), ('area'...  11.1 us
    all_to_all x1, starting transfers between devices, on_device(): lax.all_to_all(outgoing.reshape(device_total, SLOT, snap_count), ('area',...  9.76 us
    all_to_all x1, waiting for transfers between devices, on_device(): lax.all_to_all(outgoing.reshape(device_total, SLOT, snap_count), ('area',...  9.36 us
  transfers between devices with their start and end apart: 3, of which 2 were waited for; matrix products, arithmetic and copies ran while one was open for 10% of the time, Pallas kernels for 0%

commit v1 on v0

v1 whole, which is shorter than its diff:
```python
import jax
import jax.numpy as jnp
from jax import lax
from jax.experimental import pallas as pl
from jax.experimental.pallas import tpu as pltpu
from jax.sharding import PartitionSpec as P

SLOT = 4
VAR_DEV = 64
ITERS = 4
PENALTY = 1.0
WIDE = 8

F32 = jnp.float32
BF16 = jnp.bfloat16


def split3(x):
    hi = x.astype(BF16)
    rest = x - hi.astype(F32)
    mid = rest.astype(BF16)
    low = (rest - mid.astype(F32)).astype(BF16)
    return [hi, mid, low]


def join3(y, at=0, width=128):
    return (y[:, at : at + width] + y[:, at + width : at + 2 * width]) + y[
        :, at + 2 * width : at + 3 * width
    ]


def dot(a, b):
    return jnp.dot(a, b, preferred_element_type=F32)


def dot_t(a, b):
    return lax.dot_general(a, b, (((0,), (0,)), ((), ())), preferred_element_type=F32)


def dot_nt(a, b):
    return lax.dot_general(a, b, (((1,), (1,)), ((), ())), preferred_element_type=F32)


def iota(shape, dim):
    return lax.broadcasted_iota(jnp.int32, shape, dim)


def prepare_kernel(
    row_ref, var_ref, ginv_ref, rhs_ref,
    inner_ref, cols_ref, place_ref, mat_ref, base_ref, term_ref, local_ref, out_ref,
    carry_ref, ids_ref, acc_ref,
):
    area = pl.program_id(0)
    last = pl.num_programs(0) - 1
    bound = row_ref.shape[1]
    state = ginv_ref.shape[1]
    slots = mat_ref.shape[0]
    owners = slots // SLOT

    @pl.when(area == 0)
    def _():
        carry_ref[...] = jnp.zeros_like(carry_ref)
        ids_ref[...] = jnp.zeros_like(ids_ref)
        acc_ref[...] = jnp.zeros_like(acc_ref)
        base_ref[...] = jnp.zeros_like(base_ref)
        term_ref[...] = jnp.zeros_like(term_ref)

    row = row_ref[pl.ds(area, 1), :]
    var = var_ref[pl.ds(area, 1), :]
    live = row >= 0
    owner = jnp.where(live, lax.shift_right_arithmetic(var, 6), -1)
    local_id = jnp.where(live, (var & (VAR_DEV - 1)) + 1, 0).astype(F32)
    owned = iota((owners, bound), 0) == owner
    owned_f = owned.astype(F32)
    before = (iota((bound, bound), 0) < iota((bound, bound), 1)).astype(F32).astype(BF16)
    earlier = dot(owned_f.astype(BF16), before)
    rank = jnp.sum(jnp.where(owned, earlier + carry_ref[...], 0.0), axis=0, keepdims=True)
    carry_ref[...] += jnp.sum(owned_f, axis=1, keepdims=True)
    rank_i = rank.astype(jnp.int32)
    slot = jnp.where(live, owner * SLOT + rank_i, -1)
    place = (iota((slots, bound), 0) == slot).astype(F32).astype(BF16)
    place_ref[...] = place
    at_rank = (iota((bound, bound), 0) == rank_i).astype(F32).astype(BF16)
    ids_ref[...] += dot_nt((owned_f * local_id).astype(BF16), at_rank)

    picks_f = (iota((state, bound), 0) == row).astype(F32)
    picks = picks_f.astype(BF16)
    is_bound = jnp.sum(picks_f, axis=1, keepdims=True) > 0.0
    rhs = rhs_ref[...]
    inner = jnp.where(is_bound, 0.0, rhs).astype(BF16)
    both = dot(ginv_ref[0], jnp.concatenate([inner, picks], axis=1))
    snaps = rhs.shape[1]
    solved = both[:, :snaps]
    cols = both[:, snaps:].astype(BF16)
    inner_ref[...] = solved
    cols_ref[0] = cols
    at_rows = dot_t(picks, jnp.concatenate(split3(solved) + split3(rhs) + [cols], axis=1))
    at_slots = dot(place, at_rows.astype(BF16))
    base_ref[...] += join3(at_slots, 0, snaps)
    term_ref[...] += join3(at_slots, 3 * snaps, snaps)
    acc_ref[...] += dot_nt(at_slots[:, 6 * snaps :].astype(BF16), place)

    @pl.when(area == last)
    def _():
        mat = acc_ref[...].astype(BF16)
        mat_ref[...] = mat
        local_ref[...] = base_ref[...] + dot(mat, term_ref[...].astype(BF16))
        for k in range(SLOT):
            out_ref[pl.ds(k, owners, stride=WIDE), :] = local_ref[pl.ds(k, owners, stride=SLOT), :]
        out_ref[pl.ds(SLOT, owners, stride=WIDE), :] = ids_ref[...] - 1.0
        for k in range(SLOT + 1, WIDE):
            out_ref[pl.ds(k, owners, stride=WIDE), :] = jnp.zeros_like(ids_ref)


def average(member, inverse, stack, ret_ref):
    totals = join3(dot_t(member, jnp.concatenate(split3(stack), axis=1)))
    consensus = totals * inverse
    back = join3(dot(member, jnp.concatenate(split3(consensus), axis=1)))
    sources = back.shape[0] // SLOT
    for k in range(SLOT):
        ret_ref[pl.ds(k, sources, stride=SLOT), :] = back[k * sources : (k + 1) * sources]
    return consensus


def first_owner_kernel(in_ref, ret_ref, member_ref, inverse_ref):
    sources = in_ref.shape[0] // WIDE
    ids = in_ref[pl.ds(SLOT, sources, stride=WIDE), :].astype(jnp.int32)
    lane = iota((sources, 128), 1)
    member = jnp.concatenate(
        [(ids[:, k : k + 1] == lane).astype(F32) for k in range(SLOT)], axis=0
    ).astype(BF16)
    counts = dot_t(member, jnp.ones((member.shape[0], 128), BF16))
    inverse = 1.0 / jnp.maximum(counts, 1.0)
    member_ref[...] = member
    inverse_ref[...] = inverse
    stack = jnp.concatenate(
        [in_ref[pl.ds(k, sources, stride=WIDE), :] for k in range(SLOT)], axis=0
    )
    average(member, inverse, stack, ret_ref)


def owner_kernel(in_ref, member_ref, inverse_ref, ret_ref, cons_ref):
    sources = in_ref.shape[0] // SLOT
    stack = jnp.concatenate(
        [in_ref[pl.ds(k, sources, stride=SLOT), :] for k in range(SLOT)], axis=0
    )
    consensus = average(member_ref[...], inverse_ref[...], stack, ret_ref)
    cons_ref[...] = consensus[:VAR_DEV]


def local_kernel(agreed_ref, local_ref, term_ref, base_ref, mat_ref, new_ref, blend_ref):
    agreed = agreed_ref[...]
    dual = local_ref[...] - agreed
    blend = (term_ref[...] + PENALTY * (agreed - dual)).astype(BF16)
    blend_ref[...] = blend
    new_ref[...] = (base_ref[...] + dot(mat_ref[...], blend)) + dual


def states_kernel(inner_ref, cols_ref, place_ref, blend_ref, states_ref):
    rows = dot_t(place_ref[...], blend_ref[...]).astype(BF16)
    states_ref[...] = inner_ref[...] + dot(cols_ref[0], rows)


def dual_kernel(agreed_ref, local_ref, place_ref, dual_ref):
    dual = local_ref[...] - agreed_ref[...]
    dual_ref[...] = join3(dot_t(place_ref[...], jnp.concatenate(split3(dual), axis=1)))


def shape(dims, dtype=F32):
    return jax.ShapeDtypeStruct(dims, dtype)


def on_device(ginv, rhs, bnd_row, bnd_var):
    areas, state, _ = ginv.shape
    snaps = rhs.shape[1]
    bound = bnd_row.shape[1]
    devices = lax.axis_size("area") * lax.axis_size("tie")
    slots = devices * SLOT
    entries = areas * bound

    def whole(*dims):
        return pl.BlockSpec(dims, lambda a: (0,) * len(dims))

    inner, cols, place, mat, base, term, local, outgoing = pl.pallas_call(
        prepare_kernel,
        grid=(areas,),
        in_specs=[
            whole(areas, bound),
            whole(areas, bound),
            pl.BlockSpec((1, state, state), lambda a: (a, 0, 0)),
            pl.BlockSpec((state, snaps), lambda a: (a, 0)),
        ],
        out_specs=[
            pl.BlockSpec((state, snaps), lambda a: (a, 0)),
            pl.BlockSpec((1, state, bound), lambda a: (a, 0, 0)),
            pl.BlockSpec((slots, bound), lambda a: (0, a)),
            whole(slots, slots),
            whole(slots, snaps),
            whole(slots, snaps),
            whole(slots, snaps),
            whole(devices * WIDE, snaps),
        ],
        out_shape=[
            shape((areas * state, snaps)),
            shape((areas, state, bound), BF16),
            shape((slots, entries), BF16),
            shape((slots, slots), BF16),
            shape((slots, snaps)),
            shape((slots, snaps)),
            shape((slots, snaps)),
            shape((devices * WIDE, snaps)),
        ],
        scratch_shapes=[
            pltpu.VMEM((devices, bound), F32),
            pltpu.VMEM((devices, bound), F32),
            pltpu.VMEM((slots, slots), F32),
        ],
        compiler_params=pltpu.CompilerParams(dimension_semantics=("arbitrary",)),
        name="prepare",
    )(bnd_row, bnd_var, ginv, rhs)

    def exchange(x):
        x = x.reshape(devices, -1, snaps)
        x = lax.all_to_all(x, ("area", "tie"), split_axis=0, concat_axis=0, tiled=True)
        return x.reshape(-1, snaps)

    returning, member, inverse = pl.pallas_call(
        first_owner_kernel,
        out_shape=[shape((slots, snaps)), shape((slots, 128), BF16), shape((128, 128))],
        name="first_owner",
    )(exchange(outgoing))
    agreed = exchange(returning)
    for _ in range(1, ITERS):
        local, blend = pl.pallas_call(
            local_kernel,
            out_shape=[shape((slots, snaps)), shape((slots, snaps), BF16)],
            name="local",
        )(agreed, local, term, base, mat)
        returning, consensus = pl.pallas_call(
            owner_kernel,
            out_shape=[shape((slots, snaps)), shape((VAR_DEV, snaps))],
            name="owner",
        )(exchange(local), member, inverse)
        agreed = exchange(returning)
    states = pl.pallas_call(
        states_kernel,
        grid=(areas,),
        in_specs=[
            pl.BlockSpec((state, snaps), lambda a: (a, 0)),
            pl.BlockSpec((1, state, bound), lambda a: (a, 0, 0)),
            pl.BlockSpec((slots, bound), lambda a: (0, a)),
            whole(slots, snaps),
        ],
        out_specs=pl.BlockSpec((state, snaps), lambda a: (a, 0)),
        out_shape=shape((areas * state, snaps)),
        name="states",
    )(inner, cols, place, blend)
    dual = pl.pallas_call(
        dual_kernel, out_shape=shape((entries, snaps)), name="dual"
    )(agreed, local, place)
    return states, consensus, dual


def solution(mesh):
    both = ("area", "tie")
    return jax.shard_map(
        on_device,
        mesh=mesh,
        in_specs=(P(both, None, None), P(both, None), P(both, None), P(both, None)),
        out_specs=(P(both, None), P(both, None), P(both, None)),
        check_vma=False,
    )
```

time: 227 us -> 174 us (0.77)
  Pallas kernels: 0 us -> 38.4 us
  matrix products: 33.6 us -> 0 us
  local copies, waits for them, and re-layouts: 32.7 us -> 0.71 us
  blocking collectives: 91.9 us -> 123 us
  starting transfers between devices: 25.7 us -> 4.42 us
  other arithmetic: 20.7 us -> 0 us
  waiting for transfers between devices: 20.4 us -> 6.14 us
    pallas_call x0 -> x10, Pallas kernels: none -> 38.4 us  [the longest x1 14.9 us: on_device(): pl.pallas_call(prepare_kernel, grid=(areas,), in_specs=[whole(areas, boun...]
    dot_general x12 -> x0, matrix products: 33.6 us -> none  [the longest x4 30.4 us: on_device(): jnp.einsum('aij,ajs->ais', ginv, blended, preferred_element_type=jnp.floa...]
    all_to_all x6 -> x7, blocking collectives: 91.9 us -> 123 us  [exchange(): lax.all_to_all(x, ('area', 'tie'), split_axis=0, concat_axis=0, tiled=True)]
    all_to_all x3 -> x1, starting transfers between devices: 25.7 us -> 4.42 us  [exchange(): lax.all_to_all(x, ('area', 'tie'), split_axis=0, concat_axis=0, tiled=True)]
    scatter-add x4 -> x0, other arithmetic: 17.1 us -> none  [on_device(): jnp.zeros((area_dev * state_size, snap_count), jnp.float32).at[state_row]]
    gather x13 -> x0, local copies, waits for them, and re-layouts: 15.3 us -> none  [the longest x4 4.76 us: on_device(): outgoing = jnp.concatenate([local_part, zero_row])[entry_of_slot]]
    all_to_all x3 -> x1, waiting for transfers between devices: 20.4 us -> 6.14 us  [exchange(): lax.all_to_all(x, ('area', 'tie'), split_axis=0, concat_axis=0, tiled=True)]
    dot_general x4 -> x0, local copies, waits for them, and re-layouts: 7.62 us -> none  [on_device(): jnp.einsum('aij,ajs->ais', ginv, blended, preferred_element_type=jnp.floa...]
  transfers between devices with their start and end apart: 3 -> 1, of which waited for: 2 -> 1; matrix products, arithmetic and copies ran while one was open for 10% -> 0% of each run, Pallas kernels for 0% -> 3%
where the time goes in v1:
time: 174 us; the launch traced here: 173 us
  blocking collectives  123 us (71%)
  Pallas kernels  38.4 us (22%)
  waiting for transfers between devices  6.14 us (4%)
  starting transfers between devices  4.42 us (3%)
    all_to_all x7, blocking collectives, exchange(): lax.all_to_all(x, ('area', 'tie'), split_axis=0, concat_axis=0, tiled=True)  123 us
    pallas_call x1, Pallas kernels, on_device(): pl.pallas_call(prepare_kernel, grid=(areas,), in_specs=[whole(areas, boun...  14.9 us
    pallas_call x3, Pallas kernels, on_device(): pl.pallas_call(local_kernel, out_shape=[shape((slots, snaps)), shape((slo...  7.12 us
    pallas_call x3, Pallas kernels, on_device(): pl.pallas_call(owner_kernel, out_shape=[shape((slots, snaps)), shape((VAR...  6.68 us
    all_to_all x1, waiting for transfers between devices, exchange(): lax.all_to_all(x, ('area', 'tie'), split_axis=0, concat_axis=0, tiled=True)  6.14 us
    pallas_call x1, Pallas kernels, on_device(): pl.pallas_call(states_kernel, grid=(areas,), in_specs=[pl.BlockSpec((stat...  4.93 us
    all_to_all x1, starting transfers between devices, exchange(): lax.all_to_all(x, ('area', 'tie'), split_axis=0, concat_axis=0, tiled=True)  4.42 us
  transfers between devices with their start and end apart: 1, of which 1 were waited for; matrix products, arithmetic and copies ran while one was open for 0% of the time, Pallas kernels for 3%

profile of v1, /device:TPU:1, one launch (start us, length us, event | category | flops | bytes accessed | tf_op | source)
XLA Modules:
  0.0 173.2 jit_solution(17045116592078057011)
XLA Ops:
  0.6 14.9 %prepare.1 = (f32[4096,128]{1,0:T(8,128)}, bf16[4,1024,128]{2,1,0:T(8,128)(2,1)}, bf16[512,512]{1,0:T(8,128)(2,1)}, bf16[512,512]{1,0:T(8,128)(2,1)}, f32[512,12...) custom-call(s32[4,128]{1,0:T(4,128)} %row_ref.1, s32[4,128]{1,0:T(4,128)} %var_ref.1, ...), custom_call_target="tpu_custom_call" | custom-call | tf_op jit(solution)/shard_map/prepare/pallas_call | solution.py:184
  15.5 25.2 %all_to_all.40 = f32[128,8,128]{2,1,0:T(8,128)} all-to-all(f32[128,8,128]{2,1,0:T(8,128)} %bitcast.27), channel_id=1, replica_groups=mesh['area'=16,'tie'=8] {'area','tie'}, dimensions={0} | all-to-all | bytes 1048576 | tf_op jit(solution)/shard_map/all_to_all | solution.py:224
  40.7 2.5 %first_owner.1 = (f32[512,128]{1,0:T(8,128)}, bf16[512,128]{1,0:T(8,128)(2,1)}, f32[128,128]{1,0:T(8,128)}) custom-call(f32[1024,128]{1,0:T(8,128)} %bitcast.16), custom_call_target="tpu_custom_call" | custom-call | tf_op jit(solution)/shard_map/first_owner/pallas_call | solution.py:227
  43.2 16.5 %all_to_all.41 = f32[128,4,128]{2,1,0:T(4,128)} all-to-all(f32[128,4,128]{2,1,0:T(4,128)} %bitcast.29), channel_id=1, replica_groups=mesh['area'=16,'tie'=8] {'area','tie'}, dimensions={0} | all-to-all | bytes 524288 | tf_op jit(solution)/shard_map/all_to_all | solution.py:224
  59.7 2.4 %local.3 = (f32[512,128]{1,0:T(8,128)}, bf16[512,128]{1,0:T(8,128)(2,1)}) custom-call(f32[512,128]{1,0:T(8,128)} %bitcast.25, f32[512,128]{1,0:T(8,128)} %get-tuple-element.27.local_ref, f32[512,128]{1,0:T(8,128)} %get-tuple-element.28.term_ref, f32[512,128]{1,0:T(8,128)} %get-tuple-element.29.base_ref, bf16[512,512]{1,0:T(8,128)(2,1)} %get-tuple-element.30.mat_ref), custom_call_target="tpu_custom_call" | custom-call | tf_op jit(solution)/shard_map/local/pallas_call | solution.py:234
  62.1 16.2 %all_to_all.42 = f32[128,4,128]{2,1,0:T(4,128)} all-to-all(f32[128,4,128]{2,1,0:T(4,128)} %bitcast.23), channel_id=1, replica_groups=mesh['area'=16,'tie'=8] {'area','tie'}, dimensions={0} | all-to-all | bytes 524288 | tf_op jit(solution)/shard_map/all_to_all | solution.py:224
  78.3 2.2 %owner.3 = (f32[512,128]{1,0:T(8,128)}, f32[64,128]{1,0:T(8,128)}) custom-call(f32[512,128]{1,0:T(8,128)} %bitcast.20, bf16[512,128]{1,0:T(8,128)(2,1)} %get-tuple-element.32.member_ref, f32[128,128]{1,0:T(8,128)} %get-tuple-element.33.inverse_ref), custom_call_target="tpu_custom_call" | custom-call | tf_op jit(solution)/shard_map/owner/pallas_call | solution.py:239
  80.5 16.2 %all_to_all.43 = f32[128,4,128]{2,1,0:T(4,128)} all-to-all(f32[128,4,128]{2,1,0:T(4,128)} %bitcast.30), channel_id=1, replica_groups=mesh['area'=16,'tie'=8] {'area','tie'}, dimensions={0} | all-to-all | bytes 524288 | tf_op jit(solution)/shard_map/all_to_all | solution.py:224
  96.7 2.4 %local.4 = (f32[512,128]{1,0:T(8,128)}, bf16[512,128]{1,0:T(8,128)(2,1)}) custom-call(f32[512,128]{1,0:T(8,128)} %bitcast.26, f32[512,128]{1,0:T(8,128)} %get-tuple-element.31.local_ref, f32[512,128]{1,0:T(8,128)} %get-tuple-element.28.term_ref, f32[512,128]{1,0:T(8,128)} %get-tuple-element.29.base_ref, bf16[512,512]{1,0:T(8,128)(2,1)} %get-tuple-element.30.mat_ref), custom_call_target="tpu_custom_call" | custom-call | tf_op jit(solution)/shard_map/local/pallas_call | solution.py:234
  99.1 16.2 %all_to_all.44 = f32[128,4,128]{2,1,0:T(4,128)} all-to-all(f32[128,4,128]{2,1,0:T(4,128)} %bitcast.22), channel_id=1, replica_groups=mesh['area'=16,'tie'=8] {'area','tie'}, dimensions={0} | all-to-all | bytes 524288 | tf_op jit(solution)/shard_map/all_to_all | solution.py:224
  115.3 2.2 %owner.4 = (f32[512,128]{1,0:T(8,128)}, f32[64,128]{1,0:T(8,128)}) custom-call(f32[512,128]{1,0:T(8,128)} %bitcast.21, bf16[512,128]{1,0:T(8,128)(2,1)} %get-tuple-element.32.member_ref, f32[128,128]{1,0:T(8,128)} %get-tuple-element.33.inverse_ref), custom_call_target="tpu_custom_call" | custom-call | tf_op jit(solution)/shard_map/owner/pallas_call | solution.py:239
  117.6 16.2 %all_to_all.45 = f32[128,4,128]{2,1,0:T(4,128)} all-to-all(f32[128,4,128]{2,1,0:T(4,128)} %bitcast.31), channel_id=1, replica_groups=mesh['area'=16,'tie'=8] {'area','tie'}, dimensions={0} | all-to-all | bytes 524288 | tf_op jit(solution)/shard_map/all_to_all | solution.py:224
  133.8 2.4 %local.5 = (f32[512,128]{1,0:T(8,128)}, bf16[512,128]{1,0:T(8,128)(2,1)}) custom-call(f32[512,128]{1,0:T(8,128)} %bitcast.24, f32[512,128]{1,0:T(8,128)} %get-tuple-element.35.local_ref, f32[512,128]{1,0:T(8,128)} %get-tuple-element.28.term_ref, f32[512,128]{1,0:T(8,128)} %get-tuple-element.29.base_ref, bf16[512,512]{1,0:T(8,128)(2,1)} %get-tuple-element.30.mat_ref), custom_call_target="tpu_custom_call" | custom-call | tf_op jit(solution)/shard_map/local/pallas_call | solution.py:234
  136.2 16.2 %all_to_all.46 = f32[128,4,128]{2,1,0:T(4,128)} all-to-all(f32[128,4,128]{2,1,0:T(4,128)} %bitcast.17), channel_id=1, replica_groups=mesh['area'=16,'tie'=8] {'area','tie'}, dimensions={0} | all-to-all | bytes 524288 | tf_op jit(solution)/shard_map/all_to_all | solution.py:224
  152.4 2.2 %owner.5 = (f32[512,128]{1,0:T(8,128)}, f32[64,128]{1,0:T(8,128)}) custom-call(f32[512,128]{1,0:T(8,128)} %bitcast.19, bf16[512,128]{1,0:T(8,128)(2,1)} %get-tuple-element.32.member_ref, f32[128,128]{1,0:T(8,128)} %get-tuple-element.33.inverse_ref), custom_call_target="tpu_custom_call" | custom-call | tf_op jit(solution)/shard_map/owner/pallas_call | solution.py:239
  154.7 4.4 %all-to-all-start.7 = ((f32[128,4,128]{2,1,0:T(4,128)}), f32[128,4,128]{2,1,0:T(4,128)S(1)}, u32[]{:S(2)}, u32[]{:S(2)}) async-start(f32[128,4,128]{2,1,0:T(4,128)} %bitcast.28), calls=%async_computation.7 | async-start | bytes 524288 | tf_op jit(solution)/shard_map/all_to_all | solution.py:224
  159.1 4.9 %states.1 = f32[4096,128]{1,0:T(8,128)} custom-call(f32[4096,128]{1,0:T(8,128)} %get-tuple-element.22.inner_ref, bf16[4,1024,128]{2,1,0:T(8,128)(2,1)} %get-tuple-element.23.cols_ref, bf16[512,512]{1,0:T(8,128)(2,1)} %get-tuple-element.24.place_ref, bf16[512,128]{1,0:T(8,128)(2,1)} %get-tuple-element.37.blend_ref), custom_call_target="tpu_custom_call" | custom-call | tf_op jit(solution)/shard_map/states/pallas_call | solution.py:245
  164.0 6.1 %all-to-all-done.7 = f32[128,4,128]{2,1,0:T(4,128)S(1)} async-done(((f32[128,4,128]{2,1,0:T(4,128)}), f32[128,4,128]{2,1,0:T(4,128)S(1)}, u32[]{:S(2)}, u32[]{:S(2)}) %all-to-all-start.7) | async-done | bytes 262176 | tf_op jit(solution)/shard_map/all_to_all | solution.py:224
  170.2 0.0 copy-start
  170.2 0.7 copy-done
  170.9 2.4 %dual.1 = f32[512,128]{1,0:T(8,128)} custom-call(f32[512,128]{1,0:T(8,128)} %bitcast.18, f32[512,128]{1,0:T(8,128)} %get-tuple-element.38.local_ref, bf16[512,512]{1,0:T(8,128)(2,1)} %get-tuple-element.24.place_ref), custom_call_target="tpu_custom_call" | custom-call | tf_op jit(solution)/shard_map/dual/pallas_call | solution.py:258
Async XLA Ops:
  154.7 15.5 %all-to-all-start.7 = ((f32[128,4,128]{2,1,0:T(4,128)}), f32[128,4,128]{2,1,0:T(4,128)S(1)}, u32[]{:S(2)}, u32[]{:S(2)}) async-start(f32[128,4,128]{2,1,0:T(4,128)} %bitcast.28), calls=%async_computation.7 | async-start | bytes 524288 | tf_op jit(solution)/shard_map/all_to_all | solution.py:224
  170.2 0.7 copy-start

commit v2 on v1

v2 whole, which is shorter than its diff:
```python
import jax
import jax.numpy as jnp
from jax import lax
from jax.experimental import pallas as pl
from jax.experimental.pallas import tpu as pltpu
from jax.sharding import PartitionSpec as P

SLOT = 4
VAR_DEV = 64
ITERS = 4
PENALTY = 1.0
WIDE = 8

F32 = jnp.float32
BF16 = jnp.bfloat16


def split3(x):
    hi = x.astype(BF16)
    rest = x - hi.astype(F32)
    mid = rest.astype(BF16)
    low = (rest - mid.astype(F32)).astype(BF16)
    return [hi, mid, low]


def join3(y, at=0, width=128):
    return (y[:, at : at + width] + y[:, at + width : at + 2 * width]) + y[
        :, at + 2 * width : at + 3 * width
    ]


def dot(a, b):
    return jnp.dot(a, b, preferred_element_type=F32)


def dot_t(a, b):
    return lax.dot_general(a, b, (((0,), (0,)), ((), ())), preferred_element_type=F32)


def dot_nt(a, b):
    return lax.dot_general(a, b, (((1,), (1,)), ((), ())), preferred_element_type=F32)


def iota(shape, dim):
    return lax.broadcasted_iota(jnp.int32, shape, dim)


def entry_slots(row, var, carry_ref, owners):
    bound = row.shape[1]
    live = row >= 0
    owner = jnp.where(live, lax.shift_right_arithmetic(var, 6), -1)
    owned = iota((owners, bound), 0) == owner
    owned_f = owned.astype(F32)
    before = (iota((bound, bound), 0) < iota((bound, bound), 1)).astype(F32).astype(BF16)
    earlier = dot(owned_f.astype(BF16), before)
    rank = jnp.sum(jnp.where(owned, earlier + carry_ref[...], 0.0), axis=0, keepdims=True)
    carry_ref[...] += jnp.sum(owned_f, axis=1, keepdims=True)
    return jnp.where(live, owner * SLOT + rank.astype(jnp.int32), -1)


def placing(slot, slots):
    return (iota((slots, slot.shape[1]), 0) == slot).astype(F32).astype(BF16)


def picking(row, state):
    bound = row.shape[1]
    down = jnp.broadcast_to(row.astype(F32), (bound, bound)).T.astype(jnp.int32)
    lane = iota((bound, bound), 1)
    parts = [(lane + at == down).astype(F32) for at in range(0, state, bound)]
    return jnp.concatenate(parts, axis=1).astype(BF16)


def start_kernel(row_ref, var_ref, ginv_ref, rhs_ref, local_ref, out_ref, carry_ref, ids_ref):
    area = pl.program_id(0)
    slots = local_ref.shape[0]
    owners = slots // SLOT

    @pl.when(area == 0)
    def _():
        carry_ref[...] = jnp.zeros_like(carry_ref)
        ids_ref[...] = jnp.zeros_like(ids_ref)
        local_ref[...] = jnp.zeros_like(local_ref)

    row = row_ref[pl.ds(area, 1), :]
    var = var_ref[pl.ds(area, 1), :]
    place = placing(entry_slots(row, var, carry_ref, owners), slots)
    local_id = jnp.where(row >= 0, (var & (VAR_DEV - 1)) + 1, 0).astype(F32)
    ids_ref[...] += dot_nt(place, jnp.broadcast_to(local_id, (128, row.shape[1])).astype(BF16))
    picks = picking(row, ginv_ref.shape[1])
    chosen = dot(picks, ginv_ref[0]).astype(BF16)
    solved = dot(chosen, rhs_ref[...].astype(BF16))
    local_ref[...] += join3(dot(place, jnp.concatenate(split3(solved), axis=1)))

    @pl.when(area == pl.num_programs(0) - 1)
    def _():
        for k in range(SLOT):
            at = pl.ds(k, owners, stride=SLOT)
            out_ref[pl.ds(k, owners, stride=WIDE), :] = local_ref[at, :]
            out_ref[pl.ds(SLOT + k, owners, stride=WIDE), :] = ids_ref[at, :]


def prepare_kernel(
    row_ref, var_ref, ginv_ref, rhs_ref,
    inner_ref, cols_ref, place_ref, mat_ref, base_ref, term_ref,
    carry_ref, acc_ref,
):
    area = pl.program_id(0)
    slots = mat_ref.shape[0]

    @pl.when(area == 0)
    def _():
        carry_ref[...] = jnp.zeros_like(carry_ref)
        acc_ref[...] = jnp.zeros_like(acc_ref)
        base_ref[...] = jnp.zeros_like(base_ref)
        term_ref[...] = jnp.zeros_like(term_ref)

    row = row_ref[pl.ds(area, 1), :]
    var = var_ref[pl.ds(area, 1), :]
    place = placing(entry_slots(row, var, carry_ref, slots // SLOT), slots)
    place_ref[...] = place
    picks_f = (iota((ginv_ref.shape[1], row.shape[1]), 0) == row).astype(F32)
    picks = picks_f.astype(BF16)
    is_bound = jnp.sum(picks_f, axis=1, keepdims=True) > 0.0
    rhs = rhs_ref[...]
    inner = jnp.where(is_bound, 0.0, rhs).astype(BF16)
    both = dot(ginv_ref[0], jnp.concatenate([inner, picks], axis=1))
    snaps = rhs.shape[1]
    solved = both[:, :snaps]
    cols = both[:, snaps:].astype(BF16)
    inner_ref[...] = solved
    cols_ref[0] = cols
    at_rows = dot_t(picks, jnp.concatenate(split3(solved) + split3(rhs) + [cols], axis=1))
    at_slots = dot(place, at_rows.astype(BF16))
    base_ref[...] += join3(at_slots, 0, snaps)
    term_ref[...] += join3(at_slots, 3 * snaps, snaps)
    acc_ref[...] += dot_nt(at_slots[:, 6 * snaps :].astype(BF16), place)

    @pl.when(area == pl.num_programs(0) - 1)
    def _():
        mat_ref[...] = acc_ref[...].astype(BF16)


def states_kernel(inner_ref, cols_ref, place_ref, blend_ref, states_ref):
    rows = dot_t(place_ref[...], blend_ref[...]).astype(BF16)
    states_ref[...] = inner_ref[...] + dot(cols_ref[0], rows)


def exact(spec, a, b):
    return jnp.einsum(spec, a, b, precision=lax.Precision.HIGHEST, preferred_element_type=F32)


def shape(dims, dtype=F32):
    return jax.ShapeDtypeStruct(dims, dtype)


def on_device(ginv, rhs, bnd_row, bnd_var):
    areas, state, _ = ginv.shape
    snaps = rhs.shape[1]
    bound = bnd_row.shape[1]
    devices = lax.axis_size("area") * lax.axis_size("tie")
    slots = devices * SLOT
    entries = areas * bound

    def whole(*dims):
        return pl.BlockSpec(dims, lambda a: (0,) * len(dims))

    in_specs = [
        whole(areas, bound),
        whole(areas, bound),
        pl.BlockSpec((1, state, state), lambda a: (a, 0, 0)),
        pl.BlockSpec((state, snaps), lambda a: (a, 0)),
    ]
    in_order = pltpu.CompilerParams(dimension_semantics=("arbitrary",))
    local, outgoing = pl.pallas_call(
        start_kernel,
        grid=(areas,),
        in_specs=in_specs,
        out_specs=[whole(slots, snaps), whole(devices * WIDE, snaps)],
        out_shape=[shape((slots, snaps)), shape((devices * WIDE, snaps))],
        scratch_shapes=[pltpu.VMEM((devices, bound), F32), pltpu.VMEM((slots, snaps), F32)],
        compiler_params=in_order,
        name="start",
    )(bnd_row, bnd_var, ginv, rhs)
    inner, cols, place, mat, base, term = pl.pallas_call(
        prepare_kernel,
        grid=(areas,),
        in_specs=in_specs,
        out_specs=[
            pl.BlockSpec((state, snaps), lambda a: (a, 0)),
            pl.BlockSpec((1, state, bound), lambda a: (a, 0, 0)),
            pl.BlockSpec((slots, bound), lambda a: (0, a)),
            whole(slots, slots),
            whole(slots, snaps),
            whole(slots, snaps),
        ],
        out_shape=[
            shape((areas * state, snaps)),
            shape((areas, state, bound), BF16),
            shape((slots, entries), BF16),
            shape((slots, slots), BF16),
            shape((slots, snaps)),
            shape((slots, snaps)),
        ],
        scratch_shapes=[pltpu.VMEM((devices, bound), F32), pltpu.VMEM((slots, slots), F32)],
        compiler_params=in_order,
        name="prepare",
    )(bnd_row, bnd_var, ginv, rhs)

    def exchange(x):
        x = x.reshape(devices, -1, snaps)
        return lax.all_to_all(x, ("area", "tie"), split_axis=0, concat_axis=0, tiled=True)

    received = exchange(outgoing)
    incoming = received[:, :SLOT].reshape(slots, snaps)
    ids = received[:, SLOT:].reshape(slots, snaps)[:, :VAR_DEV]
    member = (ids == jnp.arange(1, VAR_DEV + 1, dtype=jnp.int32).astype(F32)).astype(F32)
    inverse = 1.0 / jnp.maximum(jnp.sum(member, axis=0), 1.0)[:, None]
    for iteration in range(ITERS):
        if iteration > 0:
            blend = (term + PENALTY * (agreed - dual)).astype(BF16)
            local = (base + dot(mat, blend)) + dual
            incoming = exchange(local).reshape(slots, snaps)
        consensus = exact("sv,sn->vn", member, incoming) * inverse
        agreed = exchange(exact("sv,vn->sn", member, consensus)).reshape(slots, snaps)
        dual = local - agreed
    states = pl.pallas_call(
        states_kernel,
        grid=(areas,),
        in_specs=[
            pl.BlockSpec((state, snaps), lambda a: (a, 0)),
            pl.BlockSpec((1, state, bound), lambda a: (a, 0, 0)),
            pl.BlockSpec((slots, bound), lambda a: (0, a)),
            whole(slots, snaps),
        ],
        out_specs=pl.BlockSpec((state, snaps), lambda a: (a, 0)),
        out_shape=shape((areas * state, snaps)),
        name="states",
    )(inner, cols, place, blend)
    dual = exact("se,sn->en", place.astype(F32), dual)
    return states, consensus, dual


def solution(mesh):
    both = ("area", "tie")
    return jax.shard_map(
        on_device,
        mesh=mesh,
        in_specs=(P(both, None, None), P(both, None), P(both, None), P(both, None)),
        out_specs=(P(both, None), P(both, None), P(both, None)),
        check_vma=False,
    )
```

time: 174 us -> 157 us (0.902)
  blocking collectives: 123 us -> 81.9 us
  starting transfers between devices: 4.42 us -> 20.4 us
  waiting for transfers between devices: 6.14 us -> 19.7 us
  Pallas kernels: 38.4 us -> 26.2 us
  matrix products: 0 us -> 7.49 us
    all_to_all x7 -> x5, blocking collectives: 123 us -> 81.9 us  [exchange(): lax.all_to_all(x, ('area', 'tie'), split_axis=0, concat_axis=0, tiled=True)]
    all_to_all x1 -> x3, starting transfers between devices: 4.42 us -> 20.4 us  [exchange(): lax.all_to_all(x, ('area', 'tie'), split_axis=0, concat_axis=0, tiled=True)]
    all_to_all x1 -> x3, waiting for transfers between devices: 6.14 us -> 19.7 us  [exchange(): lax.all_to_all(x, ('area', 'tie'), split_axis=0, concat_axis=0, tiled=True)]
    pallas_call x9 -> x2, Pallas kernels: 33.5 us -> 21.3 us  [the longest x1 13.7 us: on_device(): pl.pallas_call(prepare_kernel, grid=(areas,), in_specs=in_specs, out_spec...]
    dot_general x0 -> x12, matrix products: none -> 7.49 us  [the longest x9 5.32 us: exact(): jnp.einsum(spec, a, b, precision=lax.Precision.HIGHEST, preferred_element...]
  transfers between devices with their start and end apart: 1 -> 3, of which waited for: 1 -> 2; matrix products, arithmetic and copies ran while one was open for 0% -> 0% of each run, Pallas kernels for 3% -> 12%
where the time goes in v2:
time: 157 us
  blocking collectives  81.9 us (52%)
  Pallas kernels  26.2 us (17%)
  starting transfers between devices  20.4 us (13%)
  waiting for transfers between devices  19.7 us (13%)
  matrix products  7.49 us (5%)
    all_to_all x5, blocking collectives, exchange(): lax.all_to_all(x, ('area', 'tie'), split_axis=0, concat_axis=0, tiled=True)  81.9 us
    all_to_all x3, starting transfers between devices, exchange(): lax.all_to_all(x, ('area', 'tie'), split_axis=0, concat_axis=0, tiled=True)  20.4 us
    all_to_all x3, waiting for transfers between devices, exchange(): lax.all_to_all(x, ('area', 'tie'), split_axis=0, concat_axis=0, tiled=True)  19.7 us
    pallas_call x1, Pallas kernels, on_device(): pl.pallas_call(prepare_kernel, grid=(areas,), in_specs=in_specs, out_spec...  13.7 us
    pallas_call x1, Pallas kernels, on_device(): pl.pallas_call(start_kernel, grid=(areas,), in_specs=in_specs, out_specs=...  7.62 us
    dot_general x9, matrix products, exact(): jnp.einsum(spec, a, b, precision=lax.Precision.HIGHEST, preferred_element...  5.32 us
    pallas_call x1, Pallas kernels, on_device(): pl.pallas_call(states_kernel, grid=(areas,), in_specs=[pl.BlockSpec((stat...  4.97 us
  transfers between devices with their start and end apart: 3, of which 2 were waited for; matrix products, arithmetic and copies ran while one was open for 0% of the time, Pallas kernels for 12%

profile of v2, /device:TPU:1, one launch (start us, length us, event | category | flops | bytes accessed | tf_op | source)
XLA Modules:
  0.0 156.8 jit_solution(6742662035541933242)
XLA Ops:
  0.6 7.6 %start.1 = (f32[512,128]{1,0:T(8,128)}, f32[1024,128]{1,0:T(8,128)}) custom-call(s32[4,128]{1,0:T(4,128)} %row_ref.3, s32[4,128]{1,0:T(4,128)} %var_ref.3, bf16[4,1024,1024]{2,1,0:T(8,128)(2,1)} %ginv_ref.3, f32[4096,128]{1,0:T(8,128)} %rhs_ref.3), custom_call_target="tpu_custom_call" | custom-call | tf_op jit(solution)/shard_map/start/pallas_call | solution.py:174
  8.3 11.5 %all-to-all-start = ((f32[128,8,128]{2,1,0:T(8,128)}), f32[128,8,128]{2,1,0:T(8,128)S(1)}, u32[]{:S(2)}, u32[]{:S(2)}) async-start(f32[128,8,128]{2,1,0:T(8,128)} %bitcast.53), calls=%async_computation | async-start | bytes 1048576 | tf_op jit(solution)/shard_map/all_to_all | solution.py:211
  19.8 13.6 %all-to-all-done = f32[128,8,128]{2,1,0:T(8,128)S(1)} async-done(((f32[128,8,128]{2,1,0:T(8,128)}), f32[128,8,128]{2,1,0:T(8,128)S(1)}, u32[]{:S(2)}, u32[]{:S(2)}) %all-to-all-start) | async-done | bytes 524320 | tf_op jit(solution)/shard_map/all_to_all | solution.py:211
  33.4 0.1 fusion.7
  33.4 0.1 convert_reduce_fusion
  33.5 0.4 convolution_multiply_fusion.3
  33.9 1.0 fusion.8
  34.9 4.6 %all-to-all-start.1 = ((f32[128,4,128]{2,1,0:T(4,128)}), f32[128,4,128]{2,1,0:T(4,128)S(1)}, u32[]{:S(2)}, u32[]{:S(2)}) async-start(f32[128,4,128]{2,1,0:T(4,128)} %bitcast.3), calls=%async_computation.1 | async-start | bytes 524288 | tf_op jit(solution)/shard_map/all_to_all | solution.py:211
  39.5 13.7 %prepare.1 = (f32[4096,128]{1,0:T(8,128)}, bf16[4,1024,128]{2,1,0:T(8,128)(2,1)}, bf16[512,512]{1,0:T(8,128)(2,1)}, bf16[512,512]{1,0:T(8,128)(2,1)}, f32[512,128]{1,0:T(8,128)}, /*index=5*/f32[512,128]{1,0:T(8,128)}) custom-call(s32[4,128]{1,0:T(4,128)} %row_ref.3, s32[4,128]{1,0:T(4,128)} %var_ref.3, bf16[4,1024,1024]{2,1,0:T(8,128)(2,1)} %ginv_ref.3, ...), custom_call_target="tpu_custom_call" | custom-call | tf_op jit(solution)/shard_map/prepare/pallas_call | solution.py:184
  53.2 0.0 copy-start
  53.2 0.0 copy-start.2
  53.2 0.0 all-to-all-done.1
  53.2 1.6 %fusion = f32[512,128]{1,0:T(8,128)S(1)} fusion(f32[512,128]{1,0:T(8,128)} %get-tuple-element.16, bf16[512,512]{1,0:T(8,128)(2,1)} %get-tuple-element.17, f32[512,128]{1,0:T(8,128)} %get-tuple-element.14, f32[512,128]{1,0:T(8,128)S(1)} %bitcast.43, f32[512,128]{1,0:T(8,128)S(1)} %copy-done.5), kind=kOutput, calls=%fused_computation.3 | convolution fusion | flops 67567616 | bytes 1835008 | tf_op jit(solution)/shard_map/dot_general | solution.py:33
  54.8 20.7 %all_to_all.40 = f32[128,4,128]{2,1,0:T(4,128)S(1)} all-to-all(f32[128,4,128]{2,1,0:T(4,128)S(1)} %bitcast.39), channel_id=1, replica_groups=mesh['area'=16,'tie'=8] {'area','tie'}, dimensions={0} | all-to-all | bytes 524288 | tf_op jit(solution)/shard_map/all_to_all | solution.py:211
  75.5 0.4 convolution_multiply_fusion.2
  75.9 0.3 fusion.9
  76.2 15.3 %all_to_all.41 = f32[128,4,128]{2,1,0:T(4,128)S(1)} all-to-all(f32[128,4,128]{2,1,0:T(4,128)S(1)} %bitcast.46), channel_id=1, replica_groups=mesh['area'=16,'tie'=8] {'area','tie'}, dimensions={0} | all-to-all | bytes 524288 | tf_op jit(solution)/shard_map/all_to_all | solution.py:211
  91.5 0.3 fusion.1
  91.8 15.3 %all_to_all.42 = f32[128,4,128]{2,1,0:T(4,128)S(1)} all-to-all(f32[128,4,128]{2,1,0:T(4,128)S(1)} %bitcast.38), channel_id=1, replica_groups=mesh['area'=16,'tie'=8] {'area','tie'}, dimensions={0} | all-to-all | bytes 524288 | tf_op jit(solution)/shard_map/all_to_all | solution.py:211
  107.1 0.4 convolution_multiply_fusion.1
  107.5 0.3 fusion.10
  107.7 15.3 %all_to_all.43 = f32[128,4,128]{2,1,0:T(4,128)S(1)} all-to-all(f32[128,4,128]{2,1,0:T(4,128)S(1)} %bitcast.47), channel_id=1, replica_groups=mesh['area'=16,'tie'=8] {'area','tie'}, dimensions={0} | all-to-all | bytes 524288 | tf_op jit(solution)/shard_map/all_to_all | solution.py:211
  123.1 0.0 copy-start.4
  123.1 0.3 fusion.2
  123.4 15.3 %all_to_all.44 = f32[128,4,128]{2,1,0:T(4,128)S(1)} all-to-all(f32[128,4,128]{2,1,0:T(4,128)S(1)} %bitcast.40), channel_id=1, replica_groups=mesh['area'=16,'tie'=8] {'area','tie'}, dimensions={0} | all-to-all | bytes 524288 | tf_op jit(solution)/shard_map/all_to_all | solution.py:211
  138.7 0.4 convolution_multiply_fusion
  139.1 0.0 copy-start.6
  139.1 1.0 fusion.11
  140.0 4.3 %all-to-all-start.7 = ((f32[128,4,128]{2,1,0:T(4,128)}), f32[128,4,128]{2,1,0:T(4,128)S(1)}, u32[]{:S(2)}, u32[]{:S(2)}) async-start(f32[128,4,128]{2,1,0:T(4,128)} %bitcast.15), calls=%async_computation.7 | async-start | bytes 524288 | tf_op jit(solution)/shard_map/all_to_all | solution.py:211
  144.4 5.0 %states.1 = f32[4096,128]{1,0:T(8,128)} custom-call(f32[4096,128]{1,0:T(8,128)} %get-tuple-element.11.inner_ref, bf16[4,1024,128]{2,1,0:T(8,128)(2,1)} %get-tuple-element.12.cols_ref, bf16[512,512]{1,0:T(8,128)(2,1)} %get-tuple-element.13.place_ref, bf16[512,128]{1,0:T(8,128)(2,1)} %copy-done.4), custom_call_target="tpu_custom_call" | custom-call | tf_op jit(solution)/shard_map/states/pallas_call | solution.py:226
  149.3 6.1 %all-to-all-done.7 = f32[128,4,128]{2,1,0:T(4,128)S(1)} async-done(((f32[128,4,128]{2,1,0:T(4,128)}), f32[128,4,128]{2,1,0:T(4,128)S(1)}, u32[]{:S(2)}, u32[]{:S(2)}) %all-to-all-start.7) | async-done | bytes 262176 | tf_op jit(solution)/shard_map/all_to_all | solution.py:211
  155.4 1.4 fusion.3
  (13 shorter events, 0.1 us)
Async XLA Ops:
  8.3 25.1 %all-to-all-start = ((f32[128,8,128]{2,1,0:T(8,128)}), f32[128,8,128]{2,1,0:T(8,128)S(1)}, u32[]{:S(2)}, u32[]{:S(2)}) async-start(f32[128,8,128]{2,1,0:T(8,128)} %bitcast.53), calls=%async_computation | async-start | bytes 1048576 | tf_op jit(solution)/shard_map/all_to_all | solution.py:211
  34.9 18.3 %all-to-all-start.1 = ((f32[128,4,128]{2,1,0:T(4,128)}), f32[128,4,128]{2,1,0:T(4,128)S(1)}, u32[]{:S(2)}, u32[]{:S(2)}) async-start(f32[128,4,128]{2,1,0:T(4,128)} %bitcast.3), calls=%async_computation.1 | async-start | bytes 524288 | tf_op jit(solution)/shard_map/all_to_all | solution.py:211
  39.5 13.7 %copy-start.5 = (f32[512,128]{1,0:T(8,128)S(1)}, f32[512,128]{1,0:T(8,128)}, u32[]{:S(2)}) copy-start(f32[512,128]{1,0:T(8,128)} %get-tuple-element.18) | copy-start | bytes 786436
  53.2 38.3 %copy-start = (bf16[512,512]{1,0:T(8,128)(2,1)S(1)}, bf16[512,512]{1,0:T(8,128)(2,1)}, u32[]{:S(2)}) copy-start(bf16[512,512]{1,0:T(8,128)(2,1)} %get-tuple-element.17) | copy-start | bytes 1572868
  53.2 38.3 %copy-start.1 = (f32[512,128]{1,0:T(8,128)S(1)}, f32[512,128]{1,0:T(8,128)}, u32[]{:S(2)}) copy-start(f32[512,128]{1,0:T(8,128)} %get-tuple-element.14) | copy-start | bytes 786436
  53.2 38.3 %copy-start.2 = (f32[512,128]{1,0:T(8,128)S(1)}, f32[512,128]{1,0:T(8,128)}, u32[]{:S(2)}) copy-start(f32[512,128]{1,0:T(8,128)} %get-tuple-element.16) | copy-start | bytes 786436
  123.1 21.3 %copy-start.4 = (bf16[512,128]{1,0:T(8,128)(2,1)}, bf16[512,128]{1,0:T(8,128)(2,1)S(1)}, u32[]{:S(2)}) copy-start(bf16[512,128]{1,0:T(8,128)(2,1)S(1)} %add_convert_fusion.blend_ref) | copy-start | bytes 393220
  139.1 10.3 %copy-start.6 = (f32[64,128]{1,0:T(8,128)}, f32[64,128]{1,0:T(8,128)S(1)}, u32[]{:S(2)}) copy-start(f32[64,128]{1,0:T(8,128)S(1)} %convolution_multiply_fusion) | copy-start | bytes 98308
  140.0 15.4 %all-to-all-start.7 = ((f32[128,4,128]{2,1,0:T(4,128)}), f32[128,4,128]{2,1,0:T(4,128)S(1)}, u32[]{:S(2)}, u32[]{:S(2)}) async-start(f32[128,4,128]{2,1,0:T(4,128)} %bitcast.15), calls=%async_computation.7 | async-start | bytes 524288 | tf_op jit(solution)/shard_map/all_to_all | solution.py:211
  144.4 11.1 %copy-start.3 = (bf16[512,512]{1,0:T(8,128)(2,1)S(1)}, bf16[512,512]{1,0:T(8,128)(2,1)}, u32[]{:S(2)}) copy-start(bf16[512,512]{1,0:T(8,128)(2,1)} %get-tuple-element.13.place_ref) | copy-start | bytes 1572868

commit v3 on v2

v3 whole, which is shorter than its diff:
```python
import jax
import jax.numpy as jnp
from jax import lax
from jax.experimental import pallas as pl
from jax.experimental.pallas import tpu as pltpu
from jax.sharding import PartitionSpec as P

SLOT = 4
VAR_DEV = 64
ITERS = 4
PENALTY = 1.0
HALVES = 2
WIDE = 8

F32 = jnp.float32
BF16 = jnp.bfloat16


def split3(x):
    hi = x.astype(BF16)
    rest = x - hi.astype(F32)
    mid = rest.astype(BF16)
    low = (rest - mid.astype(F32)).astype(BF16)
    return [hi, mid, low]


def join3(y, at=0, width=128):
    return (y[:, at : at + width] + y[:, at + width : at + 2 * width]) + y[
        :, at + 2 * width : at + 3 * width
    ]


def dot(a, b):
    return jnp.dot(a, b, preferred_element_type=F32)


def dot_t(a, b):
    return lax.dot_general(a, b, (((0,), (0,)), ((), ())), preferred_element_type=F32)


def dot_nt(a, b):
    return lax.dot_general(a, b, (((1,), (1,)), ((), ())), preferred_element_type=F32)


def iota(shape, dim):
    return lax.broadcasted_iota(jnp.int32, shape, dim)


def entry_slots(row, var, carry_ref, owners):
    bound = row.shape[1]
    live = row >= 0
    owner = jnp.where(live, lax.shift_right_arithmetic(var, 6), -1)
    owned = iota((owners, bound), 0) == owner
    owned_f = owned.astype(F32)
    before = (iota((bound, bound), 0) < iota((bound, bound), 1)).astype(F32).astype(BF16)
    earlier = dot(owned_f.astype(BF16), before)
    rank = jnp.sum(jnp.where(owned, earlier + carry_ref[...], 0.0), axis=0, keepdims=True)
    carry_ref[...] += jnp.sum(owned_f, axis=1, keepdims=True)
    return jnp.where(live, owner * SLOT + rank.astype(jnp.int32), -1)


def placing(slot, slots):
    return (iota((slots, slot.shape[1]), 0) == slot).astype(F32).astype(BF16)


def picking(row, state):
    bound = row.shape[1]
    down = jnp.broadcast_to(row.astype(F32), (bound, bound)).T.astype(jnp.int32)
    lane = iota((bound, bound), 1)
    parts = [(lane + at == down).astype(F32) for at in range(0, state, bound)]
    return jnp.concatenate(parts, axis=1).astype(BF16)


def start_kernel(
    row_ref, var_ref, ginv_ref, rhs_ref, local_ref, out_ref, chosen_ref,
    block_ref, right_ref, carry_ref, block_sems, right_sems,
):
    areas = row_ref.shape[0]
    state = ginv_ref.shape[1]
    slots = local_ref.shape[0]
    owners = slots // SLOT
    half = state // HALVES

    def block_copy(area, at):
        rows = pl.ds(at * half, half)
        return pltpu.make_async_copy(
            ginv_ref.at[area, rows], block_ref.at[area, rows], block_sems.at[area * HALVES + at]
        )

    def right_copy(area):
        rows = pl.ds(area * state, state)
        return pltpu.make_async_copy(rhs_ref.at[rows], right_ref.at[rows], right_sems.at[area])

    for area in range(areas):
        for at in range(HALVES):
            block_copy(area, at).start()
        right_copy(area).start()
    carry_ref[...] = jnp.zeros_like(carry_ref)
    ids = jnp.zeros(local_ref.shape, F32)
    places = []
    picks = []
    for area in range(areas):
        row = row_ref[area : area + 1, :]
        var = var_ref[area : area + 1, :]
        places.append(placing(entry_slots(row, var, carry_ref, owners), slots))
        picks.append(picking(row, state))
        local_id = jnp.where(row >= 0, (var & (VAR_DEV - 1)) + 1, 0).astype(F32)
        ids += dot_nt(places[area], jnp.broadcast_to(local_id, (128, row.shape[1])).astype(BF16))
    local_ref[...] = ids
    for k in range(SLOT):
        at = pl.ds(k, owners, stride=SLOT)
        out_ref[pl.ds(SLOT + k, owners, stride=WIDE), :] = local_ref[at, :]
    local = jnp.zeros(local_ref.shape, F32)
    for area in range(areas):
        chosen = jnp.zeros((row_ref.shape[1], state), F32)
        for at in range(HALVES):
            block_copy(area, at).wait()
            rows = slice(at * half, (at + 1) * half)
            chosen += dot(picks[area][:, rows], block_ref[area, rows, :])
        chosen = chosen.astype(BF16)
        chosen_ref[area] = chosen
        right_copy(area).wait()
        solved = dot(chosen, right_ref[area * state : (area + 1) * state, :].astype(BF16))
        local += join3(dot(places[area], jnp.concatenate(split3(solved), axis=1)))
    local_ref[...] = local
    for k in range(SLOT):
        at = pl.ds(k, owners, stride=SLOT)
        out_ref[pl.ds(k, owners, stride=WIDE), :] = local_ref[at, :]


def prepare_kernel(
    row_ref, var_ref, chosen_ref, rhs_ref, local_ref,
    place_ref, mat_ref, base_ref, term_ref,
    carry_ref, acc_ref,
):
    area = pl.program_id(0)
    slots = mat_ref.shape[0]
    state, snaps = rhs_ref.shape

    @pl.when(area == 0)
    def _():
        carry_ref[...] = jnp.zeros_like(carry_ref)
        acc_ref[...] = jnp.zeros_like(acc_ref)
        term_ref[...] = jnp.zeros_like(term_ref)

    row = row_ref[pl.ds(area, 1), :]
    var = var_ref[pl.ds(area, 1), :]
    place = placing(entry_slots(row, var, carry_ref, slots // SLOT), slots)
    place_ref[...] = place
    at_rows = dot(picking(row, state), jnp.concatenate(split3(rhs_ref[...]), axis=1))
    coupling = dot(chosen_ref[0], placing(row, state))
    at_slots = dot(place, jnp.concatenate([at_rows, coupling], axis=1).astype(BF16))
    term_ref[...] += join3(at_slots, 0, snaps)
    acc_ref[...] += dot_nt(at_slots[:, 3 * snaps :].astype(BF16), place)

    @pl.when(area == pl.num_programs(0) - 1)
    def _():
        mat = acc_ref[...].astype(BF16)
        mat_ref[...] = mat
        base_ref[...] = local_ref[...] - dot(mat, term_ref[...].astype(BF16))


def states_kernel(row_ref, ginv_ref, rhs_ref, place_ref, blend_ref, states_ref):
    row = row_ref[pl.ds(pl.program_id(0), 1), :]
    state, snaps = rhs_ref.shape
    rows = dot_t(place_ref[...], blend_ref[...]).astype(BF16)
    placed = dot(placing(row, state), jnp.concatenate([rows, jnp.ones_like(rows)], axis=1))
    blended = jnp.where(placed[:, snaps:] > 0.0, placed[:, :snaps], rhs_ref[...])
    states_ref[...] = dot(ginv_ref[0], blended.astype(BF16))


def exact(spec, a, b):
    return jnp.einsum(spec, a, b, precision=lax.Precision.HIGHEST, preferred_element_type=F32)


def shape(dims, dtype=F32):
    return jax.ShapeDtypeStruct(dims, dtype)


def on_device(ginv, rhs, bnd_row, bnd_var):
    areas, state, _ = ginv.shape
    snaps = rhs.shape[1]
    bound = bnd_row.shape[1]
    devices = lax.axis_size("area") * lax.axis_size("tie")
    slots = devices * SLOT
    entries = areas * bound

    def whole(*dims):
        return pl.BlockSpec(dims, lambda a: (0,) * len(dims))

    in_order = pltpu.CompilerParams(dimension_semantics=("arbitrary",))
    anywhere = pl.BlockSpec(memory_space=pl.ANY)
    small = pl.BlockSpec((areas, bound), lambda: (0, 0))
    local, outgoing, chosen = pl.pallas_call(
        start_kernel,
        in_specs=[small, small, anywhere, anywhere],
        out_shape=[
            pltpu.VMEM((slots, snaps), F32),
            pltpu.VMEM((devices * WIDE, snaps), F32),
            pltpu.VMEM((areas, bound, state), BF16),
        ],
        scratch_shapes=[
            pltpu.VMEM((areas, state, state), BF16),
            pltpu.VMEM((areas * state, snaps), F32),
            pltpu.VMEM((devices, bound), F32),
            pltpu.SemaphoreType.DMA((areas * HALVES,)),
            pltpu.SemaphoreType.DMA((areas,)),
        ],
        name="start",
    )(bnd_row, bnd_var, ginv, rhs)
    place, mat, base, term = pl.pallas_call(
        prepare_kernel,
        grid=(areas,),
        in_specs=[
            whole(areas, bound),
            whole(areas, bound),
            pl.BlockSpec((1, bound, state), lambda a: (a, 0, 0)),
            pl.BlockSpec((state, snaps), lambda a: (a, 0)),
            whole(slots, snaps),
        ],
        out_specs=[
            pl.BlockSpec((slots, bound), lambda a: (0, a)),
            whole(slots, slots),
            whole(slots, snaps),
            whole(slots, snaps),
        ],
        out_shape=[
            pltpu.VMEM((slots, entries), BF16),
            pltpu.VMEM((slots, slots), BF16),
            pltpu.VMEM((slots, snaps), F32),
            pltpu.VMEM((slots, snaps), F32),
        ],
        scratch_shapes=[pltpu.VMEM((devices, bound), F32), pltpu.VMEM((slots, slots), F32)],
        compiler_params=in_order,
        name="prepare",
    )(bnd_row, bnd_var, chosen, rhs, local)

    def exchange(x):
        x = x.reshape(devices, -1, snaps)
        return lax.all_to_all(x, ("area", "tie"), split_axis=0, concat_axis=0, tiled=True)

    received, place, mat, base, term = lax.optimization_barrier(
        (exchange(outgoing), place, mat, base, term)
    )
    incoming = received[:, :SLOT].reshape(slots, snaps)
    ids = received[:, SLOT:].reshape(slots, snaps)[:, :VAR_DEV]
    member = (ids == jnp.arange(1, VAR_DEV + 1, dtype=jnp.int32).astype(F32)).astype(F32)
    inverse = 1.0 / jnp.maximum(jnp.sum(member, axis=0), 1.0)[:, None]
    for iteration in range(ITERS):
        if iteration > 0:
            blend = (term + PENALTY * (agreed - dual)).astype(BF16)
            local = (base + dot(mat, blend)) + dual
            incoming = exchange(local).reshape(slots, snaps)
        consensus = exact("sv,sn->vn", member, incoming) * inverse
        agreed = exchange(exact("sv,vn->sn", member, consensus)).reshape(slots, snaps)
        dual = local - agreed
    states = pl.pallas_call(
        states_kernel,
        grid=(areas,),
        in_specs=[
            whole(areas, bound),
            pl.BlockSpec((1, state, state), lambda a: (a, 0, 0)),
            pl.BlockSpec((state, snaps), lambda a: (a, 0)),
            pl.BlockSpec((slots, bound), lambda a: (0, a)),
            whole(slots, snaps),
        ],
        out_specs=pl.BlockSpec((state, snaps), lambda a: (a, 0)),
        out_shape=shape((areas * state, snaps)),
        compiler_params=in_order,
        name="states",
    )(bnd_row, ginv, rhs, place, blend)
    dual = exact("se,sn->en", place.astype(F32), dual)
    return states, consensus, dual


def solution(mesh):
    both = ("area", "tie")
    return jax.shard_map(
        on_device,
        mesh=mesh,
        in_specs=(P(both, None, None), P(both, None), P(both, None), P(both, None)),
        out_specs=(P(both, None), P(both, None), P(both, None)),
        check_vma=False,
    )
```

time: 157 us -> 148 us (0.943)
  blocking collectives: 81.9 us -> 92.1 us
  waiting for transfers between devices: 19.7 us -> 10.2 us
  starting transfers between devices: 20.4 us -> 15.8 us
  Pallas kernels: 26.2 us -> 22 us
  matrix products: 7.49 us -> 5.51 us
    all_to_all x5 -> x6, blocking collectives: 81.9 us -> 92.1 us  [exchange(): lax.all_to_all(x, ('area', 'tie'), split_axis=0, concat_axis=0, tiled=True)]
    all_to_all x3 -> x2, waiting for transfers between devices: 19.7 us -> 10.2 us  [exchange(): lax.all_to_all(x, ('area', 'tie'), split_axis=0, concat_axis=0, tiled=True)]
    all_to_all x3 -> x2, starting transfers between devices: 20.4 us -> 15.8 us  [exchange(): lax.all_to_all(x, ('area', 'tie'), split_axis=0, concat_axis=0, tiled=True)]
    pallas_call x3, Pallas kernels: 26.2 us -> 22 us  [the longest x1 8.74 us: on_device(): pl.pallas_call(states_kernel, grid=(areas,), in_specs=[whole(areas, bound...]
  transfers between devices with their start and end apart: 3 -> 2, of which waited for: 2 -> 2; matrix products, arithmetic and copies ran while one was open for 0% -> 0% of each run, Pallas kernels for 12% -> 10%
where the time goes in v3:
time: 148 us; the launch traced here: 147 us
  blocking collectives  92.1 us (62%)
  Pallas kernels  22 us (15%)
  starting transfers between devices  15.8 us (11%)
  waiting for transfers between devices  10.2 us (7%)
  matrix products  5.51 us (4%)
    all_to_all x6, blocking collectives, exchange(): lax.all_to_all(x, ('area', 'tie'), split_axis=0, concat_axis=0, tiled=True)  92.1 us
    all_to_all x2, starting transfers between devices, exchange(): lax.all_to_all(x, ('area', 'tie'), split_axis=0, concat_axis=0, tiled=True)  15.8 us
    all_to_all x2, waiting for transfers between devices, exchange(): lax.all_to_all(x, ('area', 'tie'), split_axis=0, concat_axis=0, tiled=True)  10.2 us
    pallas_call x1, Pallas kernels, on_device(): pl.pallas_call(states_kernel, grid=(areas,), in_specs=[whole(areas, bound...  8.74 us
    pallas_call x1, Pallas kernels, on_device(): pl.pallas_call(start_kernel, in_specs=[small, small, anywhere, anywhere],...  7.66 us
    pallas_call x1, Pallas kernels, on_device(): pl.pallas_call(prepare_kernel, grid=(areas,), in_specs=[whole(areas, boun...  5.64 us
    dot_general x9, matrix products, exact(): jnp.einsum(spec, a, b, precision=lax.Precision.HIGHEST, preferred_element...  4.61 us
  transfers between devices with their start and end apart: 2, of which 2 were waited for; matrix products, arithmetic and copies ran while one was open for 0% of the time, Pallas kernels for 10%

profile of v3, /device:TPU:1, one launch (start us, length us, event | category | flops | bytes accessed | tf_op | source)
XLA Modules:
  0.0 147.4 jit_solution(4821103006957174046)
XLA Ops:
  0.6 7.7 %start.1 = (f32[512,128]{1,0:T(8,128)S(1)}, f32[1024,128]{1,0:T(8,128)}, bf16[4,128,1024]{2,1,0:T(8,128)(2,1)S(1)}) custom-call(s32[4,128]{1,0:T(4,128)} %row_ref.5, s32[4,128]{1,0:T(4,128)} %var_ref.3, bf16[4,1024,1024]{2,1,0:T(8,128)(2,1)} %ginv_ref.3, f32[4096,128]{1,0:T(8,128)} %rhs_ref.5), custom_call_target="tpu_custom_call" | custom-call | tf_op jit(solution)/shard_map/start/pallas_call | solution.py:194
  8.3 0.0 copy-start.3
  8.3 0.7 copy-done.3
  9.0 11.5 %all-to-all-start = ((f32[128,8,128]{2,1,0:T(8,128)}), f32[128,8,128]{2,1,0:T(8,128)S(1)}, u32[]{:S(2)}, u32[]{:S(2)}) async-start(f32[128,8,128]{2,1,0:T(8,128)} %bitcast), calls=%async_computation | async-start | bytes 1048576 | tf_op jit(solution)/shard_map/all_to_all | solution.py:240
  20.5 5.6 %prepare.1 = (bf16[512,512]{1,0:T(8,128)(2,1)S(1)}, bf16[512,512]{1,0:T(8,128)(2,1)S(1)}, f32[512,128]{1,0:T(8,128)S(1)}, f32[512,128]{1,0:T(8,128)S(1)}) custom-call(s32[4,128]{1,0:T(4,128)} %row_ref.5, s32[4,128]{1,0:T(4,128)} %var_ref.3, bf16[4,128,1024]{2,1,0:T(8,128)(2,1)} %copy-done.2, f32[4096,128]{1,0:T(8,128)} %rhs_ref.5, f32[512,128]{1,0:T(8,128)} %copy-done.3), custom_call_target="tpu_custom_call" | custom-call | tf_op jit(solution)/shard_map/prepare/pallas_call | solution.py:211
  26.2 0.0 copy-start.4
  26.2 7.9 %all-to-all-done = f32[128,8,128]{2,1,0:T(8,128)S(1)} async-done(((f32[128,8,128]{2,1,0:T(8,128)}), f32[128,8,128]{2,1,0:T(8,128)S(1)}, u32[]{:S(2)}, u32[]{:S(2)}) %all-to-all-start) | async-done | bytes 524320 | tf_op jit(solution)/shard_map/all_to_all | solution.py:240
  34.1 0.1 fusion.7
  34.2 0.1 convert_reduce_fusion
  34.3 0.4 convolution_multiply_fusion.3
  34.7 0.3 fusion.8
  34.9 15.6 %all_to_all.40 = f32[128,4,128]{2,1,0:T(4,128)S(1)} all-to-all(f32[128,4,128]{2,1,0:T(4,128)S(1)} %bitcast.46), channel_id=1, replica_groups=mesh['area'=16,'tie'=8] {'area','tie'}, dimensions={0} | all-to-all | bytes 524288 | tf_op jit(solution)/shard_map/all_to_all | solution.py:240
  50.5 0.3 fusion
  50.8 15.3 %all_to_all.41 = f32[128,4,128]{2,1,0:T(4,128)S(1)} all-to-all(f32[128,4,128]{2,1,0:T(4,128)S(1)} %bitcast.39), channel_id=1, replica_groups=mesh['area'=16,'tie'=8] {'area','tie'}, dimensions={0} | all-to-all | bytes 524288 | tf_op jit(solution)/shard_map/all_to_all | solution.py:240
  66.1 0.4 convolution_multiply_fusion.2
  66.5 0.3 fusion.9
  66.8 15.3 %all_to_all.42 = f32[128,4,128]{2,1,0:T(4,128)S(1)} all-to-all(f32[128,4,128]{2,1,0:T(4,128)S(1)} %bitcast.47), channel_id=1, replica_groups=mesh['area'=16,'tie'=8] {'area','tie'}, dimensions={0} | all-to-all | bytes 524288 | tf_op jit(solution)/shard_map/all_to_all | solution.py:240
  82.1 0.3 fusion.1
  82.4 15.3 %all_to_all.43 = f32[128,4,128]{2,1,0:T(4,128)S(1)} all-to-all(f32[128,4,128]{2,1,0:T(4,128)S(1)} %bitcast.38), channel_id=1, replica_groups=mesh['area'=16,'tie'=8] {'area','tie'}, dimensions={0} | all-to-all | bytes 524288 | tf_op jit(solution)/shard_map/all_to_all | solution.py:240
  97.7 0.4 convolution_multiply_fusion.1
  98.1 0.3 fusion.10
  98.3 15.3 %all_to_all.44 = f32[128,4,128]{2,1,0:T(4,128)S(1)} all-to-all(f32[128,4,128]{2,1,0:T(4,128)S(1)} %bitcast.48), channel_id=1, replica_groups=mesh['area'=16,'tie'=8] {'area','tie'}, dimensions={0} | all-to-all | bytes 524288 | tf_op jit(solution)/shard_map/all_to_all | solution.py:240
  113.7 0.0 copy-start.5
  113.7 0.3 fusion.2
  114.0 15.3 %all_to_all.45 = f32[128,4,128]{2,1,0:T(4,128)S(1)} all-to-all(f32[128,4,128]{2,1,0:T(4,128)S(1)} %bitcast.40), channel_id=1, replica_groups=mesh['area'=16,'tie'=8] {'area','tie'}, dimensions={0} | all-to-all | bytes 524288 | tf_op jit(solution)/shard_map/all_to_all | solution.py:240
  129.3 0.4 convolution_multiply_fusion
  129.7 0.0 copy-start.6
  129.7 1.0 fusion.11
  130.6 4.3 %all-to-all-start.7 = ((f32[128,4,128]{2,1,0:T(4,128)}), f32[128,4,128]{2,1,0:T(4,128)S(1)}, u32[]{:S(2)}, u32[]{:S(2)}) async-start(f32[128,4,128]{2,1,0:T(4,128)} %bitcast.15), calls=%async_computation.7 | async-start | bytes 524288 | tf_op jit(solution)/shard_map/all_to_all | solution.py:240
  135.0 8.7 %states.1 = f32[4096,128]{1,0:T(8,128)} custom-call(s32[4,128]{1,0:T(4,128)} %row_ref.5, bf16[4,1024,1024]{2,1,0:T(8,128)(2,1)} %ginv_ref.3, f32[4096,128]{1,0:T(8,128)} %rhs_ref.5, bf16[512,512]{1,0:T(8,128)(2,1)} %copy-done, bf16[512,128]{1,0:T(8,128)(2,1)} %copy-done.5), custom_call_target="tpu_custom_call" | custom-call | tf_op jit(solution)/shard_map/states/pallas_call | solution.py:257
  143.7 2.3 %all-to-all-done.7 = f32[128,4,128]{2,1,0:T(4,128)S(1)} async-done(((f32[128,4,128]{2,1,0:T(4,128)}), f32[128,4,128]{2,1,0:T(4,128)S(1)}, u32[]{:S(2)}, u32[]{:S(2)}) %all-to-all-start.7) | async-done | bytes 262176 | tf_op jit(solution)/shard_map/all_to_all | solution.py:240
  146.0 1.4 fusion.3
  (12 shorter events, 0.1 us)
Async XLA Ops:
  8.3 0.7 copy-start.3
  9.0 11.5 %copy-start.2 = (bf16[4,128,1024]{2,1,0:T(8,128)(2,1)}, bf16[4,128,1024]{2,1,0:T(8,128)(2,1)S(1)}, u32[]{:S(2)}) copy-start(bf16[4,128,1024]{2,1,0:T(8,128)(2,1)S(1)} %get-tuple-element.16.chosen_ref) | copy-start | bytes 3145732
  9.0 25.1 %all-to-all-start = ((f32[128,8,128]{2,1,0:T(8,128)}), f32[128,8,128]{2,1,0:T(8,128)S(1)}, u32[]{:S(2)}, u32[]{:S(2)}) async-start(f32[128,8,128]{2,1,0:T(8,128)} %bitcast), calls=%async_computation | async-start | bytes 1048576 | tf_op jit(solution)/shard_map/all_to_all | solution.py:240
  26.2 24.7 %copy-start = (bf16[512,512]{1,0:T(8,128)(2,1)}, bf16[512,512]{1,0:T(8,128)(2,1)S(1)}, u32[]{:S(2)}) copy-start(bf16[512,512]{1,0:T(8,128)(2,1)S(1)} %get-tuple-element.22.place_ref) | copy-start | bytes 1572868
  26.2 24.3 %copy-start.4 = (f32[512,128]{1,0:T(8,128)S(1)}, f32[512,128]{1,0:T(8,128)}, u32[]{:S(2)}) copy-start(f32[512,128]{1,0:T(8,128)} %copy-done.3) | copy-start | bytes 786436
  113.7 21.3 %copy-start.5 = (bf16[512,128]{1,0:T(8,128)(2,1)}, bf16[512,128]{1,0:T(8,128)(2,1)S(1)}, u32[]{:S(2)}) copy-start(bf16[512,128]{1,0:T(8,128)(2,1)S(1)} %add_convert_fusion.blend_ref) | copy-start | bytes 393220
  129.7 14.1 %copy-start.6 = (f32[64,128]{1,0:T(8,128)}, f32[64,128]{1,0:T(8,128)S(1)}, u32[]{:S(2)}) copy-start(f32[64,128]{1,0:T(8,128)S(1)} %convolution_multiply_fusion) | copy-start | bytes 98308
  130.6 15.4 %all-to-all-start.7 = ((f32[128,4,128]{2,1,0:T(4,128)}), f32[128,4,128]{2,1,0:T(4,128)S(1)}, u32[]{:S(2)}, u32[]{:S(2)}) async-start(f32[128,4,128]{2,1,0:T(4,128)} %bitcast.15), calls=%async_computation.7 | async-start | bytes 524288 | tf_op jit(solution)/shard_map/all_to_all | solution.py:240
  135.0 11.1 %copy-start.1 = (bf16[512,512]{1,0:T(8,128)(2,1)S(1)}, bf16[512,512]{1,0:T(8,128)(2,1)}, u32[]{:S(2)}) copy-start(bf16[512,512]{1,0:T(8,128)(2,1)} %copy-done) | copy-start | bytes 1572868

commit v4 on v3

--- a/solution.py
+++ b/solution.py
@@ -9,7 +9,8 @@
 VAR_DEV = 64
 ITERS = 4
 PENALTY = 1.0
-HALVES = 2
+PIECE = 128
+BUILD = 256
 WIDE = 8
 
 F32 = jnp.float32
@@ -73,64 +74,55 @@
 
 def start_kernel(
     row_ref, var_ref, ginv_ref, rhs_ref, local_ref, out_ref, chosen_ref,
-    block_ref, right_ref, carry_ref, block_sems, right_sems,
+    block_ref, right_ref, carry_ref, place_ref, solved_ref, block_sems, right_sems,
 ):
-    areas = row_ref.shape[0]
+    areas, bound = row_ref.shape
     state = ginv_ref.shape[1]
-    slots = local_ref.shape[0]
+    slots, snaps = local_ref.shape
     owners = slots // SLOT
-    half = state // HALVES
-
-    def block_copy(area, at):
-        rows = pl.ds(at * half, half)
-        return pltpu.make_async_copy(
-            ginv_ref.at[area, rows], block_ref.at[area, rows], block_sems.at[area * HALVES + at]
-        )
+
+    def block_copy(area):
+        return pltpu.make_async_copy(ginv_ref.at[area], block_ref.at[area], block_sems.at[area])
 
     def right_copy(area):
         rows = pl.ds(area * state, state)
         return pltpu.make_async_copy(rhs_ref.at[rows], right_ref.at[rows], right_sems.at[area])
 
     for area in range(areas):
-        for at in range(HALVES):
-            block_copy(area, at).start()
+        block_copy(area).start()
         right_copy(area).start()
     carry_ref[...] = jnp.zeros_like(carry_ref)
-    ids = jnp.zeros(local_ref.shape, F32)
-    places = []
     picks = []
+    local_ids = []
     for area in range(areas):
         row = row_ref[area : area + 1, :]
         var = var_ref[area : area + 1, :]
-        places.append(placing(entry_slots(row, var, carry_ref, owners), slots))
+        place_ref[:, area * bound : (area + 1) * bound] = placing(
+            entry_slots(row, var, carry_ref, owners), slots
+        )
         picks.append(picking(row, state))
-        local_id = jnp.where(row >= 0, (var & (VAR_DEV - 1)) + 1, 0).astype(F32)
-        ids += dot_nt(places[area], jnp.broadcast_to(local_id, (128, row.shape[1])).astype(BF16))
-    local_ref[...] = ids
+        local_ids.append(jnp.where(row >= 0, (var & (VAR_DEV - 1)) + 1, 0).astype(F32))
+    local_ids = jnp.broadcast_to(jnp.concatenate(local_ids, axis=1), (128, areas * bound))
+    local_ref[...] = dot_nt(place_ref[...], local_ids.astype(BF16))
     for k in range(SLOT):
         at = pl.ds(k, owners, stride=SLOT)
         out_ref[pl.ds(SLOT + k, owners, stride=WIDE), :] = local_ref[at, :]
-    local = jnp.zeros(local_ref.shape, F32)
-    for area in range(areas):
-        chosen = jnp.zeros((row_ref.shape[1], state), F32)
-        for at in range(HALVES):
-            block_copy(area, at).wait()
-            rows = slice(at * half, (at + 1) * half)
-            chosen += dot(picks[area][:, rows], block_ref[area, rows, :])
-        chosen = chosen.astype(BF16)
+    for area in range(areas):
+        block_copy(area).wait()
+        right_copy(area).wait()
+        chosen = dot(picks[area], block_ref[area]).astype(BF16)
         chosen_ref[area] = chosen
-        right_copy(area).wait()
         solved = dot(chosen, right_ref[area * state : (area + 1) * state, :].astype(BF16))
-        local += join3(dot(places[area], jnp.concatenate(split3(solved), axis=1)))
-    local_ref[...] = local
+        solved_ref[area * bound : (area + 1) * bound, :] = jnp.concatenate(split3(solved), axis=1)
+    local_ref[...] = join3(dot(place_ref[...], solved_ref[...]), 0, snaps)
     for k in range(SLOT):
         at = pl.ds(k, owners, stride=SLOT)
         out_ref[pl.ds(k, owners, stride=WIDE), :] = local_ref[at, :]
 
 
 def prepare_kernel(
-    row_ref, var_ref, chosen_ref, rhs_ref, local_ref,
-    place_ref, mat_ref, base_ref, term_ref,
+    row_ref, var_ref, chosen_ref, rhs_ref,
+    place_ref, mat_ref, term_ref,
     carry_ref, acc_ref,
 ):
     area = pl.program_id(0)
@@ -155,18 +147,54 @@
 
     @pl.when(area == pl.num_programs(0) - 1)
     def _():
-        mat = acc_ref[...].astype(BF16)
-        mat_ref[...] = mat
-        base_ref[...] = local_ref[...] - dot(mat, term_ref[...].astype(BF16))
-
-
-def states_kernel(row_ref, ginv_ref, rhs_ref, place_ref, blend_ref, states_ref):
-    row = row_ref[pl.ds(pl.program_id(0), 1), :]
-    state, snaps = rhs_ref.shape
-    rows = dot_t(place_ref[...], blend_ref[...]).astype(BF16)
-    placed = dot(placing(row, state), jnp.concatenate([rows, jnp.ones_like(rows)], axis=1))
-    blended = jnp.where(placed[:, snaps:] > 0.0, placed[:, :snaps], rhs_ref[...])
-    states_ref[...] = dot(ginv_ref[0], blended.astype(BF16))
+        mat_ref[...] = acc_ref[...].astype(BF16)
+
+
+def states_kernel(
+    row_ref, ginv_ref, rhs_ref, place_ref, blend_ref, states_ref,
+    block_ref, right_ref, solved_ref, block_sems, right_sems, out_sems,
+):
+    areas, bound = row_ref.shape
+    state = ginv_ref.shape[1]
+    snaps = rhs_ref.shape[1]
+
+    def rows_of(area):
+        return pl.ds(area * state, state)
+
+    def right_copy(area):
+        rows = rows_of(area)
+        return pltpu.make_async_copy(rhs_ref.at[rows], right_ref.at[rows], right_sems.at[area])
+
+    def block_copy(area):
+        return pltpu.make_async_copy(ginv_ref.at[area], block_ref.at[area], block_sems.at[area])
+
+    def out_copy(area):
+        rows = rows_of(area)
+        return pltpu.make_async_copy(solved_ref.at[rows], states_ref.at[rows], out_sems.at[area])
+
+    for area in range(areas):
+        right_copy(area).start()
+        block_copy(area).start()
+    entry_rows = dot_t(place_ref[...], blend_ref[...]).astype(BF16)
+    for area in range(areas):
+        row = row_ref[area : area + 1, :]
+        rows = entry_rows[area * bound : (area + 1) * bound]
+        both = jnp.concatenate([rows, jnp.ones_like(rows)], axis=1)
+        right_copy(area).wait()
+        pieces = []
+        for at in range(0, state, BUILD):
+            placed = dot(placing(row - at, BUILD), both)
+            right = right_ref[area * state + at : area * state + at + BUILD, :]
+            piece = jnp.where(placed[:, snaps:] > 0.0, placed[:, :snaps], right)
+            pieces.append(piece.astype(BF16))
+        blended = jnp.concatenate(pieces, axis=0)
+        block_copy(area).wait()
+        for at in range(0, state, PIECE):
+            solved = dot(block_ref[area, at : at + PIECE, :], blended)
+            solved_ref[area * state + at : area * state + at + PIECE, :] = solved
+        out_copy(area).start()
+    for area in range(areas):
+        out_copy(area).wait()
 
 
 def exact(spec, a, b):
@@ -203,12 +231,14 @@
             pltpu.VMEM((areas, state, state), BF16),
             pltpu.VMEM((areas * state, snaps), F32),
             pltpu.VMEM((devices, bound), F32),
-            pltpu.SemaphoreType.DMA((areas * HALVES,)),
+            pltpu.VMEM((slots, entries), BF16),
+            pltpu.VMEM((entries, 3 * snaps), BF16),
+            pltpu.SemaphoreType.DMA((areas,)),
             pltpu.SemaphoreType.DMA((areas,)),
         ],
         name="start",
     )(bnd_row, bnd_var, ginv, rhs)
-    place, mat, base, term = pl.pallas_call(
+    place, mat, term = pl.pallas_call(
         prepare_kernel,
         grid=(areas,),
         in_specs=[
@@ -216,29 +246,27 @@
             whole(areas, bound),
             pl.BlockSpec((1, bound, state), lambda a: (a, 0, 0)),
             pl.BlockSpec((state, snaps), lambda a: (a, 0)),
-            whole(slots, snaps),
         ],
         out_specs=[
             pl.BlockSpec((slots, bound), lambda a: (0, a)),
             whole(slots, slots),
             whole(slots, snaps),
-            whole(slots, snaps),
         ],
         out_shape=[
             pltpu.VMEM((slots, entries), BF16),
             pltpu.VMEM((slots, slots), BF16),
             pltpu.VMEM((slots, snaps), F32),
-            pltpu.VMEM((slots, snaps), F32),
         ],
         scratch_shapes=[pltpu.VMEM((devices, bound), F32), pltpu.VMEM((slots, slots), F32)],
         compiler_params=in_order,
         name="prepare",
-    )(bnd_row, bnd_var, chosen, rhs, local)
+    )(bnd_row, bnd_var, chosen, rhs)
 
     def exchange(x):
         x = x.reshape(devices, -1, snaps)
         return lax.all_to_all(x, ("area", "tie"), split_axis=0, concat_axis=0, tiled=True)
 
+    base = local - dot(mat, term.astype(BF16))
     received, place, mat, base, term = lax.optimization_barrier(
         (exchange(outgoing), place, mat, base, term)
     )
@@ -256,17 +284,23 @@
         dual = local - agreed
     states = pl.pallas_call(
         states_kernel,
-        grid=(areas,),
         in_specs=[
-            whole(areas, bound),
-            pl.BlockSpec((1, state, state), lambda a: (a, 0, 0)),
-            pl.BlockSpec((state, snaps), lambda a: (a, 0)),
-            pl.BlockSpec((slots, bound), lambda a: (0, a)),
-            whole(slots, snaps),
-        ],
-        out_specs=pl.BlockSpec((state, snaps), lambda a: (a, 0)),
+            small,
+            anywhere,
+            anywhere,
+            pl.BlockSpec((slots, entries), lambda: (0, 0)),
+            pl.BlockSpec((slots, snaps), lambda: (0, 0)),
+        ],
+        out_specs=anywhere,
         out_shape=shape((areas * state, snaps)),
-        compiler_params=in_order,
+        scratch_shapes=[
+            pltpu.VMEM((areas, state, state), BF16),
+            pltpu.VMEM((areas * state, snaps), F32),
+            pltpu.VMEM((areas * state, snaps), F32),
+            pltpu.SemaphoreType.DMA((areas,)),
+            pltpu.SemaphoreType.DMA((areas,)),
+            pltpu.SemaphoreType.DMA((areas,)),
+        ],
         name="states",
     )(bnd_row, ginv, rhs, place, blend)
     dual = exact("se,sn->en", place.astype(F32), dual)

time: 148 us -> 146 us (0.986)
  Pallas kernels: 22 us -> 19.1 us
  transfers between devices with their start and end apart: 2 -> 2, of which waited for: 2 -> 2; matrix products, arithmetic and copies ran while one was open for 0% -> 0% of each run, Pallas kernels for 10% -> 9%
where the time goes in v4:
time: 146 us
  blocking collectives  92.1 us (63%)
  Pallas kernels  19.1 us (13%)
  starting transfers between devices  15.8 us (11%)
  waiting for transfers between devices  11.6 us (8%)
  matrix products  5.81 us (4%)
    all_to_all x6, blocking collectives, exchange(): lax.all_to_all(x, ('area', 'tie'), split_axis=0, concat_axis=0, tiled=True)  92.1 us
    all_to_all x2, starting transfers between devices, exchange(): lax.all_to_all(x, ('area', 'tie'), split_axis=0, concat_axis=0, tiled=True)  15.8 us
    all_to_all x2, waiting for transfers between devices, exchange(): lax.all_to_all(x, ('area', 'tie'), split_axis=0, concat_axis=0, tiled=True)  11.6 us
    pallas_call x1, Pallas kernels, on_device(): pl.pallas_call(states_kernel, in_specs=[small, anywhere, anywhere, pl.Blo...  7.45 us
    pallas_call x1, Pallas kernels, on_device(): pl.pallas_call(start_kernel, in_specs=[small, small, anywhere, anywhere],...  6.43 us
    pallas_call x1, Pallas kernels, on_device(): pl.pallas_call(prepare_kernel, grid=(areas,), in_specs=[whole(areas, boun...  5.25 us
    dot_general x9, matrix products, exact(): jnp.einsum(spec, a, b, precision=lax.Precision.HIGHEST, preferred_element...  4.61 us
  transfers between devices with their start and end apart: 2, of which 2 were waited for; matrix products, arithmetic and copies ran while one was open for 0% of the time, Pallas kernels for 9%

profile of v4, /device:TPU:1, one launch (start us, length us, event | category | flops | bytes accessed | tf_op | source)
XLA Modules:
  0.0 145.5 jit_solution(11713735633651226695)
XLA Ops:
  0.6 6.4 %start.1 = (f32[512,128]{1,0:T(8,128)S(1)}, f32[1024,128]{1,0:T(8,128)}, bf16[4,128,1024]{2,1,0:T(8,128)(2,1)S(1)}) custom-call(s32[4,128]{1,0:T(4,128)} %row_ref.5, s32[4,128]{1,0:T(4,128)} %var_ref.3, bf16[4,1024,1024]{2,1,0:T(8,128)(2,1)} %ginv_ref.3, f32[4096,128]{1,0:T(8,128)} %rhs_ref.5), custom_call_target="tpu_custom_call" | custom-call | tf_op jit(solution)/shard_map/start/pallas_call | solution.py:222
  7.1 0.0 copy-start.2
  7.1 11.5 %all-to-all-start = ((f32[128,8,128]{2,1,0:T(8,128)}), f32[128,8,128]{2,1,0:T(8,128)S(1)}, u32[]{:S(2)}, u32[]{:S(2)}) async-start(f32[128,8,128]{2,1,0:T(8,128)} %bitcast), calls=%async_computation | async-start | bytes 1048576 | tf_op jit(solution)/shard_map/all_to_all | solution.py:267
  18.6 5.2 %prepare.1 = (bf16[512,512]{1,0:T(8,128)(2,1)S(1)}, bf16[512,512]{1,0:T(8,128)(2,1)S(1)}, f32[512,128]{1,0:T(8,128)S(1)}) custom-call(s32[4,128]{1,0:T(4,128)} %row_ref.5, s32[4,128]{1,0:T(4,128)} %var_ref.3, bf16[4,128,1024]{2,1,0:T(8,128)(2,1)} %copy-done.2, f32[4096,128]{1,0:T(8,128)} %rhs_ref.5), custom_call_target="tpu_custom_call" | custom-call | tf_op jit(solution)/shard_map/prepare/pallas_call | solution.py:241
  23.8 0.0 copy-start
  23.9 0.3 convolution_subtract_fusion
  24.2 8.0 %all-to-all-done = f32[128,8,128]{2,1,0:T(8,128)S(1)} async-done(((f32[128,8,128]{2,1,0:T(8,128)}), f32[128,8,128]{2,1,0:T(8,128)S(1)}, u32[]{:S(2)}, u32[]{:S(2)}) %all-to-all-start) | async-done | bytes 524320 | tf_op jit(solution)/shard_map/all_to_all | solution.py:267
  32.2 0.1 fusion.8
  32.3 0.1 convert_reduce_fusion
  32.4 0.4 convolution_multiply_fusion.3
  32.7 0.3 fusion.9
  33.0 15.6 %all_to_all.40 = f32[128,4,128]{2,1,0:T(4,128)S(1)} all-to-all(f32[128,4,128]{2,1,0:T(4,128)S(1)} %bitcast.47), channel_id=1, replica_groups=mesh['area'=16,'tie'=8] {'area','tie'}, dimensions={0} | all-to-all | bytes 524288 | tf_op jit(solution)/shard_map/all_to_all | solution.py:267
  48.6 0.3 fusion
  48.9 15.3 %all_to_all.41 = f32[128,4,128]{2,1,0:T(4,128)S(1)} all-to-all(f32[128,4,128]{2,1,0:T(4,128)S(1)} %bitcast.40), channel_id=1, replica_groups=mesh['area'=16,'tie'=8] {'area','tie'}, dimensions={0} | all-to-all | bytes 524288 | tf_op jit(solution)/shard_map/all_to_all | solution.py:267
  64.2 0.4 convolution_multiply_fusion.2
  64.6 0.3 fusion.10
  64.8 15.3 %all_to_all.42 = f32[128,4,128]{2,1,0:T(4,128)S(1)} all-to-all(f32[128,4,128]{2,1,0:T(4,128)S(1)} %bitcast.48), channel_id=1, replica_groups=mesh['area'=16,'tie'=8] {'area','tie'}, dimensions={0} | all-to-all | bytes 524288 | tf_op jit(solution)/shard_map/all_to_all | solution.py:267
  80.1 0.3 fusion.1
  80.5 15.3 %all_to_all.43 = f32[128,4,128]{2,1,0:T(4,128)S(1)} all-to-all(f32[128,4,128]{2,1,0:T(4,128)S(1)} %bitcast.39), channel_id=1, replica_groups=mesh['area'=16,'tie'=8] {'area','tie'}, dimensions={0} | all-to-all | bytes 524288 | tf_op jit(solution)/shard_map/all_to_all | solution.py:267
  95.8 0.4 convolution_multiply_fusion.1
  96.1 0.2 fusion.11
  96.4 15.3 %all_to_all.44 = f32[128,4,128]{2,1,0:T(4,128)S(1)} all-to-all(f32[128,4,128]{2,1,0:T(4,128)S(1)} %bitcast.49), channel_id=1, replica_groups=mesh['area'=16,'tie'=8] {'area','tie'}, dimensions={0} | all-to-all | bytes 524288 | tf_op jit(solution)/shard_map/all_to_all | solution.py:267
  111.7 0.3 fusion.2
  112.0 15.3 %all_to_all.45 = f32[128,4,128]{2,1,0:T(4,128)S(1)} all-to-all(f32[128,4,128]{2,1,0:T(4,128)S(1)} %bitcast.41), channel_id=1, replica_groups=mesh['area'=16,'tie'=8] {'area','tie'}, dimensions={0} | all-to-all | bytes 524288 | tf_op jit(solution)/shard_map/all_to_all | solution.py:267
  127.3 0.4 convolution_multiply_fusion
  127.7 0.0 copy-start.4
  127.7 1.0 fusion.12
  128.7 4.3 %all-to-all-start.7 = ((f32[128,4,128]{2,1,0:T(4,128)}), f32[128,4,128]{2,1,0:T(4,128)S(1)}, u32[]{:S(2)}, u32[]{:S(2)}) async-start(f32[128,4,128]{2,1,0:T(4,128)} %bitcast.15), calls=%async_computation.7 | async-start | bytes 524288 | tf_op jit(solution)/shard_map/all_to_all | solution.py:267
  133.0 7.5 %states.1 = f32[4096,128]{1,0:T(8,128)} custom-call(s32[4,128]{1,0:T(4,128)} %row_ref.5, bf16[4,1024,1024]{2,1,0:T(8,128)(2,1)} %ginv_ref.3, f32[4096,128]{1,0:T(8,128)} %rhs_ref.5, bf16[512,512]{1,0:T(8,128)(2,1)} %copy-done, bf16[512,128]{1,0:T(8,128)(2,1)} %copy-done.3), custom_call_target="tpu_custom_call" | custom-call | tf_op jit(solution)/shard_map/states/pallas_call | solution.py:285
  140.5 0.0 copy-done.4
  140.5 3.6 %all-to-all-done.7 = f32[128,4,128]{2,1,0:T(4,128)S(1)} async-done(((f32[128,4,128]{2,1,0:T(4,128)}), f32[128,4,128]{2,1,0:T(4,128)S(1)}, u32[]{:S(2)}, u32[]{:S(2)}) %all-to-all-start.7) | async-done | bytes 262176 | tf_op jit(solution)/shard_map/all_to_all | solution.py:267
  144.1 1.4 fusion.3
  (9 shorter events, 0.1 us)
Async XLA Ops:
  7.1 11.5 %copy-start.2 = (bf16[4,128,1024]{2,1,0:T(8,128)(2,1)}, bf16[4,128,1024]{2,1,0:T(8,128)(2,1)S(1)}, u32[]{:S(2)}) copy-start(bf16[4,128,1024]{2,1,0:T(8,128)(2,1)S(1)} %get-tuple-element.15.chosen_ref) | copy-start | bytes 3145732
  7.1 25.1 %all-to-all-start = ((f32[128,8,128]{2,1,0:T(8,128)}), f32[128,8,128]{2,1,0:T(8,128)S(1)}, u32[]{:S(2)}, u32[]{:S(2)}) async-start(f32[128,8,128]{2,1,0:T(8,128)} %bitcast), calls=%async_computation | async-start | bytes 1048576 | tf_op jit(solution)/shard_map/all_to_all | solution.py:267
  23.8 25.1 %copy-start = (bf16[512,512]{1,0:T(8,128)(2,1)}, bf16[512,512]{1,0:T(8,128)(2,1)S(1)}, u32[]{:S(2)}) copy-start(bf16[512,512]{1,0:T(8,128)(2,1)S(1)} %get-tuple-element.20.place_ref) | copy-start | bytes 1572868
  111.7 21.3 %copy-start.3 = (bf16[512,128]{1,0:T(8,128)(2,1)}, bf16[512,128]{1,0:T(8,128)(2,1)S(1)}, u32[]{:S(2)}) copy-start(bf16[512,128]{1,0:T(8,128)(2,1)S(1)} %add_convert_fusion.blend_ref) | copy-start | bytes 393220
  127.7 12.8 %copy-start.4 = (f32[64,128]{1,0:T(8,128)}, f32[64,128]{1,0:T(8,128)S(1)}, u32[]{:S(2)}) copy-start(f32[64,128]{1,0:T(8,128)S(1)} %convolution_multiply_fusion) | copy-start | bytes 98308
  128.7 15.4 %all-to-all-start.7 = ((f32[128,4,128]{2,1,0:T(4,128)}), f32[128,4,128]{2,1,0:T(4,128)S(1)}, u32[]{:S(2)}, u32[]{:S(2)}) async-start(f32[128,4,128]{2,1,0:T(4,128)} %bitcast.15), calls=%async_computation.7 | async-start | bytes 524288 | tf_op jit(solution)/shard_map/all_to_all | solution.py:267
  133.0 11.1 %copy-start.1 = (bf16[512,512]{1,0:T(8,128)(2,1)S(1)}, bf16[512,512]{1,0:T(8,128)(2,1)}, u32[]{:S(2)}) copy-start(bf16[512,512]{1,0:T(8,128)(2,1)} %copy-done) | copy-start | bytes 1572868

commit v5 on v4

--- a/solution.py
+++ b/solution.py
@@ -122,7 +122,7 @@
 
 def prepare_kernel(
     row_ref, var_ref, chosen_ref, rhs_ref,
-    place_ref, mat_ref, term_ref,
+    place_ref, mat_ref, term_ref, inner_ref,
     carry_ref, acc_ref,
 ):
     area = pl.program_id(0)
@@ -139,6 +139,11 @@
     var = var_ref[pl.ds(area, 1), :]
     place = placing(entry_slots(row, var, carry_ref, slots // SLOT), slots)
     place_ref[...] = place
+    for at in range(0, state, BUILD):
+        bound_rows = dot(placing(row - at, BUILD), jnp.ones((row.shape[1], snaps), BF16)) > 0.0
+        inner_ref[at : at + BUILD, :] = jnp.where(
+            bound_rows, 0.0, rhs_ref[at : at + BUILD, :]
+        ).astype(BF16)
     at_rows = dot(picking(row, state), jnp.concatenate(split3(rhs_ref[...]), axis=1))
     coupling = dot(chosen_ref[0], placing(row, state))
     at_slots = dot(place, jnp.concatenate([at_rows, coupling], axis=1).astype(BF16))
@@ -151,19 +156,18 @@
 
 
 def states_kernel(
-    row_ref, ginv_ref, rhs_ref, place_ref, blend_ref, states_ref,
+    row_ref, ginv_ref, inner_ref, place_ref, blend_ref, states_ref,
     block_ref, right_ref, solved_ref, block_sems, right_sems, out_sems,
 ):
     areas, bound = row_ref.shape
     state = ginv_ref.shape[1]
-    snaps = rhs_ref.shape[1]
 
     def rows_of(area):
         return pl.ds(area * state, state)
 
     def right_copy(area):
         rows = rows_of(area)
-        return pltpu.make_async_copy(rhs_ref.at[rows], right_ref.at[rows], right_sems.at[area])
+        return pltpu.make_async_copy(inner_ref.at[rows], right_ref.at[rows], right_sems.at[area])
 
     def block_copy(area):
         return pltpu.make_async_copy(ginv_ref.at[area], block_ref.at[area], block_sems.at[area])
@@ -179,14 +183,11 @@
     for area in range(areas):
         row = row_ref[area : area + 1, :]
         rows = entry_rows[area * bound : (area + 1) * bound]
-        both = jnp.concatenate([rows, jnp.ones_like(rows)], axis=1)
         right_copy(area).wait()
         pieces = []
         for at in range(0, state, BUILD):
-            placed = dot(placing(row - at, BUILD), both)
-            right = right_ref[area * state + at : area * state + at + BUILD, :]
-            piece = jnp.where(placed[:, snaps:] > 0.0, placed[:, :snaps], right)
-            pieces.append(piece.astype(BF16))
+            placed = dot(placing(row - at, BUILD), rows).astype(BF16)
+            pieces.append(right_ref[area * state + at : area * state + at + BUILD, :] + placed)
         blended = jnp.concatenate(pieces, axis=0)
         block_copy(area).wait()
         for at in range(0, state, PIECE):
@@ -197,8 +198,8 @@
         out_copy(area).wait()
 
 
-def exact(spec, a, b):
-    return jnp.einsum(spec, a, b, precision=lax.Precision.HIGHEST, preferred_element_type=F32)
+def select(spec, a, b):
+    return jnp.einsum(spec, a, b, precision=lax.Precision.HIGH, preferred_element_type=F32)
 
 
 def shape(dims, dtype=F32):
@@ -238,7 +239,7 @@
         ],
         name="start",
     )(bnd_row, bnd_var, ginv, rhs)
-    place, mat, term = pl.pallas_call(
+    place, mat, term, inner = pl.pallas_call(
         prepare_kernel,
         grid=(areas,),
         in_specs=[
@@ -251,11 +252,13 @@
             pl.BlockSpec((slots, bound), lambda a: (0, a)),
             whole(slots, slots),
             whole(slots, snaps),
+            pl.BlockSpec((state, snaps), lambda a: (a, 0)),
         ],
         out_shape=[
             pltpu.VMEM((slots, entries), BF16),
             pltpu.VMEM((slots, slots), BF16),
             pltpu.VMEM((slots, snaps), F32),
+            shape((areas * state, snaps), BF16),
         ],
         scratch_shapes=[pltpu.VMEM((devices, bound), F32), pltpu.VMEM((slots, slots), F32)],
         compiler_params=in_order,
@@ -267,8 +270,8 @@
         return lax.all_to_all(x, ("area", "tie"), split_axis=0, concat_axis=0, tiled=True)
 
     base = local - dot(mat, term.astype(BF16))
-    received, place, mat, base, term = lax.optimization_barrier(
-        (exchange(outgoing), place, mat, base, term)
+    received, place, mat, base, term, inner = lax.optimization_barrier(
+        (exchange(outgoing), place, mat, base, term, inner)
     )
     incoming = received[:, :SLOT].reshape(slots, snaps)
     ids = received[:, SLOT:].reshape(slots, snaps)[:, :VAR_DEV]
@@ -279,8 +282,8 @@
             blend = (term + PENALTY * (agreed - dual)).astype(BF16)
             local = (base + dot(mat, blend)) + dual
             incoming = exchange(local).reshape(slots, snaps)
-        consensus = exact("sv,sn->vn", member, incoming) * inverse
-        agreed = exchange(exact("sv,vn->sn", member, consensus)).reshape(slots, snaps)
+        consensus = select("sv,sn->vn", member, incoming) * inverse
+        agreed = exchange(select("sv,vn->sn", member, consensus)).reshape(slots, snaps)
         dual = local - agreed
     states = pl.pallas_call(
         states_kernel,
@@ -295,15 +298,15 @@
         out_shape=shape((areas * state, snaps)),
         scratch_shapes=[
             pltpu.VMEM((areas, state, state), BF16),
+            pltpu.VMEM((areas * state, snaps), BF16),
             pltpu.VMEM((areas * state, snaps), F32),
-            pltpu.VMEM((areas * state, snaps), F32),
             pltpu.SemaphoreType.DMA((areas,)),
             pltpu.SemaphoreType.DMA((areas,)),
             pltpu.SemaphoreType.DMA((areas,)),
         ],
         name="states",
-    )(bnd_row, ginv, rhs, place, blend)
-    dual = exact("se,sn->en", place.astype(F32), dual)
+    )(bnd_row, ginv, inner, place, blend)
+    dual = select("se,sn->en", place.astype(F32), dual)
     return states, consensus, dual
 
 

time: 146 us -> 145 us (level)
  no operation moved by 1% of the time
where the time goes in v5:
time: 145 us
  blocking collectives  92.1 us (64%)
  Pallas kernels  19.9 us (14%)
  starting transfers between devices  15.8 us (11%)
  waiting for transfers between devices  10.8 us (7%)
  matrix products  5.23 us (4%)
    all_to_all x6, blocking collectives, exchange(): lax.all_to_all(x, ('area', 'tie'), split_axis=0, concat_axis=0, tiled=True)  92.1 us
    all_to_all x2, starting transfers between devices, exchange(): lax.all_to_all(x, ('area', 'tie'), split_axis=0, concat_axis=0, tiled=True)  15.8 us
    all_to_all x2, waiting for transfers between devices, exchange(): lax.all_to_all(x, ('area', 'tie'), split_axis=0, concat_axis=0, tiled=True)  10.8 us
    pallas_call x1, Pallas kernels, on_device(): pl.pallas_call(states_kernel, in_specs=[small, anywhere, anywhere, pl.Blo...  7.23 us
    pallas_call x1, Pallas kernels, on_device(): pl.pallas_call(start_kernel, in_specs=[small, small, anywhere, anywhere],...  6.45 us
    pallas_call x1, Pallas kernels, on_device(): pl.pallas_call(prepare_kernel, grid=(areas,), in_specs=[whole(areas, boun...  6.26 us
    dot_general x9, matrix products, select(): jnp.einsum(spec, a, b, precision=lax.Precision.HIGH, preferred_element_ty...  4.03 us
  transfers between devices with their start and end apart: 2, of which 2 were waited for; matrix products, arithmetic and copies ran while one was open for 0% of the time, Pallas kernels for 9%

profile of v5, /device:TPU:1, one launch (start us, length us, event | category | flops | bytes accessed | tf_op | source)
XLA Modules:
  0.0 144.9 jit_solution(18243124612584647671)
XLA Ops:
  0.6 6.4 %start.1 = (f32[512,128]{1,0:T(8,128)S(1)}, f32[1024,128]{1,0:T(8,128)}, bf16[4,128,1024]{2,1,0:T(8,128)(2,1)S(1)}) custom-call(s32[4,128]{1,0:T(4,128)} %row_ref.5, s32[4,128]{1,0:T(4,128)} %var_ref.3, bf16[4,1024,1024]{2,1,0:T(8,128)(2,1)} %ginv_ref.3, f32[4096,128]{1,0:T(8,128)} %rhs_ref.3), custom_call_target="tpu_custom_call" | custom-call | tf_op jit(solution)/shard_map/start/pallas_call | solution.py:223
  7.1 0.0 copy-start.2
  7.1 11.5 %all-to-all-start = ((f32[128,8,128]{2,1,0:T(8,128)}), f32[128,8,128]{2,1,0:T(8,128)S(1)}, u32[]{:S(2)}, u32[]{:S(2)}) async-start(f32[128,8,128]{2,1,0:T(8,128)} %bitcast), calls=%async_computation | async-start | bytes 1048576 | tf_op jit(solution)/shard_map/all_to_all | solution.py:270
  18.6 0.0 copy-done.2
  18.6 6.3 %prepare.1 = (bf16[512,512]{1,0:T(8,128)(2,1)S(1)}, bf16[512,512]{1,0:T(8,128)(2,1)S(1)}, f32[512,128]{1,0:T(8,128)S(1)}, bf16[4096,128]{1,0:T(8,128)(2,1)}) custom-call(s32[4,128]{1,0:T(4,128)} %row_ref.5, s32[4,128]{1,0:T(4,128)} %var_ref.3, bf16[4,128,1024]{2,1,0:T(8,128)(2,1)} %copy-done.2, f32[4096,128]{1,0:T(8,128)} %rhs_ref.3), custom_call_target="tpu_custom_call" | custom-call | tf_op jit(solution)/shard_map/prepare/pallas_call | solution.py:242
  24.9 0.3 convolution_subtract_fusion
  25.2 7.0 %all-to-all-done = f32[128,8,128]{2,1,0:T(8,128)S(1)} async-done(((f32[128,8,128]{2,1,0:T(8,128)}), f32[128,8,128]{2,1,0:T(8,128)S(1)}, u32[]{:S(2)}, u32[]{:S(2)}) %all-to-all-start) | async-done | bytes 524320 | tf_op jit(solution)/shard_map/all_to_all | solution.py:270
  32.2 0.1 fusion.8
  32.3 0.1 convert_reduce_fusion
  32.4 0.3 convolution_multiply_fusion.3
  32.7 0.2 fusion.9
  32.9 15.6 %all_to_all.40 = f32[128,4,128]{2,1,0:T(4,128)S(1)} all-to-all(f32[128,4,128]{2,1,0:T(4,128)S(1)} %bitcast.47), channel_id=1, replica_groups=mesh['area'=16,'tie'=8] {'area','tie'}, dimensions={0} | all-to-all | bytes 524288 | tf_op jit(solution)/shard_map/all_to_all | solution.py:270
  48.5 0.3 fusion
  48.8 0.0 copy-done
  48.8 15.3 %all_to_all.41 = f32[128,4,128]{2,1,0:T(4,128)S(1)} all-to-all(f32[128,4,128]{2,1,0:T(4,128)S(1)} %bitcast.40), channel_id=1, replica_groups=mesh['area'=16,'tie'=8] {'area','tie'}, dimensions={0} | all-to-all | bytes 524288 | tf_op jit(solution)/shard_map/all_to_all | solution.py:270
  64.1 0.3 convolution_multiply_fusion.2
  64.4 0.2 fusion.10
  64.7 15.3 %all_to_all.42 = f32[128,4,128]{2,1,0:T(4,128)S(1)} all-to-all(f32[128,4,128]{2,1,0:T(4,128)S(1)} %bitcast.48), channel_id=1, replica_groups=mesh['area'=16,'tie'=8] {'area','tie'}, dimensions={0} | all-to-all | bytes 524288 | tf_op jit(solution)/shard_map/all_to_all | solution.py:270
  80.0 0.3 fusion.1
  80.3 15.3 %all_to_all.43 = f32[128,4,128]{2,1,0:T(4,128)S(1)} all-to-all(f32[128,4,128]{2,1,0:T(4,128)S(1)} %bitcast.39), channel_id=1, replica_groups=mesh['area'=16,'tie'=8] {'area','tie'}, dimensions={0} | all-to-all | bytes 524288 | tf_op jit(solution)/shard_map/all_to_all | solution.py:270
  95.6 0.3 convolution_multiply_fusion.1
  95.9 0.2 fusion.11
  96.1 15.3 %all_to_all.44 = f32[128,4,128]{2,1,0:T(4,128)S(1)} all-to-all(f32[128,4,128]{2,1,0:T(4,128)S(1)} %bitcast.49), channel_id=1, replica_groups=mesh['area'=16,'tie'=8] {'area','tie'}, dimensions={0} | all-to-all | bytes 524288 | tf_op jit(solution)/shard_map/all_to_all | solution.py:270
  111.5 0.3 fusion.2
  111.8 15.3 %all_to_all.45 = f32[128,4,128]{2,1,0:T(4,128)S(1)} all-to-all(f32[128,4,128]{2,1,0:T(4,128)S(1)} %bitcast.41), channel_id=1, replica_groups=mesh['area'=16,'tie'=8] {'area','tie'}, dimensions={0} | all-to-all | bytes 524288 | tf_op jit(solution)/shard_map/all_to_all | solution.py:270
  127.1 0.3 convolution_multiply_fusion
  127.4 0.0 copy-start.4
  127.4 0.9 fusion.12
  128.3 4.3 %all-to-all-start.7 = ((f32[128,4,128]{2,1,0:T(4,128)}), f32[128,4,128]{2,1,0:T(4,128)S(1)}, u32[]{:S(2)}, u32[]{:S(2)}) async-start(f32[128,4,128]{2,1,0:T(4,128)} %bitcast.15), calls=%async_computation.7 | async-start | bytes 524288 | tf_op jit(solution)/shard_map/all_to_all | solution.py:270
  132.6 7.2 %states.1 = f32[4096,128]{1,0:T(8,128)} custom-call(s32[4,128]{1,0:T(4,128)} %row_ref.5, bf16[4,1024,1024]{2,1,0:T(8,128)(2,1)} %ginv_ref.3, bf16[4096,128]{1,0:T(8,128)(2,1)} %get-tuple-element.23.inner_ref, bf16[512,512]{1,0:T(8,128)(2,1)} %copy-done, bf16[512,128]{1,0:T(8,128)(2,1)} %copy-done.3), custom_call_target="tpu_custom_call" | custom-call | tf_op jit(solution)/shard_map/states/pallas_call | solution.py:288
  139.9 3.8 %all-to-all-done.7 = f32[128,4,128]{2,1,0:T(4,128)S(1)} async-done(((f32[128,4,128]{2,1,0:T(4,128)}), f32[128,4,128]{2,1,0:T(4,128)S(1)}, u32[]{:S(2)}, u32[]{:S(2)}) %all-to-all-start.7) | async-done | bytes 262176 | tf_op jit(solution)/shard_map/all_to_all | solution.py:270
  143.7 1.2 fusion.3
  (9 shorter events, 0.1 us)
Async XLA Ops:
  7.1 11.5 %copy-start.2 = (bf16[4,128,1024]{2,1,0:T(8,128)(2,1)}, bf16[4,128,1024]{2,1,0:T(8,128)(2,1)S(1)}, u32[]{:S(2)}) copy-start(bf16[4,128,1024]{2,1,0:T(8,128)(2,1)S(1)} %get-tuple-element.17.chosen_ref) | copy-start | bytes 3145732
  7.1 25.1 %all-to-all-start = ((f32[128,8,128]{2,1,0:T(8,128)}), f32[128,8,128]{2,1,0:T(8,128)S(1)}, u32[]{:S(2)}, u32[]{:S(2)}) async-start(f32[128,8,128]{2,1,0:T(8,128)} %bitcast), calls=%async_computation | async-start | bytes 1048576 | tf_op jit(solution)/shard_map/all_to_all | solution.py:270
  24.9 24.0 %copy-start = (bf16[512,512]{1,0:T(8,128)(2,1)}, bf16[512,512]{1,0:T(8,128)(2,1)S(1)}, u32[]{:S(2)}) copy-start(bf16[512,512]{1,0:T(8,128)(2,1)S(1)} %get-tuple-element.24.place_ref) | copy-start | bytes 1572868
  111.4 21.2 %copy-start.3 = (bf16[512,128]{1,0:T(8,128)(2,1)}, bf16[512,128]{1,0:T(8,128)(2,1)S(1)}, u32[]{:S(2)}) copy-start(bf16[512,128]{1,0:T(8,128)(2,1)S(1)} %add_convert_fusion.blend_ref) | copy-start | bytes 393220
  127.4 12.5 %copy-start.4 = (f32[64,128]{1,0:T(8,128)}, f32[64,128]{1,0:T(8,128)S(1)}, u32[]{:S(2)}) copy-start(f32[64,128]{1,0:T(8,128)S(1)} %convolution_multiply_fusion) | copy-start | bytes 98308
  128.3 15.4 %all-to-all-start.7 = ((f32[128,4,128]{2,1,0:T(4,128)}), f32[128,4,128]{2,1,0:T(4,128)S(1)}, u32[]{:S(2)}, u32[]{:S(2)}) async-start(f32[128,4,128]{2,1,0:T(4,128)} %bitcast.15), calls=%async_computation.7 | async-start | bytes 524288 | tf_op jit(solution)/shard_map/all_to_all | solution.py:270
  132.6 11.1 %copy-start.1 = (bf16[512,512]{1,0:T(8,128)(2,1)S(1)}, bf16[512,512]{1,0:T(8,128)(2,1)}, u32[]{:S(2)}) copy-start(bf16[512,512]{1,0:T(8,128)(2,1)} %copy-done) | copy-start | bytes 1572868

commit v6 on v5

--- a/solution.py
+++ b/solution.py
@@ -11,7 +11,7 @@
 PENALTY = 1.0
 PIECE = 128
 BUILD = 256
-WIDE = 8
+WIDE = SLOT + 1
 
 F32 = jnp.float32
 BF16 = jnp.bfloat16
@@ -104,9 +104,11 @@
         local_ids.append(jnp.where(row >= 0, (var & (VAR_DEV - 1)) + 1, 0).astype(F32))
     local_ids = jnp.broadcast_to(jnp.concatenate(local_ids, axis=1), (128, areas * bound))
     local_ref[...] = dot_nt(place_ref[...], local_ids.astype(BF16))
+    lane = iota((owners, snaps), 1)
+    ids = jnp.zeros((owners, snaps), F32)
     for k in range(SLOT):
-        at = pl.ds(k, owners, stride=SLOT)
-        out_ref[pl.ds(SLOT + k, owners, stride=WIDE), :] = local_ref[at, :]
+        ids += jnp.where(lane == k, local_ref[pl.ds(k, owners, stride=SLOT), :], 0.0)
+    out_ref[pl.ds(SLOT, owners, stride=WIDE), :] = ids
     for area in range(areas):
         block_copy(area).wait()
         right_copy(area).wait()
@@ -155,6 +157,27 @@
         mat_ref[...] = acc_ref[...].astype(BF16)
 
 
+def first_owner_kernel(in_ref, ret_ref, member_ref, inverse_ref):
+    sources = in_ref.shape[0] // WIDE
+    snaps = in_ref.shape[1]
+    ids = in_ref[pl.ds(SLOT, sources, stride=WIDE), :].astype(jnp.int32)
+    lane = iota((sources, 128), 1) + 1
+    parts = [(ids[:, k : k + 1] == lane).astype(F32) for k in range(SLOT)]
+    for k in range(SLOT):
+        member_ref[pl.ds(k, sources, stride=SLOT), :] = parts[k]
+    member = jnp.concatenate(parts, axis=0).astype(BF16)
+    values = [in_ref[pl.ds(k, sources, stride=WIDE), :] for k in range(SLOT)]
+    values = jnp.concatenate(values, axis=0)
+    columns = jnp.concatenate(split3(values) + [jnp.ones(values.shape, BF16)], axis=1)
+    sums = dot_t(member, columns)
+    inverse = 1.0 / jnp.maximum(sums[:, 3 * snaps :], 1.0)
+    inverse_ref[...] = inverse
+    consensus = join3(sums, 0, snaps) * inverse
+    back = join3(dot(member, jnp.concatenate(split3(consensus), axis=1)), 0, snaps)
+    for k in range(SLOT):
+        ret_ref[pl.ds(k, sources, stride=SLOT), :] = back[k * sources : (k + 1) * sources]
+
+
 def states_kernel(
     row_ref, ginv_ref, inner_ref, place_ref, blend_ref, states_ref,
     block_ref, right_ref, solved_ref, block_sems, right_sems, out_sems,
@@ -265,26 +288,34 @@
         name="prepare",
     )(bnd_row, bnd_var, chosen, rhs)
 
-    def exchange(x):
-        x = x.reshape(devices, -1, snaps)
-        return lax.all_to_all(x, ("area", "tie"), split_axis=0, concat_axis=0, tiled=True)
+    def exchange(x, rows=SLOT, width=snaps):
+        x = x.reshape(devices, rows, width)
+        x = lax.all_to_all(x, ("area", "tie"), split_axis=0, concat_axis=0, tiled=True)
+        return x.reshape(-1, snaps)
 
     base = local - dot(mat, term.astype(BF16))
     received, place, mat, base, term, inner = lax.optimization_barrier(
-        (exchange(outgoing), place, mat, base, term, inner)
+        (exchange(outgoing, 1, WIDE * snaps), place, mat, base, term, inner)
     )
-    incoming = received[:, :SLOT].reshape(slots, snaps)
-    ids = received[:, SLOT:].reshape(slots, snaps)[:, :VAR_DEV]
-    member = (ids == jnp.arange(1, VAR_DEV + 1, dtype=jnp.int32).astype(F32)).astype(F32)
-    inverse = 1.0 / jnp.maximum(jnp.sum(member, axis=0), 1.0)[:, None]
+    returning, member, inverse = pl.pallas_call(
+        first_owner_kernel,
+        in_specs=[pl.BlockSpec(memory_space=pltpu.VMEM)],
+        out_shape=[
+            pltpu.VMEM((slots, snaps), F32),
+            pltpu.VMEM((slots, 128), F32),
+            pltpu.VMEM((128, snaps), F32),
+        ],
+        name="first_owner",
+    )(pltpu.with_memory_space_constraint(received, pltpu.VMEM))
     for iteration in range(ITERS):
         if iteration > 0:
             blend = (term + PENALTY * (agreed - dual)).astype(BF16)
             local = (base + dot(mat, blend)) + dual
-            incoming = exchange(local).reshape(slots, snaps)
-        consensus = select("sv,sn->vn", member, incoming) * inverse
-        agreed = exchange(select("sv,vn->sn", member, consensus)).reshape(slots, snaps)
+            consensus = select("sv,sn->vn", member, exchange(local)) * inverse
+            returning = select("sv,vn->sn", member, consensus)
+        agreed = exchange(returning)
         dual = local - agreed
+    consensus = consensus[:VAR_DEV]
     states = pl.pallas_call(
         states_kernel,
         in_specs=[

time: 145 us -> 145 us (level)
  waiting for transfers between devices: 10.8 us -> 8.41 us
  local copies, waits for them, and re-layouts: 0.11 us -> 1.59 us
    all_to_all x2, waiting for transfers between devices: 10.8 us -> 8.41 us  [exchange(): lax.all_to_all(x, ('area', 'tie'), split_axis=0, concat_axis=0, tiled=True)]
    dot_general x9 -> x7, matrix products: 4.03 us -> 3.86 us  [select(): jnp.einsum(spec, a, b, precision=lax.Precision.HIGH, preferred_element_ty...]
  transfers between devices with their start and end apart: 2 -> 2, of which waited for: 2 -> 2; matrix products, arithmetic and copies ran while one was open for 0% -> 1% of each run, Pallas kernels for 9% -> 9%
where the time goes in v6:
time: 145 us
  blocking collectives  92.6 us (64%)
  Pallas kernels  20.6 us (14%)
  starting transfers between devices  15.8 us (11%)
  waiting for transfers between devices  8.41 us (6%)
  matrix products  5.06 us (3%)
  local copies, waits for them, and re-layouts  1.59 us (1%)
    all_to_all x6, blocking collectives, exchange(): lax.all_to_all(x, ('area', 'tie'), split_axis=0, concat_axis=0, tiled=True)  92.6 us
    all_to_all x2, starting transfers between devices, exchange(): lax.all_to_all(x, ('area', 'tie'), split_axis=0, concat_axis=0, tiled=True)  15.8 us
    all_to_all x2, waiting for transfers between devices, exchange(): lax.all_to_all(x, ('area', 'tie'), split_axis=0, concat_axis=0, tiled=True)  8.41 us
    pallas_call x1, Pallas kernels, on_device(): pl.pallas_call(states_kernel, in_specs=[small, anywhere, anywhere, pl.Blo...  7.22 us
    pallas_call x1, Pallas kernels, on_device(): pl.pallas_call(start_kernel, in_specs=[small, small, anywhere, anywhere],...  6.39 us
    pallas_call x1, Pallas kernels, on_device(): pl.pallas_call(prepare_kernel, grid=(areas,), in_specs=[whole(areas, boun...  6.27 us
    dot_general x7, matrix products, select(): jnp.einsum(spec, a, b, precision=lax.Precision.HIGH, preferred_element_ty...  3.86 us
  transfers between devices with their start and end apart: 2, of which 2 were waited for; matrix products, arithmetic and copies ran while one was open for 1% of the time, Pallas kernels for 9%

profile of v6, /device:TPU:1, one launch (start us, length us, event | category | flops | bytes accessed | tf_op | source)
XLA Modules:
  0.0 144.8 jit_solution(8925662992409797561)
XLA Ops:
  0.6 6.4 %start.1 = (f32[512,128]{1,0:T(8,128)S(1)}, f32[640,128]{1,0:T(8,128)}, bf16[4,128,1024]{2,1,0:T(8,128)(2,1)S(1)}) custom-call(s32[4,128]{1,0:T(4,128)} %row_ref.5, s32[4,128]{1,0:T(4,128)} %var_ref.3, bf16[4,1024,1024]{2,1,0:T(8,128)(2,1)} %ginv_ref.3, f32[4096,128]{1,0:T(8,128)} %rhs_ref.3), custom_call_target="tpu_custom_call" | custom-call | tf_op jit(solution)/shard_map/start/pallas_call | solution.py:246
  7.0 0.0 copy-start.2
  7.0 1.0 copy-done.2
  8.0 11.5 %all-to-all-start = ((f32[128,1,640]{2,1,0:T(1,128)}), f32[128,1,640]{2,1,0:T(1,128)S(1)}, u32[]{:S(2)}, u32[]{:S(2)}) async-start(f32[128,1,640]{2,1,0:T(1,128)} %bitcast), calls=%async_computation | async-start | bytes 655360 | tf_op jit(solution)/shard_map/all_to_all | solution.py:293
  19.5 6.3 %prepare.1 = (bf16[512,512]{1,0:T(8,128)(2,1)S(1)}, bf16[512,512]{1,0:T(8,128)(2,1)S(1)}, f32[512,128]{1,0:T(8,128)S(1)}, bf16[4096,128]{1,0:T(8,128)(2,1)}) custom-call(s32[4,128]{1,0:T(4,128)} %row_ref.5, s32[4,128]{1,0:T(4,128)} %var_ref.3, bf16[4,128,1024]{2,1,0:T(8,128)(2,1)} %copy-done.2, f32[4096,128]{1,0:T(8,128)} %rhs_ref.3), custom_call_target="tpu_custom_call" | custom-call | tf_op jit(solution)/shard_map/prepare/pallas_call | solution.py:265
  25.8 0.3 convolution_subtract_fusion
  26.1 5.2 %all-to-all-done = f32[128,1,640]{2,1,0:T(1,128)S(1)} async-done(((f32[128,1,640]{2,1,0:T(1,128)}), f32[128,1,640]{2,1,0:T(1,128)S(1)}, u32[]{:S(2)}, u32[]{:S(2)}) %all-to-all-start) | async-done | bytes 327712 | tf_op jit(solution)/shard_map/all_to_all | solution.py:293
  31.3 0.0 copy-done
  31.3 0.7 first_owner.1
  32.0 16.1 %all_to_all.40 = f32[128,4,128]{2,1,0:T(4,128)S(1)} all-to-all(f32[128,4,128]{2,1,0:T(4,128)S(1)} %bitcast.35), channel_id=1, replica_groups=mesh['area'=16,'tie'=8] {'area','tie'}, dimensions={0} | all-to-all | bytes 524288 | tf_op jit(solution)/shard_map/all_to_all | solution.py:293
  48.1 0.3 fusion
  48.4 15.3 %all_to_all.41 = f32[128,4,128]{2,1,0:T(4,128)S(1)} all-to-all(f32[128,4,128]{2,1,0:T(4,128)S(1)} %bitcast.37), channel_id=1, replica_groups=mesh['area'=16,'tie'=8] {'area','tie'}, dimensions={0} | all-to-all | bytes 524288 | tf_op jit(solution)/shard_map/all_to_all | solution.py:293
  63.7 0.4 convolution_multiply_fusion.2
  64.0 0.3 fusion.8
  64.3 15.3 %all_to_all.42 = f32[128,4,128]{2,1,0:T(4,128)S(1)} all-to-all(f32[128,4,128]{2,1,0:T(4,128)S(1)} %bitcast.45), channel_id=1, replica_groups=mesh['area'=16,'tie'=8] {'area','tie'}, dimensions={0} | all-to-all | bytes 524288 | tf_op jit(solution)/shard_map/all_to_all | solution.py:293
  79.6 0.3 fusion.1
  79.9 15.3 %all_to_all.43 = f32[128,4,128]{2,1,0:T(4,128)S(1)} all-to-all(f32[128,4,128]{2,1,0:T(4,128)S(1)} %bitcast.36), channel_id=1, replica_groups=mesh['area'=16,'tie'=8] {'area','tie'}, dimensions={0} | all-to-all | bytes 524288 | tf_op jit(solution)/shard_map/all_to_all | solution.py:293
  95.2 0.4 convolution_multiply_fusion.1
  95.6 0.3 fusion.9
  95.9 15.3 %all_to_all.44 = f32[128,4,128]{2,1,0:T(4,128)S(1)} all-to-all(f32[128,4,128]{2,1,0:T(4,128)S(1)} %bitcast.46), channel_id=1, replica_groups=mesh['area'=16,'tie'=8] {'area','tie'}, dimensions={0} | all-to-all | bytes 524288 | tf_op jit(solution)/shard_map/all_to_all | solution.py:293
  111.2 0.0 copy-start.3
  111.2 0.3 fusion.2
  111.5 15.3 %all_to_all.45 = f32[128,4,128]{2,1,0:T(4,128)S(1)} all-to-all(f32[128,4,128]{2,1,0:T(4,128)S(1)} %bitcast.38), channel_id=1, replica_groups=mesh['area'=16,'tie'=8] {'area','tie'}, dimensions={0} | all-to-all | bytes 524288 | tf_op jit(solution)/shard_map/all_to_all | solution.py:293
  126.8 0.4 convolution_multiply_fusion
  127.2 1.0 fusion.10
  128.2 4.3 %all-to-all-start.7 = ((f32[128,4,128]{2,1,0:T(4,128)}), f32[128,4,128]{2,1,0:T(4,128)S(1)}, u32[]{:S(2)}, u32[]{:S(2)}) async-start(f32[128,4,128]{2,1,0:T(4,128)} %bitcast.14), calls=%async_computation.7 | async-start | bytes 524288 | tf_op jit(solution)/shard_map/all_to_all | solution.py:293
  132.5 0.0 copy-done.3
  132.5 0.0 copy-start.1
  132.5 7.2 %states.1 = f32[4096,128]{1,0:T(8,128)} custom-call(s32[4,128]{1,0:T(4,128)} %row_ref.5, bf16[4,1024,1024]{2,1,0:T(8,128)(2,1)} %ginv_ref.3, bf16[4096,128]{1,0:T(8,128)(2,1)} %get-tuple-element.26.inner_ref, bf16[512,512]{1,0:T(8,128)(2,1)} %copy-done, bf16[512,128]{1,0:T(8,128)(2,1)} %copy-done.3), custom_call_target="tpu_custom_call" | custom-call | tf_op jit(solution)/shard_map/states/pallas_call | solution.py:319
  139.7 0.6 slice.4
  140.4 3.2 %all-to-all-done.7 = f32[128,4,128]{2,1,0:T(4,128)S(1)} async-done(((f32[128,4,128]{2,1,0:T(4,128)}), f32[128,4,128]{2,1,0:T(4,128)S(1)}, u32[]{:S(2)}, u32[]{:S(2)}) %all-to-all-start.7) | async-done | bytes 262176 | tf_op jit(solution)/shard_map/all_to_all | solution.py:293
  143.6 1.2 fusion.3
  (3 shorter events, 0.0 us)
Async XLA Ops:
  7.0 1.0 copy-start.2
  8.0 23.3 %all-to-all-start = ((f32[128,1,640]{2,1,0:T(1,128)}), f32[128,1,640]{2,1,0:T(1,128)S(1)}, u32[]{:S(2)}, u32[]{:S(2)}) async-start(f32[128,1,640]{2,1,0:T(1,128)} %bitcast), calls=%async_computation | async-start | bytes 655360 | tf_op jit(solution)/shard_map/all_to_all | solution.py:293
  25.8 5.5 %copy-start = (bf16[512,512]{1,0:T(8,128)(2,1)}, bf16[512,512]{1,0:T(8,128)(2,1)S(1)}, u32[]{:S(2)}) copy-start(bf16[512,512]{1,0:T(8,128)(2,1)S(1)} %get-tuple-element.27.place_ref) | copy-start | bytes 1572868
  111.2 21.3 %copy-start.3 = (bf16[512,128]{1,0:T(8,128)(2,1)}, bf16[512,128]{1,0:T(8,128)(2,1)S(1)}, u32[]{:S(2)}) copy-start(bf16[512,128]{1,0:T(8,128)(2,1)S(1)} %add_convert_fusion.blend_ref) | copy-start | bytes 393220
  128.2 15.4 %all-to-all-start.7 = ((f32[128,4,128]{2,1,0:T(4,128)}), f32[128,4,128]{2,1,0:T(4,128)S(1)}, u32[]{:S(2)}, u32[]{:S(2)}) async-start(f32[128,4,128]{2,1,0:T(4,128)} %bitcast.14), calls=%async_computation.7 | async-start | bytes 524288 | tf_op jit(solution)/shard_map/all_to_all | solution.py:293
  132.5 11.1 %copy-start.1 = (bf16[512,512]{1,0:T(8,128)(2,1)S(1)}, bf16[512,512]{1,0:T(8,128)(2,1)}, u32[]{:S(2)}) copy-start(bf16[512,512]{1,0:T(8,128)(2,1)} %copy-done) | copy-start | bytes 1572868

commit v7 on v6

--- a/solution.py
+++ b/solution.py
@@ -37,10 +37,6 @@
 
 def dot_t(a, b):
     return lax.dot_general(a, b, (((0,), (0,)), ((), ())), preferred_element_type=F32)
-
-
-def dot_nt(a, b):
-    return lax.dot_general(a, b, (((1,), (1,)), ((), ())), preferred_element_type=F32)
 
 
 def iota(shape, dim):
@@ -74,7 +70,8 @@
 
 def start_kernel(
     row_ref, var_ref, ginv_ref, rhs_ref, local_ref, out_ref, chosen_ref,
-    block_ref, right_ref, carry_ref, place_ref, solved_ref, block_sems, right_sems,
+    block_ref, right_ref, picked_ref, carry_ref, place_ref, solved_ref,
+    block_sems, right_sems, out_sems,
 ):
     areas, bound = row_ref.shape
     state = ginv_ref.shape[1]
@@ -87,6 +84,9 @@
     def right_copy(area):
         rows = pl.ds(area * state, state)
         return pltpu.make_async_copy(rhs_ref.at[rows], right_ref.at[rows], right_sems.at[area])
+
+    def out_copy(area):
+        return pltpu.make_async_copy(picked_ref.at[area], chosen_ref.at[area], out_sems.at[area])
 
     for area in range(areas):
         block_copy(area).start()
@@ -101,9 +101,11 @@
             entry_slots(row, var, carry_ref, owners), slots
         )
         picks.append(picking(row, state))
-        local_ids.append(jnp.where(row >= 0, (var & (VAR_DEV - 1)) + 1, 0).astype(F32))
-    local_ids = jnp.broadcast_to(jnp.concatenate(local_ids, axis=1), (128, areas * bound))
-    local_ref[...] = dot_nt(place_ref[...], local_ids.astype(BF16))
+        local_id = jnp.where(row >= 0, (var & (VAR_DEV - 1)) + 1, 0).astype(F32)
+        local_ids.append(jnp.broadcast_to(local_id, (snaps, bound)).T.astype(BF16))
+    local_ids = jnp.concatenate(local_ids, axis=0)
+    for at in range(0, slots, PIECE):
+        local_ref[at : at + PIECE, :] = dot(place_ref[at : at + PIECE, :], local_ids)
     lane = iota((owners, snaps), 1)
     ids = jnp.zeros((owners, snaps), F32)
     for k in range(SLOT):
@@ -112,49 +114,76 @@
     for area in range(areas):
         block_copy(area).wait()
         right_copy(area).wait()
-        chosen = dot(picks[area], block_ref[area]).astype(BF16)
-        chosen_ref[area] = chosen
-        solved = dot(chosen, right_ref[area * state : (area + 1) * state, :].astype(BF16))
+        for at in range(0, state, BUILD):
+            part = dot(picks[area], block_ref[area, :, at : at + BUILD])
+            picked_ref[area, :, at : at + BUILD] = part.astype(BF16)
+        out_copy(area).start()
+        right = right_ref[area * state : (area + 1) * state, :].astype(BF16)
+        solved = dot(picked_ref[area], right)
         solved_ref[area * bound : (area + 1) * bound, :] = jnp.concatenate(split3(solved), axis=1)
-    local_ref[...] = join3(dot(place_ref[...], solved_ref[...]), 0, snaps)
+    for at in range(0, slots, PIECE):
+        local_ref[at : at + PIECE, :] = join3(dot(place_ref[at : at + PIECE, :], solved_ref[...]), 0, snaps)
     for k in range(SLOT):
         at = pl.ds(k, owners, stride=SLOT)
         out_ref[pl.ds(k, owners, stride=WIDE), :] = local_ref[at, :]
+    for area in range(areas):
+        out_copy(area).wait()
 
 
 def prepare_kernel(
-    row_ref, var_ref, chosen_ref, rhs_ref,
-    place_ref, mat_ref, term_ref, inner_ref,
-    carry_ref, acc_ref,
+    row_ref, var_ref, chosen_ref, rhs_ref, back_ref, mat_ref, term_ref, inner_ref,
+    picked_ref, right_ref, kept_ref, carry_ref, rows_ref, spread_ref, place_ref,
+    picked_sems, right_sems, out_sems,
 ):
-    area = pl.program_id(0)
-    slots = mat_ref.shape[0]
-    state, snaps = rhs_ref.shape
-
-    @pl.when(area == 0)
-    def _():
-        carry_ref[...] = jnp.zeros_like(carry_ref)
-        acc_ref[...] = jnp.zeros_like(acc_ref)
-        term_ref[...] = jnp.zeros_like(term_ref)
-
-    row = row_ref[pl.ds(area, 1), :]
-    var = var_ref[pl.ds(area, 1), :]
-    place = placing(entry_slots(row, var, carry_ref, slots // SLOT), slots)
-    place_ref[...] = place
-    for at in range(0, state, BUILD):
-        bound_rows = dot(placing(row - at, BUILD), jnp.ones((row.shape[1], snaps), BF16)) > 0.0
-        inner_ref[at : at + BUILD, :] = jnp.where(
-            bound_rows, 0.0, rhs_ref[at : at + BUILD, :]
-        ).astype(BF16)
-    at_rows = dot(picking(row, state), jnp.concatenate(split3(rhs_ref[...]), axis=1))
-    coupling = dot(chosen_ref[0], placing(row, state))
-    at_slots = dot(place, jnp.concatenate([at_rows, coupling], axis=1).astype(BF16))
-    term_ref[...] += join3(at_slots, 0, snaps)
-    acc_ref[...] += dot_nt(at_slots[:, 3 * snaps :].astype(BF16), place)
-
-    @pl.when(area == pl.num_programs(0) - 1)
-    def _():
-        mat_ref[...] = acc_ref[...].astype(BF16)
+    areas, bound = row_ref.shape
+    state = chosen_ref.shape[2]
+    slots, snaps = term_ref.shape
+
+    def picked_copy(area):
+        return pltpu.make_async_copy(chosen_ref.at[area], picked_ref.at[area], picked_sems.at[area])
+
+    def right_copy(area):
+        rows = pl.ds(area * state, state)
+        return pltpu.make_async_copy(rhs_ref.at[rows], right_ref.at[rows], right_sems.at[area])
+
+    def out_copy(area):
+        rows = pl.ds(area * state, state)
+        return pltpu.make_async_copy(kept_ref.at[rows], inner_ref.at[rows], out_sems.at[area])
+
+    for area in range(areas):
+        right_copy(area).start()
+        picked_copy(area).start()
+    carry_ref[...] = jnp.zeros_like(carry_ref)
+    for area in range(areas):
+        var = var_ref[area : area + 1, :]
+        slot = entry_slots(row_ref[area : area + 1, :], var, carry_ref, slots // SLOT)
+        entries = slice(area * bound, (area + 1) * bound)
+        place_ref[:, entries] = placing(slot, slots)
+        back_ref[entries, :] = picking(slot, slots)
+    ones = jnp.ones((bound, snaps), BF16)
+    for area in range(areas):
+        entries = slice(area * bound, (area + 1) * bound)
+        row = row_ref[area : area + 1, :]
+        right_copy(area).wait()
+        for at in range(0, state, BUILD):
+            here = slice(area * state + at, area * state + at + BUILD)
+            is_bound = dot(placing(row - at, BUILD), ones) > 0.0
+            kept_ref[here, :] = jnp.where(is_bound, 0.0, right_ref[here, :]).astype(BF16)
+        out_copy(area).start()
+        right = right_ref[area * state : (area + 1) * state, :]
+        at_rows = dot(picking(row, state), jnp.concatenate(split3(right), axis=1))
+        rows_ref[entries, :] = at_rows.astype(BF16)
+        picked_copy(area).wait()
+        coupling = dot(picked_ref[area], placing(row, state)).astype(BF16)
+        for at in range(0, slots, PIECE):
+            spread = dot(place_ref[at : at + PIECE, entries], coupling)
+            spread_ref[at : at + PIECE, entries] = spread.astype(BF16)
+    for at in range(0, slots, PIECE):
+        here = slice(at, at + PIECE)
+        term_ref[here, :] = join3(dot(place_ref[here, :], rows_ref[...]), 0, snaps)
+        mat_ref[here, :] = dot(spread_ref[here, :], back_ref[...]).astype(BF16)
+    for area in range(areas):
+        out_copy(area).wait()
 
 
 def first_owner_kernel(in_ref, ret_ref, member_ref, inverse_ref):
@@ -164,14 +193,14 @@
     lane = iota((sources, 128), 1) + 1
     parts = [(ids[:, k : k + 1] == lane).astype(F32) for k in range(SLOT)]
     for k in range(SLOT):
-        member_ref[pl.ds(k, sources, stride=SLOT), :] = parts[k]
+        member_ref[pl.ds(k, sources, stride=SLOT), :] = parts[k][:, :VAR_DEV]
     member = jnp.concatenate(parts, axis=0).astype(BF16)
     values = [in_ref[pl.ds(k, sources, stride=WIDE), :] for k in range(SLOT)]
     values = jnp.concatenate(values, axis=0)
     columns = jnp.concatenate(split3(values) + [jnp.ones(values.shape, BF16)], axis=1)
     sums = dot_t(member, columns)
     inverse = 1.0 / jnp.maximum(sums[:, 3 * snaps :], 1.0)
-    inverse_ref[...] = inverse
+    inverse_ref[...] = inverse[:VAR_DEV]
     consensus = join3(sums, 0, snaps) * inverse
     back = join3(dot(member, jnp.concatenate(split3(consensus), axis=1)), 0, snaps)
     for k in range(SLOT):
@@ -179,7 +208,7 @@
 
 
 def states_kernel(
-    row_ref, ginv_ref, inner_ref, place_ref, blend_ref, states_ref,
+    row_ref, ginv_ref, inner_ref, back_ref, blend_ref, states_ref,
     block_ref, right_ref, solved_ref, block_sems, right_sems, out_sems,
 ):
     areas, bound = row_ref.shape
@@ -202,7 +231,7 @@
     for area in range(areas):
         right_copy(area).start()
         block_copy(area).start()
-    entry_rows = dot_t(place_ref[...], blend_ref[...]).astype(BF16)
+    entry_rows = dot(back_ref[...], blend_ref[...]).astype(BF16)
     for area in range(areas):
         row = row_ref[area : area + 1, :]
         rows = entry_rows[area * bound : (area + 1) * bound]
@@ -237,54 +266,53 @@
     slots = devices * SLOT
     entries = areas * bound
 
-    def whole(*dims):
-        return pl.BlockSpec(dims, lambda a: (0,) * len(dims))
-
-    in_order = pltpu.CompilerParams(dimension_semantics=("arbitrary",))
     anywhere = pl.BlockSpec(memory_space=pl.ANY)
     small = pl.BlockSpec((areas, bound), lambda: (0, 0))
+    whole = pl.BlockSpec(memory_space=pltpu.VMEM)
     local, outgoing, chosen = pl.pallas_call(
         start_kernel,
         in_specs=[small, small, anywhere, anywhere],
+        out_specs=[whole, whole, anywhere],
         out_shape=[
             pltpu.VMEM((slots, snaps), F32),
             pltpu.VMEM((devices * WIDE, snaps), F32),
-            pltpu.VMEM((areas, bound, state), BF16),
+            shape((areas, bound, state), BF16),
         ],
         scratch_shapes=[
             pltpu.VMEM((areas, state, state), BF16),
             pltpu.VMEM((areas * state, snaps), F32),
+            pltpu.VMEM((areas, bound, state), BF16),
             pltpu.VMEM((devices, bound), F32),
             pltpu.VMEM((slots, entries), BF16),
             pltpu.VMEM((entries, 3 * snaps), BF16),
             pltpu.SemaphoreType.DMA((areas,)),
             pltpu.SemaphoreType.DMA((areas,)),
+            pltpu.SemaphoreType.DMA((areas,)),
         ],
         name="start",
     )(bnd_row, bnd_var, ginv, rhs)
-    place, mat, term, inner = pl.pallas_call(
+    back, mat, term, inner = pl.pallas_call(
         prepare_kernel,
-        grid=(areas,),
-        in_specs=[
-            whole(areas, bound),
-            whole(areas, bound),
-            pl.BlockSpec((1, bound, state), lambda a: (a, 0, 0)),
-            pl.BlockSpec((state, snaps), lambda a: (a, 0)),
-        ],
-        out_specs=[
-            pl.BlockSpec((slots, bound), lambda a: (0, a)),
-            whole(slots, slots),
-            whole(slots, snaps),
-            pl.BlockSpec((state, snaps), lambda a: (a, 0)),
-        ],
+        in_specs=[small, small, anywhere, anywhere],
+        out_specs=[whole, whole, whole, anywhere],
         out_shape=[
-            pltpu.VMEM((slots, entries), BF16),
+            pltpu.VMEM((entries, slots), BF16),
             pltpu.VMEM((slots, slots), BF16),
             pltpu.VMEM((slots, snaps), F32),
             shape((areas * state, snaps), BF16),
         ],
-        scratch_shapes=[pltpu.VMEM((devices, bound), F32), pltpu.VMEM((slots, slots), F32)],
-        compiler_params=in_order,
+        scratch_shapes=[
+            pltpu.VMEM((areas, bound, state), BF16),
+            pltpu.VMEM((areas * state, snaps), F32),
+            pltpu.VMEM((areas * state, snaps), BF16),
+            pltpu.VMEM((devices, bound), F32),
+            pltpu.VMEM((entries, 3 * snaps), BF16),
+            pltpu.VMEM((slots, entries), BF16),
+            pltpu.VMEM((slots, entries), BF16),
+            pltpu.SemaphoreType.DMA((areas,)),
+            pltpu.SemaphoreType.DMA((areas,)),
+            pltpu.SemaphoreType.DMA((areas,)),
+        ],
         name="prepare",
     )(bnd_row, bnd_var, chosen, rhs)
 
@@ -294,16 +322,16 @@
         return x.reshape(-1, snaps)
 
     base = local - dot(mat, term.astype(BF16))
-    received, place, mat, base, term, inner = lax.optimization_barrier(
-        (exchange(outgoing, 1, WIDE * snaps), place, mat, base, term, inner)
+    received, back, mat, base, term, inner = lax.optimization_barrier(
+        (exchange(outgoing, 1, WIDE * snaps), back, mat, base, term, inner)
     )
     returning, member, inverse = pl.pallas_call(
         first_owner_kernel,
-        in_specs=[pl.BlockSpec(memory_space=pltpu.VMEM)],
+        in_specs=[whole],
         out_shape=[
             pltpu.VMEM((slots, snaps), F32),
-            pltpu.VMEM((slots, 128), F32),
-            pltpu.VMEM((128, snaps), F32),
+            pltpu.VMEM((slots, VAR_DEV), F32),
+            pltpu.VMEM((VAR_DEV, snaps), F32),
         ],
         name="first_owner",
     )(pltpu.with_memory_space_constraint(received, pltpu.VMEM))
@@ -315,14 +343,13 @@
             returning = select("sv,vn->sn", member, consensus)
         agreed = exchange(returning)
         dual = local - agreed
-    consensus = consensus[:VAR_DEV]
     states = pl.pallas_call(
         states_kernel,
         in_specs=[
             small,
             anywhere,
             anywhere,
-            pl.BlockSpec((slots, entries), lambda: (0, 0)),
+            pl.BlockSpec((entries, slots), lambda: (0, 0)),
             pl.BlockSpec((slots, snaps), lambda: (0, 0)),
         ],
         out_specs=anywhere,
@@ -336,8 +363,8 @@
             pltpu.SemaphoreType.DMA((areas,)),
         ],
         name="states",
-    )(bnd_row, ginv, inner, place, blend)
-    dual = select("se,sn->en", place.astype(F32), dual)
+    )(bnd_row, ginv, inner, back, blend)
+    dual = select("es,sn->en", back.astype(F32), dual)
     return states, consensus, dual
 
 

time: 145 us -> 144 us (level)
  local copies, waits for them, and re-layouts: 1.59 us -> 0.02 us
  transfers between devices with their start and end apart: 2 -> 2, of which waited for: 2 -> 2; matrix products, arithmetic and copies ran while one was open for 1% -> 0% of each run, Pallas kernels for 9% -> 9%
where the time goes in v7:
time: 144 us
  blocking collectives  91.9 us (64%)
  Pallas kernels  20.4 us (14%)
  starting transfers between devices  15.8 us (11%)
  waiting for transfers between devices  9.67 us (7%)
  matrix products  4.88 us (3%)
    all_to_all x6, blocking collectives, exchange(): lax.all_to_all(x, ('area', 'tie'), split_axis=0, concat_axis=0, tiled=True)  91.9 us
    all_to_all x2, starting transfers between devices, exchange(): lax.all_to_all(x, ('area', 'tie'), split_axis=0, concat_axis=0, tiled=True)  15.8 us
    all_to_all x2, waiting for transfers between devices, exchange(): lax.all_to_all(x, ('area', 'tie'), split_axis=0, concat_axis=0, tiled=True)  9.67 us
    pallas_call x1, Pallas kernels, on_device(): pl.pallas_call(states_kernel, in_specs=[small, anywhere, anywhere, pl.Blo...  7.22 us
    pallas_call x1, Pallas kernels, on_device(): pl.pallas_call(start_kernel, in_specs=[small, small, anywhere, anywhere],...  6.87 us
    pallas_call x1, Pallas kernels, on_device(): pl.pallas_call(prepare_kernel, in_specs=[small, small, anywhere, anywhere...  5.6 us
    dot_general x7, matrix products, select(): jnp.einsum(spec, a, b, precision=lax.Precision.HIGH, preferred_element_ty...  3.69 us
  transfers between devices with their start and end apart: 2, of which 2 were waited for; matrix products, arithmetic and copies ran while one was open for 0% of the time, Pallas kernels for 9%

profile of v7, /device:TPU:1, one launch (start us, length us, event | category | flops | bytes accessed | tf_op | source)
XLA Modules:
  0.0 143.5 jit_solution(14501798100646127297)
XLA Ops:
  0.6 6.9 %start.1 = (f32[512,128]{1,0:T(8,128)S(1)}, f32[640,128]{1,0:T(8,128)}, bf16[4,128,1024]{2,1,0:T(8,128)(2,1)}) custom-call(s32[4,128]{1,0:T(4,128)} %row_ref.5, s32[4,128]{1,0:T(4,128)} %var_ref.3, bf16[4,1024,1024]{2,1,0:T(8,128)(2,1)} %ginv_ref.3, f32[4096,128]{1,0:T(8,128)} %rhs_ref.3), custom_call_target="tpu_custom_call" | custom-call | tf_op jit(solution)/shard_map/start/pallas_call | solution.py:272
  7.5 11.5 %all-to-all-start = ((f32[128,1,640]{2,1,0:T(1,128)}), f32[128,1,640]{2,1,0:T(1,128)S(1)}, u32[]{:S(2)}, u32[]{:S(2)}) async-start(f32[128,1,640]{2,1,0:T(1,128)} %bitcast), calls=%async_computation | async-start | bytes 655360 | tf_op jit(solution)/shard_map/all_to_all | solution.py:321
  19.0 5.6 %prepare.1 = (bf16[512,512]{1,0:T(8,128)(2,1)S(1)}, bf16[512,512]{1,0:T(8,128)(2,1)S(1)}, f32[512,128]{1,0:T(8,128)S(1)}, bf16[4096,128]{1,0:T(8,128)(2,1)}) custom-call(s32[4,128]{1,0:T(4,128)} %row_ref.5, s32[4,128]{1,0:T(4,128)} %var_ref.3, bf16[4,128,1024]{2,1,0:T(8,128)(2,1)} %get-tuple-element.20.chosen_ref, f32[4096,128]{1,0:T(8,128)} %rhs_ref.3), custom_call_target="tpu_custom_call" | custom-call | tf_op jit(solution)/shard_map/prepare/pallas_call | solution.py:294
  24.6 0.0 copy-start
  24.6 0.3 convolution_subtract_fusion
  24.9 5.9 %all-to-all-done = f32[128,1,640]{2,1,0:T(1,128)S(1)} async-done(((f32[128,1,640]{2,1,0:T(1,128)}), f32[128,1,640]{2,1,0:T(1,128)S(1)}, u32[]{:S(2)}, u32[]{:S(2)}) %all-to-all-start) | async-done | bytes 327712 | tf_op jit(solution)/shard_map/all_to_all | solution.py:321
  30.8 0.0 copy-done
  30.8 0.7 first_owner.1
  31.5 15.4 %all_to_all.40 = f32[128,4,128]{2,1,0:T(4,128)S(1)} all-to-all(f32[128,4,128]{2,1,0:T(4,128)S(1)} %bitcast.35), channel_id=1, replica_groups=mesh['area'=16,'tie'=8] {'area','tie'}, dimensions={0} | all-to-all | bytes 524288 | tf_op jit(solution)/shard_map/all_to_all | solution.py:321
  46.9 0.3 fusion
  47.2 15.3 %all_to_all.41 = f32[128,4,128]{2,1,0:T(4,128)S(1)} all-to-all(f32[128,4,128]{2,1,0:T(4,128)S(1)} %bitcast.37), channel_id=1, replica_groups=mesh['area'=16,'tie'=8] {'area','tie'}, dimensions={0} | all-to-all | bytes 524288 | tf_op jit(solution)/shard_map/all_to_all | solution.py:321
  62.5 0.4 convolution_multiply_fusion.2
  62.9 0.2 fusion.8
  63.2 15.3 %all_to_all.42 = f32[128,4,128]{2,1,0:T(4,128)S(1)} all-to-all(f32[128,4,128]{2,1,0:T(4,128)S(1)} %bitcast.45), channel_id=1, replica_groups=mesh['area'=16,'tie'=8] {'area','tie'}, dimensions={0} | all-to-all | bytes 524288 | tf_op jit(solution)/shard_map/all_to_all | solution.py:321
  78.5 0.3 fusion.1
  78.8 15.3 %all_to_all.43 = f32[128,4,128]{2,1,0:T(4,128)S(1)} all-to-all(f32[128,4,128]{2,1,0:T(4,128)S(1)} %bitcast.36), channel_id=1, replica_groups=mesh['area'=16,'tie'=8] {'area','tie'}, dimensions={0} | all-to-all | bytes 524288 | tf_op jit(solution)/shard_map/all_to_all | solution.py:321
  94.1 0.4 convolution_multiply_fusion.1
  94.4 0.2 fusion.9
  94.7 15.3 %all_to_all.44 = f32[128,4,128]{2,1,0:T(4,128)S(1)} all-to-all(f32[128,4,128]{2,1,0:T(4,128)S(1)} %bitcast.46), channel_id=1, replica_groups=mesh['area'=16,'tie'=8] {'area','tie'}, dimensions={0} | all-to-all | bytes 524288 | tf_op jit(solution)/shard_map/all_to_all | solution.py:321
  110.0 0.0 copy-start.2
  110.0 0.3 fusion.2
  110.3 15.3 %all_to_all.45 = f32[128,4,128]{2,1,0:T(4,128)S(1)} all-to-all(f32[128,4,128]{2,1,0:T(4,128)S(1)} %bitcast.38), channel_id=1, replica_groups=mesh['area'=16,'tie'=8] {'area','tie'}, dimensions={0} | all-to-all | bytes 524288 | tf_op jit(solution)/shard_map/all_to_all | solution.py:321
  125.6 0.4 convolution_multiply_fusion
  126.0 0.0 copy-start.3
  126.0 0.9 fusion.10
  127.0 4.3 %all-to-all-start.7 = ((f32[128,4,128]{2,1,0:T(4,128)}), f32[128,4,128]{2,1,0:T(4,128)S(1)}, u32[]{:S(2)}, u32[]{:S(2)}) async-start(f32[128,4,128]{2,1,0:T(4,128)} %bitcast.14), calls=%async_computation.7 | async-start | bytes 524288 | tf_op jit(solution)/shard_map/all_to_all | solution.py:321
  131.3 0.0 copy-done.2
  131.3 0.0 copy-start.1
  131.3 7.2 %states.1 = f32[4096,128]{1,0:T(8,128)} custom-call(s32[4,128]{1,0:T(4,128)} %row_ref.5, bf16[4,1024,1024]{2,1,0:T(8,128)(2,1)} %ginv_ref.3, bf16[4096,128]{1,0:T(8,128)(2,1)} %get-tuple-element.26.inner_ref, bf16[512,512]{1,0:T(8,128)(2,1)} %copy-done, bf16[512,128]{1,0:T(8,128)(2,1)} %copy-done.2), custom_call_target="tpu_custom_call" | custom-call | tf_op jit(solution)/shard_map/states/pallas_call | solution.py:346
  138.6 0.0 copy-done.3
  138.6 3.8 %all-to-all-done.7 = f32[128,4,128]{2,1,0:T(4,128)S(1)} async-done(((f32[128,4,128]{2,1,0:T(4,128)}), f32[128,4,128]{2,1,0:T(4,128)S(1)}, u32[]{:S(2)}, u32[]{:S(2)}) %all-to-all-start.7) | async-done | bytes 262176 | tf_op jit(solution)/shard_map/all_to_all | solution.py:321
  142.4 1.1 fusion.3
  (2 shorter events, 0.0 us)
Async XLA Ops:
  7.5 23.3 %all-to-all-start = ((f32[128,1,640]{2,1,0:T(1,128)}), f32[128,1,640]{2,1,0:T(1,128)S(1)}, u32[]{:S(2)}, u32[]{:S(2)}) async-start(f32[128,1,640]{2,1,0:T(1,128)} %bitcast), calls=%async_computation | async-start | bytes 655360 | tf_op jit(solution)/shard_map/all_to_all | solution.py:321
  24.6 6.2 %copy-start = (bf16[512,512]{1,0:T(8,128)(2,1)}, bf16[512,512]{1,0:T(8,128)(2,1)S(1)}, u32[]{:S(2)}) copy-start(bf16[512,512]{1,0:T(8,128)(2,1)S(1)} %get-tuple-element.27.back_ref) | copy-start | bytes 1572868
  110.0 21.3 %copy-start.2 = (bf16[512,128]{1,0:T(8,128)(2,1)}, bf16[512,128]{1,0:T(8,128)(2,1)S(1)}, u32[]{:S(2)}) copy-start(bf16[512,128]{1,0:T(8,128)(2,1)S(1)} %add_convert_fusion.blend_ref) | copy-start | bytes 393220
  126.0 12.5 %copy-start.3 = (f32[64,128]{1,0:T(8,128)}, f32[64,128]{1,0:T(8,128)S(1)}, u32[]{:S(2)}) copy-start(f32[64,128]{1,0:T(8,128)S(1)} %convolution_multiply_fusion) | copy-start | bytes 98308
  127.0 15.4 %all-to-all-start.7 = ((f32[128,4,128]{2,1,0:T(4,128)}), f32[128,4,128]{2,1,0:T(4,128)S(1)}, u32[]{:S(2)}, u32[]{:S(2)}) async-start(f32[128,4,128]{2,1,0:T(4,128)} %bitcast.14), calls=%async_computation.7 | async-start | bytes 524288 | tf_op jit(solution)/shard_map/all_to_all | solution.py:321
  131.3 11.1 %copy-start.1 = (bf16[512,512]{1,0:T(8,128)(2,1)S(1)}, bf16[512,512]{1,0:T(8,128)(2,1)}, u32[]{:S(2)}) copy-start(bf16[512,512]{1,0:T(8,128)(2,1)} %copy-done) | copy-start | bytes 1572868

commit v8 on v7

--- a/solution.py
+++ b/solution.py
@@ -11,6 +11,7 @@
 PENALTY = 1.0
 PIECE = 128
 BUILD = 256
+OUT = 512
 WIDE = SLOT + 1
 
 F32 = jnp.float32
@@ -69,9 +70,9 @@
 
 
 def start_kernel(
-    row_ref, var_ref, ginv_ref, rhs_ref, local_ref, out_ref, chosen_ref,
+    row_ref, var_ref, ginv_ref, rhs_ref, local_ref, out_ref, couple_ref,
     block_ref, right_ref, picked_ref, carry_ref, place_ref, solved_ref,
-    block_sems, right_sems, out_sems,
+    block_sems, right_sems,
 ):
     areas, bound = row_ref.shape
     state = ginv_ref.shape[1]
@@ -85,14 +86,12 @@
         rows = pl.ds(area * state, state)
         return pltpu.make_async_copy(rhs_ref.at[rows], right_ref.at[rows], right_sems.at[area])
 
-    def out_copy(area):
-        return pltpu.make_async_copy(picked_ref.at[area], chosen_ref.at[area], out_sems.at[area])
-
     for area in range(areas):
         block_copy(area).start()
         right_copy(area).start()
     carry_ref[...] = jnp.zeros_like(carry_ref)
     picks = []
+    columns = []
     local_ids = []
     for area in range(areas):
         row = row_ref[area : area + 1, :]
@@ -101,6 +100,7 @@
             entry_slots(row, var, carry_ref, owners), slots
         )
         picks.append(picking(row, state))
+        columns.append(placing(row, state))
         local_id = jnp.where(row >= 0, (var & (VAR_DEV - 1)) + 1, 0).astype(F32)
         local_ids.append(jnp.broadcast_to(local_id, (snaps, bound)).T.astype(BF16))
     local_ids = jnp.concatenate(local_ids, axis=0)
@@ -116,31 +116,27 @@
         right_copy(area).wait()
         for at in range(0, state, BUILD):
             part = dot(picks[area], block_ref[area, :, at : at + BUILD])
-            picked_ref[area, :, at : at + BUILD] = part.astype(BF16)
-        out_copy(area).start()
+            picked_ref[:, at : at + BUILD] = part.astype(BF16)
         right = right_ref[area * state : (area + 1) * state, :].astype(BF16)
-        solved = dot(picked_ref[area], right)
+        both = dot(picked_ref[...], jnp.concatenate([right, columns[area]], axis=1))
+        solved = both[:, :snaps]
+        couple_ref[area] = both[:, snaps:].astype(BF16)
         solved_ref[area * bound : (area + 1) * bound, :] = jnp.concatenate(split3(solved), axis=1)
     for at in range(0, slots, PIECE):
         local_ref[at : at + PIECE, :] = join3(dot(place_ref[at : at + PIECE, :], solved_ref[...]), 0, snaps)
     for k in range(SLOT):
         at = pl.ds(k, owners, stride=SLOT)
         out_ref[pl.ds(k, owners, stride=WIDE), :] = local_ref[at, :]
-    for area in range(areas):
-        out_copy(area).wait()
 
 
 def prepare_kernel(
-    row_ref, var_ref, chosen_ref, rhs_ref, back_ref, mat_ref, term_ref, inner_ref,
-    picked_ref, right_ref, kept_ref, carry_ref, rows_ref, spread_ref, place_ref,
-    picked_sems, right_sems, out_sems,
+    row_ref, var_ref, couple_ref, rhs_ref, back_ref, mat_ref, term_ref, inner_ref,
+    right_ref, kept_ref, carry_ref, rows_ref, spread_ref, place_ref,
+    right_sems, out_sems,
 ):
     areas, bound = row_ref.shape
-    state = chosen_ref.shape[2]
+    state = rhs_ref.shape[0] // areas
     slots, snaps = term_ref.shape
-
-    def picked_copy(area):
-        return pltpu.make_async_copy(chosen_ref.at[area], picked_ref.at[area], picked_sems.at[area])
 
     def right_copy(area):
         rows = pl.ds(area * state, state)
@@ -152,7 +148,6 @@
 
     for area in range(areas):
         right_copy(area).start()
-        picked_copy(area).start()
     carry_ref[...] = jnp.zeros_like(carry_ref)
     for area in range(areas):
         var = var_ref[area : area + 1, :]
@@ -173,10 +168,8 @@
         right = right_ref[area * state : (area + 1) * state, :]
         at_rows = dot(picking(row, state), jnp.concatenate(split3(right), axis=1))
         rows_ref[entries, :] = at_rows.astype(BF16)
-        picked_copy(area).wait()
-        coupling = dot(picked_ref[area], placing(row, state)).astype(BF16)
         for at in range(0, slots, PIECE):
-            spread = dot(place_ref[at : at + PIECE, entries], coupling)
+            spread = dot(place_ref[at : at + PIECE, entries], couple_ref[area])
             spread_ref[at : at + PIECE, entries] = spread.astype(BF16)
     for at in range(0, slots, PIECE):
         here = slice(at, at + PIECE)
@@ -224,9 +217,9 @@
     def block_copy(area):
         return pltpu.make_async_copy(ginv_ref.at[area], block_ref.at[area], block_sems.at[area])
 
-    def out_copy(area):
-        rows = rows_of(area)
-        return pltpu.make_async_copy(solved_ref.at[rows], states_ref.at[rows], out_sems.at[area])
+    def out_copy(piece):
+        rows = pl.ds(piece * OUT, OUT)
+        return pltpu.make_async_copy(solved_ref.at[rows], states_ref.at[rows], out_sems.at[piece])
 
     for area in range(areas):
         right_copy(area).start()
@@ -245,9 +238,10 @@
         for at in range(0, state, PIECE):
             solved = dot(block_ref[area, at : at + PIECE, :], blended)
             solved_ref[area * state + at : area * state + at + PIECE, :] = solved
-        out_copy(area).start()
-    for area in range(areas):
-        out_copy(area).wait()
+            if (at + PIECE) % OUT == 0:
+                out_copy((area * state + at) // OUT).start()
+    for piece in range(areas * state // OUT):
+        out_copy(piece).wait()
 
 
 def select(spec, a, b):
@@ -269,23 +263,22 @@
     anywhere = pl.BlockSpec(memory_space=pl.ANY)
     small = pl.BlockSpec((areas, bound), lambda: (0, 0))
     whole = pl.BlockSpec(memory_space=pltpu.VMEM)
-    local, outgoing, chosen = pl.pallas_call(
+    local, outgoing, couple = pl.pallas_call(
         start_kernel,
         in_specs=[small, small, anywhere, anywhere],
-        out_specs=[whole, whole, anywhere],
+        out_specs=[whole, whole, whole],
         out_shape=[
             pltpu.VMEM((slots, snaps), F32),
             pltpu.VMEM((devices * WIDE, snaps), F32),
-            shape((areas, bound, state), BF16),
+            shape((areas, bound, bound), BF16),
         ],
         scratch_shapes=[
             pltpu.VMEM((areas, state, state), BF16),
             pltpu.VMEM((areas * state, snaps), F32),
-            pltpu.VMEM((areas, bound, state), BF16),
+            pltpu.VMEM((bound, state), BF16),
             pltpu.VMEM((devices, bound), F32),
             pltpu.VMEM((slots, entries), BF16),
             pltpu.VMEM((entries, 3 * snaps), BF16),
-            pltpu.SemaphoreType.DMA((areas,)),
             pltpu.SemaphoreType.DMA((areas,)),
             pltpu.SemaphoreType.DMA((areas,)),
         ],
@@ -293,7 +286,7 @@
     )(bnd_row, bnd_var, ginv, rhs)
     back, mat, term, inner = pl.pallas_call(
         prepare_kernel,
-        in_specs=[small, small, anywhere, anywhere],
+        in_specs=[small, small, whole, anywhere],
         out_specs=[whole, whole, whole, anywhere],
         out_shape=[
             pltpu.VMEM((entries, slots), BF16),
@@ -302,7 +295,6 @@
             shape((areas * state, snaps), BF16),
         ],
         scratch_shapes=[
-            pltpu.VMEM((areas, bound, state), BF16),
             pltpu.VMEM((areas * state, snaps), F32),
             pltpu.VMEM((areas * state, snaps), BF16),
             pltpu.VMEM((devices, bound), F32),
@@ -311,10 +303,9 @@
             pltpu.VMEM((slots, entries), BF16),
             pltpu.SemaphoreType.DMA((areas,)),
             pltpu.SemaphoreType.DMA((areas,)),
-            pltpu.SemaphoreType.DMA((areas,)),
         ],
         name="prepare",
-    )(bnd_row, bnd_var, chosen, rhs)
+    )(bnd_row, bnd_var, couple, rhs)
 
     def exchange(x, rows=SLOT, width=snaps):
         x = x.reshape(devices, rows, width)
@@ -360,7 +351,7 @@
             pltpu.VMEM((areas * state, snaps), F32),
             pltpu.SemaphoreType.DMA((areas,)),
             pltpu.SemaphoreType.DMA((areas,)),
-            pltpu.SemaphoreType.DMA((areas,)),
+            pltpu.SemaphoreType.DMA((areas * state // OUT,)),
         ],
         name="states",
     )(bnd_row, ginv, inner, back, blend)

time: 144 us -> 143 us (level)
  Pallas kernels: 20.4 us -> 18.7 us
  transfers between devices with their start and end apart: 2 -> 2, of which waited for: 2 -> 2; matrix products, arithmetic and copies ran while one was open for 0% -> 0% of each run, Pallas kernels for 9% -> 8%
where the time goes in v8:
time: 143 us
  blocking collectives  91.9 us (64%)
  Pallas kernels  18.7 us (13%)
  starting transfers between devices  15.8 us (11%)
  waiting for transfers between devices  10.9 us (8%)
  matrix products  4.88 us (3%)
    all_to_all x6, blocking collectives, exchange(): lax.all_to_all(x, ('area', 'tie'), split_axis=0, concat_axis=0, tiled=True)  91.9 us
    all_to_all x2, starting transfers between devices, exchange(): lax.all_to_all(x, ('area', 'tie'), split_axis=0, concat_axis=0, tiled=True)  15.8 us
    all_to_all x2, waiting for transfers between devices, exchange(): lax.all_to_all(x, ('area', 'tie'), split_axis=0, concat_axis=0, tiled=True)  10.9 us
    pallas_call x1, Pallas kernels, on_device(): pl.pallas_call(states_kernel, in_specs=[small, anywhere, anywhere, pl.Blo...  7.17 us
    pallas_call x1, Pallas kernels, on_device(): pl.pallas_call(start_kernel, in_specs=[small, small, anywhere, anywhere],...  6.48 us
    pallas_call x1, Pallas kernels, on_device(): pl.pallas_call(prepare_kernel, in_specs=[small, small, whole, anywhere],...  4.38 us
    dot_general x7, matrix products, select(): jnp.einsum(spec, a, b, precision=lax.Precision.HIGH, preferred_element_ty...  3.69 us
  transfers between devices with their start and end apart: 2, of which 2 were waited for; matrix products, arithmetic and copies ran while one was open for 0% of the time, Pallas kernels for 8%

profile of v8, /device:TPU:1, one launch (start us, length us, event | category | flops | bytes accessed | tf_op | source)
XLA Modules:
  0.0 143.1 jit_solution(9935005229160958762)
XLA Ops:
  0.6 6.5 %start.1 = (f32[512,128]{1,0:T(8,128)S(1)}, f32[640,128]{1,0:T(8,128)}, bf16[4,128,128]{2,1,0:T(8,128)(2,1)}) custom-call(s32[4,128]{1,0:T(4,128)} %row_ref.5, s32[4,128]{1,0:T(4,128)} %var_ref.3, bf16[4,1024,1024]{2,1,0:T(8,128)(2,1)} %ginv_ref.3, f32[4096,128]{1,0:T(8,128)} %rhs_ref.3), custom_call_target="tpu_custom_call" | custom-call | tf_op jit(solution)/shard_map/start/pallas_call | solution.py:266
  7.1 11.5 %all-to-all-start = ((f32[128,1,640]{2,1,0:T(1,128)}), f32[128,1,640]{2,1,0:T(1,128)S(1)}, u32[]{:S(2)}, u32[]{:S(2)}) async-start(f32[128,1,640]{2,1,0:T(1,128)} %bitcast), calls=%async_computation | async-start | bytes 655360 | tf_op jit(solution)/shard_map/all_to_all | solution.py:312
  18.6 4.4 %prepare.1 = (bf16[512,512]{1,0:T(8,128)(2,1)S(1)}, bf16[512,512]{1,0:T(8,128)(2,1)S(1)}, f32[512,128]{1,0:T(8,128)S(1)}, bf16[4096,128]{1,0:T(8,128)(2,1)}) custom-call(s32[4,128]{1,0:T(4,128)} %row_ref.5, s32[4,128]{1,0:T(4,128)} %var_ref.3, bf16[4,128,128]{2,1,0:T(8,128)(2,1)} %get-tuple-element.20.couple_ref, f32[4096,128]{1,0:T(8,128)} %rhs_ref.3), custom_call_target="tpu_custom_call" | custom-call | tf_op jit(solution)/shard_map/prepare/pallas_call | solution.py:287
  23.0 0.0 copy-start
  23.0 0.3 convolution_subtract_fusion
  23.3 7.1 %all-to-all-done = f32[128,1,640]{2,1,0:T(1,128)S(1)} async-done(((f32[128,1,640]{2,1,0:T(1,128)}), f32[128,1,640]{2,1,0:T(1,128)S(1)}, u32[]{:S(2)}, u32[]{:S(2)}) %all-to-all-start) | async-done | bytes 327712 | tf_op jit(solution)/shard_map/all_to_all | solution.py:312
  30.4 0.0 copy-done
  30.4 0.7 first_owner.1
  31.1 15.4 %all_to_all.40 = f32[128,4,128]{2,1,0:T(4,128)S(1)} all-to-all(f32[128,4,128]{2,1,0:T(4,128)S(1)} %bitcast.35), channel_id=1, replica_groups=mesh['area'=16,'tie'=8] {'area','tie'}, dimensions={0} | all-to-all | bytes 524288 | tf_op jit(solution)/shard_map/all_to_all | solution.py:312
  46.5 0.3 fusion
  46.8 15.3 %all_to_all.41 = f32[128,4,128]{2,1,0:T(4,128)S(1)} all-to-all(f32[128,4,128]{2,1,0:T(4,128)S(1)} %bitcast.37), channel_id=1, replica_groups=mesh['area'=16,'tie'=8] {'area','tie'}, dimensions={0} | all-to-all | bytes 524288 | tf_op jit(solution)/shard_map/all_to_all | solution.py:312
  62.1 0.4 convolution_multiply_fusion.2
  62.5 0.2 fusion.8
  62.7 15.3 %all_to_all.42 = f32[128,4,128]{2,1,0:T(4,128)S(1)} all-to-all(f32[128,4,128]{2,1,0:T(4,128)S(1)} %bitcast.45), channel_id=1, replica_groups=mesh['area'=16,'tie'=8] {'area','tie'}, dimensions={0} | all-to-all | bytes 524288 | tf_op jit(solution)/shard_map/all_to_all | solution.py:312
  78.0 0.3 fusion.1
  78.3 15.3 %all_to_all.43 = f32[128,4,128]{2,1,0:T(4,128)S(1)} all-to-all(f32[128,4,128]{2,1,0:T(4,128)S(1)} %bitcast.36), channel_id=1, replica_groups=mesh['area'=16,'tie'=8] {'area','tie'}, dimensions={0} | all-to-all | bytes 524288 | tf_op jit(solution)/shard_map/all_to_all | solution.py:312
  93.6 0.4 convolution_multiply_fusion.1
  94.0 0.2 fusion.9
  94.3 15.2 %all_to_all.44 = f32[128,4,128]{2,1,0:T(4,128)S(1)} all-to-all(f32[128,4,128]{2,1,0:T(4,128)S(1)} %bitcast.46), channel_id=1, replica_groups=mesh['area'=16,'tie'=8] {'area','tie'}, dimensions={0} | all-to-all | bytes 524288 | tf_op jit(solution)/shard_map/all_to_all | solution.py:312
  109.5 0.0 copy-start.2
  109.5 0.3 fusion.2
  109.8 15.4 %all_to_all.45 = f32[128,4,128]{2,1,0:T(4,128)S(1)} all-to-all(f32[128,4,128]{2,1,0:T(4,128)S(1)} %bitcast.38), channel_id=1, replica_groups=mesh['area'=16,'tie'=8] {'area','tie'}, dimensions={0} | all-to-all | bytes 524288 | tf_op jit(solution)/shard_map/all_to_all | solution.py:312
  125.2 0.4 convolution_multiply_fusion
  125.6 0.0 copy-start.3
  125.6 0.9 fusion.10
  126.6 4.3 %all-to-all-start.7 = ((f32[128,4,128]{2,1,0:T(4,128)}), f32[128,4,128]{2,1,0:T(4,128)S(1)}, u32[]{:S(2)}, u32[]{:S(2)}) async-start(f32[128,4,128]{2,1,0:T(4,128)} %bitcast.14), calls=%async_computation.7 | async-start | bytes 524288 | tf_op jit(solution)/shard_map/all_to_all | solution.py:312
  130.9 0.0 copy-done.2
  130.9 0.0 copy-start.1
  130.9 7.2 %states.1 = f32[4096,128]{1,0:T(8,128)} custom-call(s32[4,128]{1,0:T(4,128)} %row_ref.5, bf16[4,1024,1024]{2,1,0:T(8,128)(2,1)} %ginv_ref.3, bf16[4096,128]{1,0:T(8,128)(2,1)} %get-tuple-element.26.inner_ref, bf16[512,512]{1,0:T(8,128)(2,1)} %copy-done, bf16[512,128]{1,0:T(8,128)(2,1)} %copy-done.2), custom_call_target="tpu_custom_call" | custom-call | tf_op jit(solution)/shard_map/states/pallas_call | solution.py:337
  138.1 3.9 %all-to-all-done.7 = f32[128,4,128]{2,1,0:T(4,128)S(1)} async-done(((f32[128,4,128]{2,1,0:T(4,128)}), f32[128,4,128]{2,1,0:T(4,128)S(1)}, u32[]{:S(2)}, u32[]{:S(2)}) %all-to-all-start.7) | async-done | bytes 262176 | tf_op jit(solution)/shard_map/all_to_all | solution.py:312
  141.9 0.0 copy-done.1
  141.9 1.1 fusion.3
  (2 shorter events, 0.0 us)
Async XLA Ops:
  7.1 23.3 %all-to-all-start = ((f32[128,1,640]{2,1,0:T(1,128)}), f32[128,1,640]{2,1,0:T(1,128)S(1)}, u32[]{:S(2)}, u32[]{:S(2)}) async-start(f32[128,1,640]{2,1,0:T(1,128)} %bitcast), calls=%async_computation | async-start | bytes 655360 | tf_op jit(solution)/shard_map/all_to_all | solution.py:312
  23.0 7.4 %copy-start = (bf16[512,512]{1,0:T(8,128)(2,1)}, bf16[512,512]{1,0:T(8,128)(2,1)S(1)}, u32[]{:S(2)}) copy-start(bf16[512,512]{1,0:T(8,128)(2,1)S(1)} %get-tuple-element.27.back_ref) | copy-start | bytes 1572868
  109.5 21.4 %copy-start.2 = (bf16[512,128]{1,0:T(8,128)(2,1)}, bf16[512,128]{1,0:T(8,128)(2,1)S(1)}, u32[]{:S(2)}) copy-start(bf16[512,128]{1,0:T(8,128)(2,1)S(1)} %add_convert_fusion.blend_ref) | copy-start | bytes 393220
  125.6 12.5 %copy-start.3 = (f32[64,128]{1,0:T(8,128)}, f32[64,128]{1,0:T(8,128)S(1)}, u32[]{:S(2)}) copy-start(f32[64,128]{1,0:T(8,128)S(1)} %convolution_multiply_fusion) | copy-start | bytes 98308
  126.6 15.4 %all-to-all-start.7 = ((f32[128,4,128]{2,1,0:T(4,128)}), f32[128,4,128]{2,1,0:T(4,128)S(1)}, u32[]{:S(2)}, u32[]{:S(2)}) async-start(f32[128,4,128]{2,1,0:T(4,128)} %bitcast.14), calls=%async_computation.7 | async-start | bytes 524288 | tf_op jit(solution)/shard_map/all_to_all | solution.py:312
  130.9 11.1 %copy-start.1 = (bf16[512,512]{1,0:T(8,128)(2,1)S(1)}, bf16[512,512]{1,0:T(8,128)(2,1)}, u32[]{:S(2)}) copy-start(bf16[512,512]{1,0:T(8,128)(2,1)} %copy-done) | copy-start | bytes 1572868

commit v9 on v8

--- a/solution.py
+++ b/solution.py
@@ -130,9 +130,10 @@
 
 
 def prepare_kernel(
-    row_ref, var_ref, couple_ref, rhs_ref, back_ref, mat_ref, term_ref, inner_ref,
+    row_ref, var_ref, couple_ref, rhs_ref, ginv_ref,
+    back_ref, mat_ref, term_ref, inner_ref, first_ref, cols_ref,
     right_ref, kept_ref, carry_ref, rows_ref, spread_ref, place_ref,
-    right_sems, out_sems,
+    block_ref, right_sems, out_sems, block_sem,
 ):
     areas, bound = row_ref.shape
     state = rhs_ref.shape[0] // areas
@@ -146,8 +147,11 @@
         rows = pl.ds(area * state, state)
         return pltpu.make_async_copy(kept_ref.at[rows], inner_ref.at[rows], out_sems.at[area])
 
+    block_copy = pltpu.make_async_copy(ginv_ref.at[0], block_ref, block_sem.at[0])
     for area in range(areas):
         right_copy(area).start()
+        if area == 0:
+            block_copy.start()
     carry_ref[...] = jnp.zeros_like(carry_ref)
     for area in range(areas):
         var = var_ref[area : area + 1, :]
@@ -171,6 +175,13 @@
         for at in range(0, slots, PIECE):
             spread = dot(place_ref[at : at + PIECE, entries], couple_ref[area])
             spread_ref[at : at + PIECE, entries] = spread.astype(BF16)
+    block_copy.wait()
+    columns = placing(row_ref[0:1, :], state)
+    columns = jnp.concatenate([kept_ref[:state, :], columns], axis=1)
+    for at in range(0, state, PIECE):
+        both = dot(block_ref[at : at + PIECE, :], columns)
+        first_ref[at : at + PIECE, :] = both[:, :snaps]
+        cols_ref[at : at + PIECE, :] = both[:, snaps:].astype(BF16)
     for at in range(0, slots, PIECE):
         here = slice(at, at + PIECE)
         term_ref[here, :] = join3(dot(place_ref[here, :], rows_ref[...]), 0, snaps)
@@ -201,8 +212,9 @@
 
 
 def states_kernel(
-    row_ref, ginv_ref, inner_ref, back_ref, blend_ref, states_ref,
-    block_ref, right_ref, solved_ref, block_sems, right_sems, out_sems,
+    row_ref, ginv_ref, inner_ref, first_ref, cols_ref, back_ref, blend_ref, states_ref,
+    block_ref, right_ref, solved_ref, made_ref, made_cols_ref,
+    block_sems, right_sems, out_sems, made_sems,
 ):
     areas, bound = row_ref.shape
     state = ginv_ref.shape[1]
@@ -215,17 +227,28 @@
         return pltpu.make_async_copy(inner_ref.at[rows], right_ref.at[rows], right_sems.at[area])
 
     def block_copy(area):
-        return pltpu.make_async_copy(ginv_ref.at[area], block_ref.at[area], block_sems.at[area])
+        return pltpu.make_async_copy(ginv_ref.at[area], block_ref.at[area - 1], block_sems.at[area])
 
     def out_copy(piece):
         rows = pl.ds(piece * OUT, OUT)
         return pltpu.make_async_copy(solved_ref.at[rows], states_ref.at[rows], out_sems.at[piece])
 
-    for area in range(areas):
+    made_copy = pltpu.make_async_copy(first_ref, made_ref, made_sems.at[0])
+    made_cols_copy = pltpu.make_async_copy(cols_ref, made_cols_ref, made_sems.at[1])
+    made_copy.start()
+    made_cols_copy.start()
+    for area in range(1, areas):
         right_copy(area).start()
         block_copy(area).start()
     entry_rows = dot(back_ref[...], blend_ref[...]).astype(BF16)
-    for area in range(areas):
+    made_copy.wait()
+    made_cols_copy.wait()
+    for at in range(0, state, PIECE):
+        here = slice(at, at + PIECE)
+        solved_ref[here, :] = made_ref[here, :] + dot(made_cols_ref[here, :], entry_rows[:bound])
+    for piece in range(state // OUT):
+        out_copy(piece).start()
+    for area in range(1, areas):
         row = row_ref[area : area + 1, :]
         rows = entry_rows[area * bound : (area + 1) * bound]
         right_copy(area).wait()
@@ -236,7 +259,7 @@
         blended = jnp.concatenate(pieces, axis=0)
         block_copy(area).wait()
         for at in range(0, state, PIECE):
-            solved = dot(block_ref[area, at : at + PIECE, :], blended)
+            solved = dot(block_ref[area - 1, at : at + PIECE, :], blended)
             solved_ref[area * state + at : area * state + at + PIECE, :] = solved
             if (at + PIECE) % OUT == 0:
                 out_copy((area * state + at) // OUT).start()
@@ -284,15 +307,17 @@
         ],
         name="start",
     )(bnd_row, bnd_var, ginv, rhs)
-    back, mat, term, inner = pl.pallas_call(
+    back, mat, term, inner, first, cols = pl.pallas_call(
         prepare_kernel,
-        in_specs=[small, small, whole, anywhere],
-        out_specs=[whole, whole, whole, anywhere],
+        in_specs=[small, small, whole, anywhere, anywhere],
+        out_specs=[whole, whole, whole, anywhere, whole, whole],
         out_shape=[
             pltpu.VMEM((entries, slots), BF16),
             pltpu.VMEM((slots, slots), BF16),
             pltpu.VMEM((slots, snaps), F32),
             shape((areas * state, snaps), BF16),
+            shape((state, snaps)),
+            shape((state, bound), BF16),
         ],
         scratch_shapes=[
             pltpu.VMEM((areas * state, snaps), F32),
@@ -301,11 +326,13 @@
             pltpu.VMEM((entries, 3 * snaps), BF16),
             pltpu.VMEM((slots, entries), BF16),
             pltpu.VMEM((slots, entries), BF16),
-            pltpu.SemaphoreType.DMA((areas,)),
-            pltpu.SemaphoreType.DMA((areas,)),
+            pltpu.VMEM((state, state), BF16),
+            pltpu.SemaphoreType.DMA((areas,)),
+            pltpu.SemaphoreType.DMA((areas,)),
+            pltpu.SemaphoreType.DMA((1,)),
         ],
         name="prepare",
-    )(bnd_row, bnd_var, couple, rhs)
+    )(bnd_row, bnd_var, couple, rhs, ginv)
 
     def exchange(x, rows=SLOT, width=snaps):
         x = x.reshape(devices, rows, width)
@@ -313,8 +340,8 @@
         return x.reshape(-1, snaps)
 
     base = local - dot(mat, term.astype(BF16))
-    received, back, mat, base, term, inner = lax.optimization_barrier(
-        (exchange(outgoing, 1, WIDE * snaps), back, mat, base, term, inner)
+    received, back, mat, base, term, inner, first, cols = lax.optimization_barrier(
+        (exchange(outgoing, 1, WIDE * snaps), back, mat, base, term, inner, first, cols)
     )
     returning, member, inverse = pl.pallas_call(
         first_owner_kernel,
@@ -340,21 +367,26 @@
             small,
             anywhere,
             anywhere,
+            anywhere,
+            anywhere,
             pl.BlockSpec((entries, slots), lambda: (0, 0)),
             pl.BlockSpec((slots, snaps), lambda: (0, 0)),
         ],
         out_specs=anywhere,
         out_shape=shape((areas * state, snaps)),
         scratch_shapes=[
-            pltpu.VMEM((areas, state, state), BF16),
+            pltpu.VMEM((areas - 1, state, state), BF16),
             pltpu.VMEM((areas * state, snaps), BF16),
             pltpu.VMEM((areas * state, snaps), F32),
+            pltpu.VMEM((state, snaps), F32),
+            pltpu.VMEM((state, bound), BF16),
             pltpu.SemaphoreType.DMA((areas,)),
             pltpu.SemaphoreType.DMA((areas,)),
             pltpu.SemaphoreType.DMA((areas * state // OUT,)),
+            pltpu.SemaphoreType.DMA((2,)),
         ],
         name="states",
-    )(bnd_row, ginv, inner, back, blend)
+    )(bnd_row, ginv, inner, first, cols, back, blend)
     dual = select("es,sn->en", back.astype(F32), dual)
     return states, consensus, dual
 

time: 143 us -> 144 us (level)
  Pallas kernels: 18.7 us -> 20.6 us
  waiting for transfers between devices: 10.9 us -> 9.03 us
    all_to_all x2, waiting for transfers between devices: 10.9 us -> 9.03 us  [exchange(): lax.all_to_all(x, ('area', 'tie'), split_axis=0, concat_axis=0, tiled=True)]
    pallas_call x2, Pallas kernels: 11.5 us -> 13.5 us  [the longest x1 7.58 us: on_device(): pl.pallas_call(states_kernel, in_specs=[small, anywhere, anywhere, anywhe...]
  transfers between devices with their start and end apart: 2 -> 2, of which waited for: 2 -> 2; matrix products, arithmetic and copies ran while one was open for 0% -> 0% of each run, Pallas kernels for 8% -> 9%
where the time goes in v9:
time: 144 us; the launch traced here: 143 us
  blocking collectives  92.2 us (64%)
  Pallas kernels  20.6 us (14%)
  starting transfers between devices  15.8 us (11%)
  waiting for transfers between devices  9.03 us (6%)
  matrix products  4.89 us (3%)
    all_to_all x6, blocking collectives, exchange(): lax.all_to_all(x, ('area', 'tie'), split_axis=0, concat_axis=0, tiled=True)  92.2 us
    all_to_all x2, starting transfers between devices, exchange(): lax.all_to_all(x, ('area', 'tie'), split_axis=0, concat_axis=0, tiled=True)  15.8 us
    all_to_all x2, waiting for transfers between devices, exchange(): lax.all_to_all(x, ('area', 'tie'), split_axis=0, concat_axis=0, tiled=True)  9.03 us
    pallas_call x1, Pallas kernels, on_device(): pl.pallas_call(states_kernel, in_specs=[small, anywhere, anywhere, anywhe...  7.58 us
    pallas_call x1, Pallas kernels, on_device(): pl.pallas_call(start_kernel, in_specs=[small, small, anywhere, anywhere],...  6.48 us
    pallas_call x1, Pallas kernels, on_device(): pl.pallas_call(prepare_kernel, in_specs=[small, small, whole, anywhere, a...  5.87 us
    dot_general x7, matrix products, select(): jnp.einsum(spec, a, b, precision=lax.Precision.HIGH, preferred_element_ty...  3.69 us
  transfers between devices with their start and end apart: 2, of which 2 were waited for; matrix products, arithmetic and copies ran while one was open for 0% of the time, Pallas kernels for 9%

profile of v9, /device:TPU:1, one launch (start us, length us, event | category | flops | bytes accessed | tf_op | source)
XLA Modules:
  0.0 143.4 jit_solution(9330582938490731640)
XLA Ops:
  0.6 6.5 %start.1 = (f32[512,128]{1,0:T(8,128)S(1)}, f32[640,128]{1,0:T(8,128)}, bf16[4,128,128]{2,1,0:T(8,128)(2,1)}) custom-call(s32[4,128]{1,0:T(4,128)} %row_ref.5, s32[4,128]{1,0:T(4,128)} %var_ref.3, bf16[4,1024,1024]{2,1,0:T(8,128)(2,1)} %ginv_ref.5, f32[4096,128]{1,0:T(8,128)} %rhs_ref.3), custom_call_target="tpu_custom_call" | custom-call | tf_op jit(solution)/shard_map/start/pallas_call | solution.py:289
  7.1 11.5 %all-to-all-start = ((f32[128,1,640]{2,1,0:T(1,128)}), f32[128,1,640]{2,1,0:T(1,128)S(1)}, u32[]{:S(2)}, u32[]{:S(2)}) async-start(f32[128,1,640]{2,1,0:T(1,128)} %bitcast), calls=%async_computation | async-start | bytes 655360 | tf_op jit(solution)/shard_map/all_to_all | solution.py:339
  18.6 5.9 %prepare.1 = (bf16[512,512]{1,0:T(8,128)(2,1)S(1)}, bf16[512,512]{1,0:T(8,128)(2,1)S(1)}, f32[512,128]{1,0:T(8,128)S(1)}, bf16[4096,128]{1,0:T(8,128)(2,1)}, f32...) custom-call(s32[4,128]{1,0:T(4,128)} %row_ref.5, s32[4,128]{1,0:T(4,128)} %var_ref.3, ...), custom_call_target="tpu_custom_call" | custom-call | tf_op jit(solution)/shard_map/prepare/pallas_call | solution.py:310
  24.5 0.0 copy-start
  24.5 0.3 convolution_subtract_fusion
  24.8 5.6 %all-to-all-done = f32[128,1,640]{2,1,0:T(1,128)S(1)} async-done(((f32[128,1,640]{2,1,0:T(1,128)}), f32[128,1,640]{2,1,0:T(1,128)S(1)}, u32[]{:S(2)}, u32[]{:S(2)}) %all-to-all-start) | async-done | bytes 327712 | tf_op jit(solution)/shard_map/all_to_all | solution.py:339
  30.4 0.0 copy-done
  30.4 0.7 first_owner.1
  31.1 15.7 %all_to_all.40 = f32[128,4,128]{2,1,0:T(4,128)S(1)} all-to-all(f32[128,4,128]{2,1,0:T(4,128)S(1)} %bitcast.35), channel_id=1, replica_groups=mesh['area'=16,'tie'=8] {'area','tie'}, dimensions={0} | all-to-all | bytes 524288 | tf_op jit(solution)/shard_map/all_to_all | solution.py:339
  46.8 0.3 fusion
  47.1 15.3 %all_to_all.41 = f32[128,4,128]{2,1,0:T(4,128)S(1)} all-to-all(f32[128,4,128]{2,1,0:T(4,128)S(1)} %bitcast.37), channel_id=1, replica_groups=mesh['area'=16,'tie'=8] {'area','tie'}, dimensions={0} | all-to-all | bytes 524288 | tf_op jit(solution)/shard_map/all_to_all | solution.py:339
  62.4 0.4 convolution_multiply_fusion.2
  62.8 0.2 fusion.8
  63.0 15.3 %all_to_all.42 = f32[128,4,128]{2,1,0:T(4,128)S(1)} all-to-all(f32[128,4,128]{2,1,0:T(4,128)S(1)} %bitcast.45), channel_id=1, replica_groups=mesh['area'=16,'tie'=8] {'area','tie'}, dimensions={0} | all-to-all | bytes 524288 | tf_op jit(solution)/shard_map/all_to_all | solution.py:339
  78.3 0.3 fusion.1
  78.6 15.3 %all_to_all.43 = f32[128,4,128]{2,1,0:T(4,128)S(1)} all-to-all(f32[128,4,128]{2,1,0:T(4,128)S(1)} %bitcast.36), channel_id=1, replica_groups=mesh['area'=16,'tie'=8] {'area','tie'}, dimensions={0} | all-to-all | bytes 524288 | tf_op jit(solution)/shard_map/all_to_all | solution.py:339
  93.9 0.4 convolution_multiply_fusion.1
  94.3 0.2 fusion.9
  94.6 15.3 %all_to_all.44 = f32[128,4,128]{2,1,0:T(4,128)S(1)} all-to-all(f32[128,4,128]{2,1,0:T(4,128)S(1)} %bitcast.46), channel_id=1, replica_groups=mesh['area'=16,'tie'=8] {'area','tie'}, dimensions={0} | all-to-all | bytes 524288 | tf_op jit(solution)/shard_map/all_to_all | solution.py:339
  109.9 0.0 copy-start.2
  109.9 0.3 fusion.2
  110.2 15.3 %all_to_all.45 = f32[128,4,128]{2,1,0:T(4,128)S(1)} all-to-all(f32[128,4,128]{2,1,0:T(4,128)S(1)} %bitcast.38), channel_id=1, replica_groups=mesh['area'=16,'tie'=8] {'area','tie'}, dimensions={0} | all-to-all | bytes 524288 | tf_op jit(solution)/shard_map/all_to_all | solution.py:339
  125.5 0.4 convolution_multiply_fusion
  125.9 0.0 copy-start.3
  125.9 0.9 fusion.10
  126.9 4.3 %all-to-all-start.7 = ((f32[128,4,128]{2,1,0:T(4,128)}), f32[128,4,128]{2,1,0:T(4,128)S(1)}, u32[]{:S(2)}, u32[]{:S(2)}) async-start(f32[128,4,128]{2,1,0:T(4,128)} %bitcast.14), calls=%async_computation.7 | async-start | bytes 524288 | tf_op jit(solution)/shard_map/all_to_all | solution.py:339
  131.2 0.0 copy-done.2
  131.2 0.0 copy-start.1
  131.2 7.6 %states.1 = f32[4096,128]{1,0:T(8,128)} custom-call(s32[4,128]{1,0:T(4,128)} %row_ref.5, bf16[4,1024,1024]{2,1,0:T(8,128)(2,1)} %ginv_ref.5, bf16[4096,128]{1,0:T(8,128)(2,1)} %get-tuple-element.32.inner_ref, f32[1024,128]{1,0:T(8,128)} %get-tuple-element.33.first_ref, bf16[1024,128]{1,0:T(8,128)(2,1)} %get-tuple-element.34.cols_ref, ...), custom_call_target="tpu_custom_call" | custom-call | tf_op jit(solution)/shard_map/states/pallas_call | solution.py:364
  138.8 0.0 copy-done.3
  138.8 3.4 %all-to-all-done.7 = f32[128,4,128]{2,1,0:T(4,128)S(1)} async-done(((f32[128,4,128]{2,1,0:T(4,128)}), f32[128,4,128]{2,1,0:T(4,128)S(1)}, u32[]{:S(2)}, u32[]{:S(2)}) %all-to-all-start.7) | async-done | bytes 262176 | tf_op jit(solution)/shard_map/all_to_all | solution.py:339
  142.2 1.2 fusion.3
  (2 shorter events, 0.0 us)
Async XLA Ops:
  7.1 23.3 %all-to-all-start = ((f32[128,1,640]{2,1,0:T(1,128)}), f32[128,1,640]{2,1,0:T(1,128)S(1)}, u32[]{:S(2)}, u32[]{:S(2)}) async-start(f32[128,1,640]{2,1,0:T(1,128)} %bitcast), calls=%async_computation | async-start | bytes 655360 | tf_op jit(solution)/shard_map/all_to_all | solution.py:339
  24.5 5.9 %copy-start = (bf16[512,512]{1,0:T(8,128)(2,1)}, bf16[512,512]{1,0:T(8,128)(2,1)S(1)}, u32[]{:S(2)}) copy-start(bf16[512,512]{1,0:T(8,128)(2,1)S(1)} %get-tuple-element.35.back_ref) | copy-start | bytes 1572868
  109.9 21.3 %copy-start.2 = (bf16[512,128]{1,0:T(8,128)(2,1)}, bf16[512,128]{1,0:T(8,128)(2,1)S(1)}, u32[]{:S(2)}) copy-start(bf16[512,128]{1,0:T(8,128)(2,1)S(1)} %add_convert_fusion.blend_ref) | copy-start | bytes 393220
  125.9 12.9 %copy-start.3 = (f32[64,128]{1,0:T(8,128)}, f32[64,128]{1,0:T(8,128)S(1)}, u32[]{:S(2)}) copy-start(f32[64,128]{1,0:T(8,128)S(1)} %convolution_multiply_fusion) | copy-start | bytes 98308
  126.9 15.4 %all-to-all-start.7 = ((f32[128,4,128]{2,1,0:T(4,128)}), f32[128,4,128]{2,1,0:T(4,128)S(1)}, u32[]{:S(2)}, u32[]{:S(2)}) async-start(f32[128,4,128]{2,1,0:T(4,128)} %bitcast.14), calls=%async_computation.7 | async-start | bytes 524288 | tf_op jit(solution)/shard_map/all_to_all | solution.py:339
  131.2 11.1 %copy-start.1 = (bf16[512,512]{1,0:T(8,128)(2,1)S(1)}, bf16[512,512]{1,0:T(8,128)(2,1)}, u32[]{:S(2)}) copy-start(bf16[512,512]{1,0:T(8,128)(2,1)} %copy-done) | copy-start | bytes 1572868
